TPU v7x, 128 devices: a whole 4x4x4 slice. The times are simulated.
128 devices in a mesh: south: 2 (over x_hi), east: 8 (over y, core), down: 8 (over z, x_lo).
Axes of the slice: x: 4 (x_hi: 2, x_lo: 2; x = x_hi * 2 + x_lo), y: 4, z: 4, core: 2. Of those that a mesh axis runs over, the one named last changes fastest.
Arguments:
- field_values: float32 [256, 64, 64, 128], P('south', 'east', 'down'), may hold values from 0.5 to 2
- flow_j: float32 [256, 64, 64, 128], P('south', 'east', 'down'), may hold values from -0.3 to 0.3
- flow_i: float32 [256, 64, 64, 128], P('south', 'east', 'down'), may hold values from -0.3 to 0.3
- flow_k: float32 [256, 64, 64, 128], P('south', 'east', 'down'), may hold values from -0.3 to 0.3
Outputs:
- standardized: float32 [256, 64, 64, 128], P('south', 'east', 'down')
- field_values_end: float32 [256, 64, 64, 128], P('south', 'east', 'down')
All inputs are finite; a program needn't handle non-finite values.
Results may differ from a plain program's by a relative error of at most 0.00002.
Values sent between devices are 32-bit elements; how exact they have to be, the bound alone decides.
No kernel may reach another device: no remote copies, remote signals or barrier semaphores. Data moves between devices by JAX's collectives and lax.ppermute only.
A program may use at most 128 MiB of HBM per device.

v0:
```python
import jax
import jax.numpy as jnp
from jax import lax
from jax.sharding import PartitionSpec as P

STEPS = 6


def with_halo(shard, sides, width):
    edges = {}
    for axis, dim in sides:
        devices, length = (lax.axis_size(axis), shard.shape[dim])
        up = [(i, (i + 1) % devices) for i in range(devices - 1)]
        last = lax.slice_in_dim(shard, length - width, length, axis=dim)
        leading = lax.slice_in_dim(shard, 0, width, axis=dim)
        edges[dim] = (
            lax.ppermute(last, axis, up),
            lax.ppermute(leading, axis, [(b, a) for a, b in up]),
        )
    done = []
    for _, dim in sides:
        low, high = edges[dim]
        around = [(width, width) if d in done else (0, 0) for d in range(shard.ndim)]
        shard = jnp.concatenate([jnp.pad(low, around), shard, jnp.pad(high, around)], axis=dim)
        done.append(dim)
    return shard


def sent_to_all(shard, axis):
    devices = lax.axis_size(axis)
    return lax.all_to_all(
        jnp.broadcast_to(shard[None], (devices, *shard.shape)), axis, 0, 0, tiled=True
    )


def taken_together(shard, axis):
    everything = sent_to_all(shard, axis)
    return jnp.sum(everything, axis=0)


def in_one(arrays, axis):
    ends = [0]
    for a in arrays:
        ends.append(ends[-1] + a.size)
    total = taken_together(jnp.concatenate([a.ravel() for a in arrays]), axis)
    return tuple((total[b:e].reshape(a.shape) for a, b, e in zip(arrays, ends, ends[1:])))


def inner_cells(values, dims):
    for dim in dims:
        values = lax.slice_in_dim(values, 1, values.shape[dim] - 1, axis=dim)
    return values


def side_cells(values, dim, start, dims):
    others = [other for other in dims if other != dim]
    values = inner_cells(values, others)
    return lax.slice_in_dim(values, start, start + values.shape[dim] - 2, axis=dim)


def advance(padded, flow_j, flow_i, flow_k):
    middle = inner_cells(padded, (0, 1, 2))
    lower = [side_cells(padded, dim, 0, (0, 1, 2)) for dim in (0, 1, 2)]
    upper = [side_cells(padded, dim, 2, (0, 1, 2)) for dim in (0, 1, 2)]
    slopes = [above - below for above, below in zip(upper, lower)]
    smooth_rate = 0.05
    spread = lower[0] + upper[0] + lower[1] + upper[1] + lower[2] + upper[2] - 6.0 * middle
    return (
        middle - flow_j * slopes[0] - flow_i * slopes[1] - flow_k * slopes[2] + smooth_rate * spread
    )


def per_device(field_values, flow_j, flow_i, flow_k):
    for step in range(STEPS):
        padded = with_halo(field_values, (("south", 0), ("east", 1), ("down", 2)), 1)
        field_values = advance(padded, flow_j, flow_i, flow_k)
    count = field_values.shape[0] * lax.axis_size("south")
    guess = 1.0
    moved = field_values - guess
    totals, squares = in_one(
        (jnp.sum(moved, axis=0, keepdims=True), jnp.sum(moved * moved, axis=0, keepdims=True)),
        "south",
    )
    line_mean = guess + totals / count
    centred = field_values - line_mean
    line_variance = squares / count - totals / count * (totals / count)
    standardized = centred * lax.rsqrt(line_variance + 0.0001)
    return (standardized, field_values)


def solution(mesh):
    return jax.shard_map(
        per_device,
        mesh=mesh,
        in_specs=(
            P("south", "east", "down", None),
            P("south", "east", "down", None),
            P("south", "east", "down", None),
            P("south", "east", "down", None),
        ),
        out_specs=(P("south", "east", "down", None), P("south", "east", "down", None)),
        check_vma=False,
    )
```

profile of v0, /device:TPU:96, one launch (start us, length us, event | category | flops | bytes accessed | tf_op | source)
XLA Modules:
  0.0 293.4 jit_solution(18436670900424788471)
XLA Ops:
  1.9 1.3 collective-permute-start.2
  3.2 3.1 %collective-permute-start.3 = (f32[128,1,8,128]{3,2,1,0:T(8,128)S(1)}, f32[128,1,8,128]{3,2,1,0:T(8,128)S(1)}, u32[]{:S(2)}, u32[]{:S(2)}) collective-permute-start(f32[128,1,8,128]{3,2,1,0:T(8,128)S(1)} %get-tuple-element.41), channel_id=1, source_target_pairs={{0,8},{8,16},{16,24},{24,32},{32,40},{40,48},{48,56},{1,9},{9,17},... | collective-permute-start | bytes 1572872 | tf_op jit(solution)/shard_map/ppermute | solution.py:17
  6.3 4.7 %fusion.31 = (f32[128,8,1,128]{3,2,1,0:T(1,128)S(1)}, f32[128,8,1,128]{3,2,1,0:T(1,128)S(1)}) fusion(f32[128,8,8,128]{3,2,1,0:T(8,128)} %param.4), kind=kLoop, calls=%fused_computation.149 | loop fusion | bytes 2097152 | tf_op jit(solution)/shard_map/slice | solution.py:14
  11.0 3.2 %collective-permute-start.4 = (f32[128,8,1,128]{3,1,2,0:T(8,128)S(1)}, f32[128,8,1,128]{3,1,2,0:T(8,128)}, u32[]{:S(2)}, u32[]{:S(2)}) collective-permute-start(f32[128,8,1,128]{3,1,2,0:T(8,128)S(1)} %bitcast.46), channel_id=1, source_target_pairs={{1,0},{2,1},{3,2},{4,3},{5,4},{6,5},{7,6},{9,8},{10,9},{11,10},{12... | collective-permute-start | bytes 1572872 | tf_op jit(solution)/shard_map/ppermute | solution.py:18
  14.3 3.4 %collective-permute-start.5 = (f32[128,8,1,128]{3,1,2,0:T(8,128)S(1)}, f32[128,8,1,128]{3,1,2,0:T(8,128)}, u32[]{:S(2)}, u32[]{:S(2)}) collective-permute-start(f32[128,8,1,128]{3,1,2,0:T(8,128)S(1)} %bitcast.40), channel_id=1, source_target_pairs={{0,1},{1,2},{2,3},{3,4},{4,5},{5,6},{6,7},{8,9},{9,10},{10,11},{11... | collective-permute-start | bytes 1572872 | tf_op jit(solution)/shard_map/ppermute | solution.py:17
  18.5 4.9 %collective-permute-start.1 = (f32[1,8,8,128]{3,2,1,0:T(8,128)S(1)}, f32[1,8,8,128]{3,2,1,0:T(8,128)S(1)}, u32[]{:S(2)}, u32[]{:S(2)}) collective-permute-start(f32[1,8,8,128]{3,2,1,0:T(8,128)S(1)} %get-tuple-element.44), channel_id=1, source_target_pairs={{0,64},{1,65},{2,66},{3,67},{4,68},{5,69},{6,70},{7,71},{8,72},{9,... | collective-permute-start | bytes 98312 | tf_op jit(solution)/shard_map/ppermute | solution.py:17
  23.4 14.9 %collective-permute-done.1 = f32[1,8,8,128]{3,2,1,0:T(8,128)S(1)} collective-permute-done((f32[1,8,8,128]{3,2,1,0:T(8,128)S(1)}, f32[1,8,8,128]{3,2,1,0:T(8,128)S(1)}, u32[]{:S(2)}, u32[]{:S(2)}) %collective-permute-start.1) | collective-permute-done | bytes 32800 | tf_op jit(solution)/shard_map/ppermute | solution.py:17
  39.6 2.7 constant_dynamic-update-slice_fusion.1
  42.3 3.3 %collective-permute-done = f32[1,8,8,128]{3,2,1,0:T(8,128)S(1)} collective-permute-done((f32[1,8,8,128]{3,2,1,0:T(8,128)S(1)}, f32[1,8,8,128]{3,2,1,0:T(8,128)S(1)}, u32[]{:S(2)}, u32[]{:S(2)}) %collective-permute-start) | collective-permute-done | bytes 32800 | tf_op jit(solution)/shard_map/ppermute | solution.py:18
  45.8 11.9 %multiply_add_fusion.5 = f32[128,8,8,128]{3,2,1,0:T(8,128)S(1)} fusion(f32[128,8,8,128]{3,2,1,0:T(8,128)} %param.4, f32[128,8,8,128]{3,2,1,0:T(8,128)S(1)} %copy-done, f32[128,8,1,128]{3,2,1,0:T(1,128)} %bitcast.25, f32[130,1,8,128]{3,2,1,0:T(8,128)S(1)} %pad.74, f32[130,8,8,128]{3,2,1,0:T(8,128)S(1)} %constant_dynamic-update-slice_fusion, ...), kind=kLoop, calls=%fused_computation.121 | loop fusion | flops 35651584 | bytes 27410432 | tf_op jit(solution)/shard_map/add | solution.py:69
  57.7 1.3 collective-permute-start.8
  59.7 3.1 %collective-permute-start.9 = (f32[128,1,8,128]{3,2,1,0:T(8,128)S(1)}, f32[128,1,8,128]{3,2,1,0:T(8,128)S(1)}, u32[]{:S(2)}, u32[]{:S(2)}) collective-permute-start(f32[128,1,8,128]{3,2,1,0:T(8,128)S(1)} %get-tuple-element.35), channel_id=1, source_target_pairs={{0,8},{8,16},{16,24},{24,32},{32,40},{40,48},{48,56},{1,9},{9,17},... | collective-permute-start | bytes 1572872 | tf_op jit(solution)/shard_map/ppermute | solution.py:17
  62.8 2.4 collective-permute-start.10
  65.2 3.4 %collective-permute-start.11 = (f32[128,8,1,128]{3,1,2,0:T(8,128)S(1)}, f32[128,8,1,128]{3,1,2,0:T(8,128)S(1)}, u32[]{:S(2)}, u32[]{:S(2)}) collective-permute-start(f32[128,8,1,128]{3,1,2,0:T(8,128)S(1)} %bitcast.41), channel_id=1, source_target_pairs={{0,1},{1,2},{2,3},{3,4},{4,5},{5,6},{6,7},{8,9},{9,10},{10,11},{11... | collective-permute-start | bytes 1572872 | tf_op jit(solution)/shard_map/ppermute | solution.py:17
  68.7 1.3 collective-permute-start.6
  70.0 6.0 %collective-permute-start.7 = (f32[1,8,8,128]{3,2,1,0:T(8,128)S(1)}, f32[1,8,8,128]{3,2,1,0:T(8,128)S(1)}, u32[]{:S(2)}, u32[]{:S(2)}) collective-permute-start(f32[1,8,8,128]{3,2,1,0:T(8,128)S(1)} %get-tuple-element.37), channel_id=1, source_target_pairs={{0,64},{1,65},{2,66},{3,67},{4,68},{5,69},{6,70},{7,71},{8,72},{9,... | collective-permute-start | bytes 98312 | tf_op jit(solution)/shard_map/ppermute | solution.py:17
  76.2 16.8 %collective-permute-done.6 = f32[1,8,8,128]{3,2,1,0:T(8,128)S(1)} collective-permute-done((f32[1,8,8,128]{3,2,1,0:T(8,128)S(1)}, f32[1,8,8,128]{3,2,1,0:T(8,128)S(1)}, u32[]{:S(2)}, u32[]{:S(2)}) %collective-permute-start.6) | collective-permute-done | bytes 32800 | tf_op jit(solution)/shard_map/ppermute | solution.py:18
  93.0 9.6 %multiply_add_fusion.4 = f32[128,8,8,128]{3,2,1,0:T(8,128)S(1)} fusion(f32[128,8,8,128]{3,2,1,0:T(8,128)S(1)} %multiply_add_fusion.5, f32[128,8,8,128]{3,2,1,0:T(8,128)S(1)} %copy-done, f32[128,8,1,128]{3,2,1,0:T(1,128)S(1)} %bitcast.31, f32[130,1,8,128]{3,2,1,0:T(8,128)S(1)} %pad.78, f32[1,8,8,128]{3,2,1,0:T(8,128)S(1)} %collective-permute-done.6, ...), kind=kLoop, calls=%fused_computation.120 | loop fusion | flops 44040192 | bytes 23150592 | tf_op jit(solution)/shard_map/add | solution.py:69
  102.7 1.3 collective-permute-start.14
  104.6 3.1 %collective-permute-start.15 = (f32[128,1,8,128]{3,2,1,0:T(8,128)S(1)}, f32[128,1,8,128]{3,2,1,0:T(8,128)S(1)}, u32[]{:S(2)}, u32[]{:S(2)}) collective-permute-start(f32[128,1,8,128]{3,2,1,0:T(8,128)S(1)} %get-tuple-element.29), channel_id=1, source_target_pairs={{0,8},{8,16},{16,24},{24,32},{32,40},{40,48},{48,56},{1,9},{9,17},... | collective-permute-start | bytes 1572872 | tf_op jit(solution)/shard_map/ppermute | solution.py:17
  107.7 1.9 collective-permute-start.16
  109.6 4.0 %collective-permute-start.17 = (f32[128,8,1,128]{3,1,2,0:T(8,128)S(1)}, f32[128,8,1,128]{3,1,2,0:T(8,128)S(1)}, u32[]{:S(2)}, u32[]{:S(2)}) collective-permute-start(f32[128,8,1,128]{3,1,2,0:T(8,128)S(1)} %bitcast.42), channel_id=1, source_target_pairs={{0,1},{1,2},{2,3},{3,4},{4,5},{5,6},{6,7},{8,9},{9,10},{10,11},{11... | collective-permute-start | bytes 1572872 | tf_op jit(solution)/shard_map/ppermute | solution.py:17
  113.6 1.3 collective-permute-start.12
  114.9 6.0 %collective-permute-start.13 = (f32[1,8,8,128]{3,2,1,0:T(8,128)S(1)}, f32[1,8,8,128]{3,2,1,0:T(8,128)S(1)}, u32[]{:S(2)}, u32[]{:S(2)}) collective-permute-start(f32[1,8,8,128]{3,2,1,0:T(8,128)S(1)} %get-tuple-element.31), channel_id=1, source_target_pairs={{0,64},{1,65},{2,66},{3,67},{4,68},{5,69},{6,70},{7,71},{8,72},{9,... | collective-permute-start | bytes 98312 | tf_op jit(solution)/shard_map/ppermute | solution.py:17
  121.1 14.8 %collective-permute-done.12 = f32[1,8,8,128]{3,2,1,0:T(8,128)S(1)} collective-permute-done((f32[1,8,8,128]{3,2,1,0:T(8,128)S(1)}, f32[1,8,8,128]{3,2,1,0:T(8,128)S(1)}, u32[]{:S(2)}, u32[]{:S(2)}) %collective-permute-start.12) | collective-permute-done | bytes 32800 | tf_op jit(solution)/shard_map/ppermute | solution.py:18
  135.9 9.6 %multiply_add_fusion.3 = f32[128,8,8,128]{3,2,1,0:T(8,128)S(1)} fusion(f32[128,8,8,128]{3,2,1,0:T(8,128)S(1)} %multiply_add_fusion.4, f32[128,8,8,128]{3,2,1,0:T(8,128)S(1)} %copy-done, f32[128,8,1,128]{3,2,1,0:T(1,128)S(1)} %bitcast.32, f32[130,1,8,128]{3,2,1,0:T(8,128)S(1)} %pad.82, f32[1,8,8,128]{3,2,1,0:T(8,128)S(1)} %collective-permute-done.12, ...), kind=kLoop, calls=%fused_computation.119 | loop fusion | flops 44040192 | bytes 23150592 | tf_op jit(solution)/shard_map/add | solution.py:69
  145.6 1.3 collective-permute-start.20
  147.6 3.1 %collective-permute-start.21 = (f32[128,1,8,128]{3,2,1,0:T(8,128)S(1)}, f32[128,1,8,128]{3,2,1,0:T(8,128)S(1)}, u32[]{:S(2)}, u32[]{:S(2)}) collective-permute-start(f32[128,1,8,128]{3,2,1,0:T(8,128)S(1)} %get-tuple-element.23), channel_id=1, source_target_pairs={{0,8},{8,16},{16,24},{24,32},{32,40},{40,48},{48,56},{1,9},{9,17},... | collective-permute-start | bytes 1572872 | tf_op jit(solution)/shard_map/ppermute | solution.py:17
  150.7 1.9 collective-permute-start.23
  152.6 4.8 %collective-permute-start.22 = (f32[128,8,1,128]{3,1,2,0:T(8,128)S(1)}, f32[128,8,1,128]{3,1,2,0:T(8,128)S(1)}, u32[]{:S(2)}, u32[]{:S(2)}) collective-permute-start(f32[128,8,1,128]{3,1,2,0:T(8,128)S(1)} %bitcast.43), channel_id=1, source_target_pairs={{1,0},{2,1},{3,2},{4,3},{5,4},{6,5},{7,6},{9,8},{10,9},{11,10},{12... | collective-permute-start | bytes 1572872 | tf_op jit(solution)/shard_map/ppermute | solution.py:18
  158.7 6.2 %collective-permute-start.19 = (f32[1,8,8,128]{3,2,1,0:T(8,128)S(1)}, f32[1,8,8,128]{3,2,1,0:T(8,128)S(1)}, u32[]{:S(2)}, u32[]{:S(2)}) collective-permute-start(f32[1,8,8,128]{3,2,1,0:T(8,128)S(1)} %get-tuple-element.25), channel_id=1, source_target_pairs={{0,64},{1,65},{2,66},{3,67},{4,68},{5,69},{6,70},{7,71},{8,72},{9,... | collective-permute-start | bytes 98312 | tf_op jit(solution)/shard_map/ppermute | solution.py:17
  165.1 12.6 %collective-permute-done.18 = f32[1,8,8,128]{3,2,1,0:T(8,128)S(1)} collective-permute-done((f32[1,8,8,128]{3,2,1,0:T(8,128)S(1)}, f32[1,8,8,128]{3,2,1,0:T(8,128)S(1)}, u32[]{:S(2)}, u32[]{:S(2)}) %collective-permute-start.18) | collective-permute-done | bytes 32800 | tf_op jit(solution)/shard_map/ppermute | solution.py:18
  177.7 9.6 %multiply_add_fusion.2 = f32[128,8,8,128]{3,2,1,0:T(8,128)S(1)} fusion(f32[128,8,8,128]{3,2,1,0:T(8,128)S(1)} %multiply_add_fusion.3, f32[128,8,8,128]{3,2,1,0:T(8,128)S(1)} %copy-done, f32[128,8,1,128]{3,2,1,0:T(1,128)S(1)} %bitcast.38, f32[130,1,8,128]{3,2,1,0:T(8,128)S(1)} %pad.86, f32[1,8,8,128]{3,2,1,0:T(8,128)S(1)} %collective-permute-done.18, ...), kind=kLoop, calls=%fused_computation.118 | loop fusion | flops 44040192 | bytes 23150592 | tf_op jit(solution)/shard_map/add | solution.py:69
  189.3 3.3 %collective-permute-start.27 = (f32[128,1,8,128]{3,2,1,0:T(8,128)S(1)}, f32[128,1,8,128]{3,2,1,0:T(8,128)S(1)}, u32[]{:S(2)}, u32[]{:S(2)}) collective-permute-start(f32[128,1,8,128]{3,2,1,0:T(8,128)S(1)} %get-tuple-element.17), channel_id=1, source_target_pairs={{0,8},{8,16},{16,24},{24,32},{32,40},{40,48},{48,56},{1,9},{9,17},... | collective-permute-start | bytes 1572872 | tf_op jit(solution)/shard_map/ppermute | solution.py:17
  192.7 4.2 %collective-permute-start.28 = (f32[128,8,1,128]{3,1,2,0:T(8,128)S(1)}, f32[128,8,1,128]{3,1,2,0:T(8,128)S(1)}, u32[]{:S(2)}, u32[]{:S(2)}) collective-permute-start(f32[128,8,1,128]{3,1,2,0:T(8,128)S(1)} %bitcast.50), channel_id=1, source_target_pairs={{1,0},{2,1},{3,2},{4,3},{5,4},{6,5},{7,6},{9,8},{10,9},{11,10},{12... | collective-permute-start | bytes 1572872 | tf_op jit(solution)/shard_map/ppermute | solution.py:18
  196.8 1.9 collective-permute-start.29
  200.1 6.0 %collective-permute-start.25 = (f32[1,8,8,128]{3,2,1,0:T(8,128)S(1)}, f32[1,8,8,128]{3,2,1,0:T(8,128)S(1)}, u32[]{:S(2)}, u32[]{:S(2)}) collective-permute-start(f32[1,8,8,128]{3,2,1,0:T(8,128)S(1)} %get-tuple-element.19), channel_id=1, source_target_pairs={{0,64},{1,65},{2,66},{3,67},{4,68},{5,69},{6,70},{7,71},{8,72},{9,... | collective-permute-start | bytes 98312 | tf_op jit(solution)/shard_map/ppermute | solution.py:17
  206.3 18.5 %collective-permute-done.24 = f32[1,8,8,128]{3,2,1,0:T(8,128)S(1)} collective-permute-done((f32[1,8,8,128]{3,2,1,0:T(8,128)S(1)}, f32[1,8,8,128]{3,2,1,0:T(8,128)S(1)}, u32[]{:S(2)}, u32[]{:S(2)}) %collective-permute-start.24) | collective-permute-done | bytes 32800 | tf_op jit(solution)/shard_map/ppermute | solution.py:18
  224.8 9.6 %multiply_add_fusion.1 = f32[128,8,8,128]{3,2,1,0:T(8,128)S(1)} fusion(f32[128,8,8,128]{3,2,1,0:T(8,128)S(1)} %multiply_add_fusion.2, f32[128,8,8,128]{3,2,1,0:T(8,128)S(1)} %copy-done, f32[128,8,1,128]{3,2,1,0:T(1,128)S(1)} %bitcast.34, f32[130,1,8,128]{3,2,1,0:T(8,128)S(1)} %pad.90, f32[1,8,8,128]{3,2,1,0:T(8,128)S(1)} %collective-permute-done.24, ...), kind=kLoop, calls=%fused_computation.117 | loop fusion | flops 44040192 | bytes 23150592 | tf_op jit(solution)/shard_map/add | solution.py:69
  234.5 1.3 collective-permute-start.32
  236.4 3.1 %collective-permute-start.33 = (f32[128,1,8,128]{3,2,1,0:T(8,128)S(1)}, f32[128,1,8,128]{3,2,1,0:T(8,128)S(1)}, u32[]{:S(2)}, u32[]{:S(2)}) collective-permute-start(f32[128,1,8,128]{3,2,1,0:T(8,128)S(1)} %get-tuple-element.11), channel_id=1, source_target_pairs={{0,8},{8,16},{16,24},{24,32},{32,40},{40,48},{48,56},{1,9},{9,17},... | collective-permute-start | bytes 1572872 | tf_op jit(solution)/shard_map/ppermute | solution.py:17
  239.5 1.9 collective-permute-start.34
  241.4 4.0 %collective-permute-start.35 = (f32[128,8,1,128]{3,1,2,0:T(8,128)S(1)}, f32[128,8,1,128]{3,1,2,0:T(8,128)S(1)}, u32[]{:S(2)}, u32[]{:S(2)}) collective-permute-start(f32[128,8,1,128]{3,1,2,0:T(8,128)S(1)} %bitcast.45), channel_id=1, source_target_pairs={{0,1},{1,2},{2,3},{3,4},{4,5},{5,6},{6,7},{8,9},{9,10},{10,11},{11... | collective-permute-start | bytes 1572872 | tf_op jit(solution)/shard_map/ppermute | solution.py:17
  246.7 6.0 %collective-permute-start.31 = (f32[1,8,8,128]{3,2,1,0:T(8,128)S(1)}, f32[1,8,8,128]{3,2,1,0:T(8,128)S(1)}, u32[]{:S(2)}, u32[]{:S(2)}) collective-permute-start(f32[1,8,8,128]{3,2,1,0:T(8,128)S(1)} %get-tuple-element.13), channel_id=1, source_target_pairs={{0,64},{1,65},{2,66},{3,67},{4,68},{5,69},{6,70},{7,71},{8,72},{9,... | collective-permute-start | bytes 98312 | tf_op jit(solution)/shard_map/ppermute | solution.py:17
  252.9 15.5 %collective-permute-done.30 = f32[1,8,8,128]{3,2,1,0:T(8,128)S(1)} collective-permute-done((f32[1,8,8,128]{3,2,1,0:T(8,128)S(1)}, f32[1,8,8,128]{3,2,1,0:T(8,128)S(1)}, u32[]{:S(2)}, u32[]{:S(2)}) %collective-permute-start.30) | collective-permute-done | bytes 32800 | tf_op jit(solution)/shard_map/ppermute | solution.py:18
  268.4 11.1 %add_reduce_fusion = (f32[8,8,128]{2,1,0:T(8,128)S(1)}, f32[8,8,128]{2,1,0:T(8,128)S(1)}, f32[128,8,8,128]{3,2,1,0:T(8,128)}) fusion(f32[128,8,8,128]{3,2,1,0:T(8,128)S(1)} %multiply_add_fusion.1, f32[128,8,8,128]{3,2,1,0:T(8,128)S(1)} %copy-done, f32[130,1,8,128]{3,2,1,0:T(8,128)S(1)} %pad.94, f32[1,8,8,128]{3,2,1,0:T(8,128)S(1)} %collective-permute-done.30, ...), kind=kLoop, calls=%fused_computation.122 | loop fusion | flops 48218112 | bytes 23216128 | tf_op jit(solution)/shard_map/reduce_sum | solution.py:81
  279.6 8.4 %all_to_all.6 = f32[2,1,16384]{2,1,0:T(1,128)S(1)} all-to-all(f32[2,1,16384]{2,1,0:T(1,128)S(1)} %broadcast_in_dim.2), channel_id=1, replica_groups=mesh['south'=2,'east'=8,'down'=8] {'south'}, dimensions={0} | all-to-all | bytes 262144 | tf_op jit(solution)/shard_map/all_to_all | solution.py:31
  288.3 5.1 %subtract_multiply_fusion = f32[128,8,8,128]{3,2,1,0:T(8,128)} fusion(f32[128,8,8,128]{3,2,1,0:T(8,128)} %get-tuple-element.8, f32[8,8,128]{2,1,0:T(8,128)S(1)} %get-tuple-element.46, f32[8,8,128]{2,1,0:T(8,128)S(1)} %get-tuple-element.45), kind=kLoop, calls=%fused_computation.114 | loop fusion | flops 2097152 | bytes 8454144 | tf_op jit(solution)/shard_map/mul | solution.py:87
  (75 shorter events, 13.1 us)
Async XLA Ops:
  1.9 43.7 %collective-permute-start.2 = (f32[128,1,8,128]{3,2,1,0:T(8,128)S(1)}, f32[128,1,8,128]{3,2,1,0:T(8,128)S(1)}, u32[]{:S(2)}, u32[]{:S(2)}) collective-permute-start(f32[128,1,8,128]{3,2,1,0:T(8,128)S(1)} %get-tuple-element.42), channel_id=1, source_target_pairs={{8,0},{16,8},{24,16},{32,24},{40,32},{48,40},{56,48},{9,1},{17,9},... | collective-permute-start | bytes 1572872 | tf_op jit(solution)/shard_map/ppermute | solution.py:18
  3.2 42.5 %collective-permute-start.3 = (f32[128,1,8,128]{3,2,1,0:T(8,128)S(1)}, f32[128,1,8,128]{3,2,1,0:T(8,128)S(1)}, u32[]{:S(2)}, u32[]{:S(2)}) collective-permute-start(f32[128,1,8,128]{3,2,1,0:T(8,128)S(1)} %get-tuple-element.41), channel_id=1, source_target_pairs={{0,8},{8,16},{16,24},{24,32},{32,40},{40,48},{48,56},{1,9},{9,17},... | collective-permute-start | bytes 1572872 | tf_op jit(solution)/shard_map/ppermute | solution.py:17
  6.3 39.5 %copy-start.2 = (f32[128,8,8,128]{3,2,1,0:T(8,128)S(1)}, f32[128,8,8,128]{3,2,1,0:T(8,128)}, u32[]{:S(2)}) copy-start(f32[128,8,8,128]{3,2,1,0:T(8,128)} %param.5) | copy-start | bytes 12582916
  11.0 34.7 %collective-permute-start.4 = (f32[128,8,1,128]{3,1,2,0:T(8,128)S(1)}, f32[128,8,1,128]{3,1,2,0:T(8,128)}, u32[]{:S(2)}, u32[]{:S(2)}) collective-permute-start(f32[128,8,1,128]{3,1,2,0:T(8,128)S(1)} %bitcast.46), channel_id=1, source_target_pairs={{1,0},{2,1},{3,2},{4,3},{5,4},{6,5},{7,6},{9,8},{10,9},{11,10},{12... | collective-permute-start | bytes 1572872 | tf_op jit(solution)/shard_map/ppermute | solution.py:18
  14.3 31.5 %collective-permute-start.5 = (f32[128,8,1,128]{3,1,2,0:T(8,128)S(1)}, f32[128,8,1,128]{3,1,2,0:T(8,128)}, u32[]{:S(2)}, u32[]{:S(2)}) collective-permute-start(f32[128,8,1,128]{3,1,2,0:T(8,128)S(1)} %bitcast.40), channel_id=1, source_target_pairs={{0,1},{1,2},{2,3},{3,4},{4,5},{5,6},{6,7},{8,9},{9,10},{10,11},{11... | collective-permute-start | bytes 1572872 | tf_op jit(solution)/shard_map/ppermute | solution.py:17
  18.5 19.9 %collective-permute-start.1 = (f32[1,8,8,128]{3,2,1,0:T(8,128)S(1)}, f32[1,8,8,128]{3,2,1,0:T(8,128)S(1)}, u32[]{:S(2)}, u32[]{:S(2)}) collective-permute-start(f32[1,8,8,128]{3,2,1,0:T(8,128)S(1)} %get-tuple-element.44), channel_id=1, source_target_pairs={{0,64},{1,65},{2,66},{3,67},{4,68},{5,69},{6,70},{7,71},{8,72},{9,... | collective-permute-start | bytes 98312 | tf_op jit(solution)/shard_map/ppermute | solution.py:17
  38.3 7.3 %collective-permute-start = (f32[1,8,8,128]{3,2,1,0:T(8,128)S(1)}, f32[1,8,8,128]{3,2,1,0:T(8,128)S(1)}, u32[]{:S(2)}, u32[]{:S(2)}) collective-permute-start(f32[1,8,8,128]{3,2,1,0:T(8,128)S(1)} %get-tuple-element.43), channel_id=1, source_target_pairs={{64,0},{65,1},{66,2},{67,3},{68,4},{69,5},{70,6},{71,7},{72,8},{73... | collective-permute-start | bytes 98312 | tf_op jit(solution)/shard_map/ppermute | solution.py:18
  39.6 6.1 %copy-start = (f32[128,8,8,128]{3,2,1,0:T(8,128)S(1)}, f32[128,8,8,128]{3,2,1,0:T(8,128)}, u32[]{:S(2)}) copy-start(f32[128,8,8,128]{3,2,1,0:T(8,128)} %param.7) | copy-start | bytes 12582916
  39.6 6.1 %copy-start.1 = (f32[128,8,8,128]{3,2,1,0:T(8,128)S(1)}, f32[128,8,8,128]{3,2,1,0:T(8,128)}, u32[]{:S(2)}) copy-start(f32[128,8,8,128]{3,2,1,0:T(8,128)} %param.6) | copy-start | bytes 12582916
  57.7 12.2 %collective-permute-start.8 = (f32[128,1,8,128]{3,2,1,0:T(8,128)S(1)}, f32[128,1,8,128]{3,2,1,0:T(8,128)S(1)}, u32[]{:S(2)}, u32[]{:S(2)}) collective-permute-start(f32[128,1,8,128]{3,2,1,0:T(8,128)S(1)} %get-tuple-element.36), channel_id=1, source_target_pairs={{8,0},{16,8},{24,16},{32,24},{40,32},{48,40},{56,48},{9,1},{17,9},... | collective-permute-start | bytes 1572872 | tf_op jit(solution)/shard_map/ppermute | solution.py:18
  59.7 16.4 %collective-permute-start.9 = (f32[128,1,8,128]{3,2,1,0:T(8,128)S(1)}, f32[128,1,8,128]{3,2,1,0:T(8,128)S(1)}, u32[]{:S(2)}, u32[]{:S(2)}) collective-permute-start(f32[128,1,8,128]{3,2,1,0:T(8,128)S(1)} %get-tuple-element.35), channel_id=1, source_target_pairs={{0,8},{8,16},{16,24},{24,32},{32,40},{40,48},{48,56},{1,9},{9,17},... | collective-permute-start | bytes 1572872 | tf_op jit(solution)/shard_map/ppermute | solution.py:17
  62.8 30.2 %collective-permute-start.10 = (f32[128,8,1,128]{3,1,2,0:T(8,128)S(1)}, f32[128,8,1,128]{3,1,2,0:T(8,128)S(1)}, u32[]{:S(2)}, u32[]{:S(2)}) collective-permute-start(f32[128,8,1,128]{3,1,2,0:T(8,128)S(1)} %bitcast.47), channel_id=1, source_target_pairs={{1,0},{2,1},{3,2},{4,3},{5,4},{6,5},{7,6},{9,8},{10,9},{11,10},{12... | collective-permute-start | bytes 1572872 | tf_op jit(solution)/shard_map/ppermute | solution.py:18
  65.2 27.7 %collective-permute-start.11 = (f32[128,8,1,128]{3,1,2,0:T(8,128)S(1)}, f32[128,8,1,128]{3,1,2,0:T(8,128)S(1)}, u32[]{:S(2)}, u32[]{:S(2)}) collective-permute-start(f32[128,8,1,128]{3,1,2,0:T(8,128)S(1)} %bitcast.41), channel_id=1, source_target_pairs={{0,1},{1,2},{2,3},{3,4},{4,5},{5,6},{6,7},{8,9},{9,10},{10,11},{11... | collective-permute-start | bytes 1572872 | tf_op jit(solution)/shard_map/ppermute | solution.py:17
  68.7 24.3 %collective-permute-start.6 = (f32[1,8,8,128]{3,2,1,0:T(8,128)S(1)}, f32[1,8,8,128]{3,2,1,0:T(8,128)S(1)}, u32[]{:S(2)}, u32[]{:S(2)}) collective-permute-start(f32[1,8,8,128]{3,2,1,0:T(8,128)S(1)} %get-tuple-element.38), channel_id=1, source_target_pairs={{64,0},{65,1},{66,2},{67,3},{68,4},{69,5},{70,6},{71,7},{72,8},{73... | collective-permute-start | bytes 98312 | tf_op jit(solution)/shard_map/ppermute | solution.py:18
  70.0 23.0 %collective-permute-start.7 = (f32[1,8,8,128]{3,2,1,0:T(8,128)S(1)}, f32[1,8,8,128]{3,2,1,0:T(8,128)S(1)}, u32[]{:S(2)}, u32[]{:S(2)}) collective-permute-start(f32[1,8,8,128]{3,2,1,0:T(8,128)S(1)} %get-tuple-element.37), channel_id=1, source_target_pairs={{0,64},{1,65},{2,66},{3,67},{4,68},{5,69},{6,70},{7,71},{8,72},{9,... | collective-permute-start | bytes 98312 | tf_op jit(solution)/shard_map/ppermute | solution.py:17
  102.7 12.2 %collective-permute-start.14 = (f32[128,1,8,128]{3,2,1,0:T(8,128)S(1)}, f32[128,1,8,128]{3,2,1,0:T(8,128)S(1)}, u32[]{:S(2)}, u32[]{:S(2)}) collective-permute-start(f32[128,1,8,128]{3,2,1,0:T(8,128)S(1)} %get-tuple-element.30), channel_id=1, source_target_pairs={{8,0},{16,8},{24,16},{32,24},{40,32},{48,40},{56,48},{9,1},{17,9},... | collective-permute-start | bytes 1572872 | tf_op jit(solution)/shard_map/ppermute | solution.py:18
  104.6 16.4 %collective-permute-start.15 = (f32[128,1,8,128]{3,2,1,0:T(8,128)S(1)}, f32[128,1,8,128]{3,2,1,0:T(8,128)S(1)}, u32[]{:S(2)}, u32[]{:S(2)}) collective-permute-start(f32[128,1,8,128]{3,2,1,0:T(8,128)S(1)} %get-tuple-element.29), channel_id=1, source_target_pairs={{0,8},{8,16},{16,24},{24,32},{32,40},{40,48},{48,56},{1,9},{9,17},... | collective-permute-start | bytes 1572872 | tf_op jit(solution)/shard_map/ppermute | solution.py:17
  107.7 28.2 %collective-permute-start.16 = (f32[128,8,1,128]{3,1,2,0:T(8,128)S(1)}, f32[128,8,1,128]{3,1,2,0:T(8,128)S(1)}, u32[]{:S(2)}, u32[]{:S(2)}) collective-permute-start(f32[128,8,1,128]{3,1,2,0:T(8,128)S(1)} %bitcast.48), channel_id=1, source_target_pairs={{1,0},{2,1},{3,2},{4,3},{5,4},{6,5},{7,6},{9,8},{10,9},{11,10},{12... | collective-permute-start | bytes 1572872 | tf_op jit(solution)/shard_map/ppermute | solution.py:18
  109.6 26.3 %collective-permute-start.17 = (f32[128,8,1,128]{3,1,2,0:T(8,128)S(1)}, f32[128,8,1,128]{3,1,2,0:T(8,128)S(1)}, u32[]{:S(2)}, u32[]{:S(2)}) collective-permute-start(f32[128,8,1,128]{3,1,2,0:T(8,128)S(1)} %bitcast.42), channel_id=1, source_target_pairs={{0,1},{1,2},{2,3},{3,4},{4,5},{5,6},{6,7},{8,9},{9,10},{10,11},{11... | collective-permute-start | bytes 1572872 | tf_op jit(solution)/shard_map/ppermute | solution.py:17
  113.6 22.3 %collective-permute-start.12 = (f32[1,8,8,128]{3,2,1,0:T(8,128)S(1)}, f32[1,8,8,128]{3,2,1,0:T(8,128)S(1)}, u32[]{:S(2)}, u32[]{:S(2)}) collective-permute-start(f32[1,8,8,128]{3,2,1,0:T(8,128)S(1)} %get-tuple-element.32), channel_id=1, source_target_pairs={{64,0},{65,1},{66,2},{67,3},{68,4},{69,5},{70,6},{71,7},{72,8},{73... | collective-permute-start | bytes 98312 | tf_op jit(solution)/shard_map/ppermute | solution.py:18
  114.9 21.0 %collective-permute-start.13 = (f32[1,8,8,128]{3,2,1,0:T(8,128)S(1)}, f32[1,8,8,128]{3,2,1,0:T(8,128)S(1)}, u32[]{:S(2)}, u32[]{:S(2)}) collective-permute-start(f32[1,8,8,128]{3,2,1,0:T(8,128)S(1)} %get-tuple-element.31), channel_id=1, source_target_pairs={{0,64},{1,65},{2,66},{3,67},{4,68},{5,69},{6,70},{7,71},{8,72},{9,... | collective-permute-start | bytes 98312 | tf_op jit(solution)/shard_map/ppermute | solution.py:17
  145.6 13.1 %collective-permute-start.20 = (f32[128,1,8,128]{3,2,1,0:T(8,128)S(1)}, f32[128,1,8,128]{3,2,1,0:T(8,128)S(1)}, u32[]{:S(2)}, u32[]{:S(2)}) collective-permute-start(f32[128,1,8,128]{3,2,1,0:T(8,128)S(1)} %get-tuple-element.24), channel_id=1, source_target_pairs={{8,0},{16,8},{24,16},{32,24},{40,32},{48,40},{56,48},{9,1},{17,9},... | collective-permute-start | bytes 1572872 | tf_op jit(solution)/shard_map/ppermute | solution.py:18
  147.6 17.4 %collective-permute-start.21 = (f32[128,1,8,128]{3,2,1,0:T(8,128)S(1)}, f32[128,1,8,128]{3,2,1,0:T(8,128)S(1)}, u32[]{:S(2)}, u32[]{:S(2)}) collective-permute-start(f32[128,1,8,128]{3,2,1,0:T(8,128)S(1)} %get-tuple-element.23), channel_id=1, source_target_pairs={{0,8},{8,16},{16,24},{24,32},{32,40},{40,48},{48,56},{1,9},{9,17},... | collective-permute-start | bytes 1572872 | tf_op jit(solution)/shard_map/ppermute | solution.py:17
  150.7 27.0 %collective-permute-start.23 = (f32[128,8,1,128]{3,1,2,0:T(8,128)S(1)}, f32[128,8,1,128]{3,1,2,0:T(8,128)S(1)}, u32[]{:S(2)}, u32[]{:S(2)}) collective-permute-start(f32[128,8,1,128]{3,1,2,0:T(8,128)S(1)} %bitcast.49), channel_id=1, source_target_pairs={{0,1},{1,2},{2,3},{3,4},{4,5},{5,6},{6,7},{8,9},{9,10},{10,11},{11... | collective-permute-start | bytes 1572872 | tf_op jit(solution)/shard_map/ppermute | solution.py:17
  152.6 25.1 %collective-permute-start.22 = (f32[128,8,1,128]{3,1,2,0:T(8,128)S(1)}, f32[128,8,1,128]{3,1,2,0:T(8,128)S(1)}, u32[]{:S(2)}, u32[]{:S(2)}) collective-permute-start(f32[128,8,1,128]{3,1,2,0:T(8,128)S(1)} %bitcast.43), channel_id=1, source_target_pairs={{1,0},{2,1},{3,2},{4,3},{5,4},{6,5},{7,6},{9,8},{10,9},{11,10},{12... | collective-permute-start | bytes 1572872 | tf_op jit(solution)/shard_map/ppermute | solution.py:18
  157.4 20.2 %collective-permute-start.18 = (f32[1,8,8,128]{3,2,1,0:T(8,128)S(1)}, f32[1,8,8,128]{3,2,1,0:T(8,128)S(1)}, u32[]{:S(2)}, u32[]{:S(2)}) collective-permute-start(f32[1,8,8,128]{3,2,1,0:T(8,128)S(1)} %get-tuple-element.26), channel_id=1, source_target_pairs={{64,0},{65,1},{66,2},{67,3},{68,4},{69,5},{70,6},{71,7},{72,8},{73... | collective-permute-start | bytes 98312 | tf_op jit(solution)/shard_map/ppermute | solution.py:18
  158.7 18.9 %collective-permute-start.19 = (f32[1,8,8,128]{3,2,1,0:T(8,128)S(1)}, f32[1,8,8,128]{3,2,1,0:T(8,128)S(1)}, u32[]{:S(2)}, u32[]{:S(2)}) collective-permute-start(f32[1,8,8,128]{3,2,1,0:T(8,128)S(1)} %get-tuple-element.25), channel_id=1, source_target_pairs={{0,64},{1,65},{2,66},{3,67},{4,68},{5,69},{6,70},{7,71},{8,72},{9,... | collective-permute-start | bytes 98312 | tf_op jit(solution)/shard_map/ppermute | solution.py:17
  187.4 12.7 %collective-permute-start.26 = (f32[128,1,8,128]{3,2,1,0:T(8,128)S(1)}, f32[128,1,8,128]{3,2,1,0:T(8,128)S(1)}, u32[]{:S(2)}, u32[]{:S(2)}) collective-permute-start(f32[128,1,8,128]{3,2,1,0:T(8,128)S(1)} %get-tuple-element.18), channel_id=1, source_target_pairs={{8,0},{16,8},{24,16},{32,24},{40,32},{48,40},{56,48},{9,1},{17,9},... | collective-permute-start | bytes 1572872 | tf_op jit(solution)/shard_map/ppermute | solution.py:18
  189.3 16.9 %collective-permute-start.27 = (f32[128,1,8,128]{3,2,1,0:T(8,128)S(1)}, f32[128,1,8,128]{3,2,1,0:T(8,128)S(1)}, u32[]{:S(2)}, u32[]{:S(2)}) collective-permute-start(f32[128,1,8,128]{3,2,1,0:T(8,128)S(1)} %get-tuple-element.17), channel_id=1, source_target_pairs={{0,8},{8,16},{16,24},{24,32},{32,40},{40,48},{48,56},{1,9},{9,17},... | collective-permute-start | bytes 1572872 | tf_op jit(solution)/shard_map/ppermute | solution.py:17
  192.7 32.1 %collective-permute-start.28 = (f32[128,8,1,128]{3,1,2,0:T(8,128)S(1)}, f32[128,8,1,128]{3,1,2,0:T(8,128)S(1)}, u32[]{:S(2)}, u32[]{:S(2)}) collective-permute-start(f32[128,8,1,128]{3,1,2,0:T(8,128)S(1)} %bitcast.50), channel_id=1, source_target_pairs={{1,0},{2,1},{3,2},{4,3},{5,4},{6,5},{7,6},{9,8},{10,9},{11,10},{12... | collective-permute-start | bytes 1572872 | tf_op jit(solution)/shard_map/ppermute | solution.py:18
  196.8 27.9 %collective-permute-start.29 = (f32[128,8,1,128]{3,1,2,0:T(8,128)S(1)}, f32[128,8,1,128]{3,1,2,0:T(8,128)S(1)}, u32[]{:S(2)}, u32[]{:S(2)}) collective-permute-start(f32[128,8,1,128]{3,1,2,0:T(8,128)S(1)} %bitcast.44), channel_id=1, source_target_pairs={{0,1},{1,2},{2,3},{3,4},{4,5},{5,6},{6,7},{8,9},{9,10},{10,11},{11... | collective-permute-start | bytes 1572872 | tf_op jit(solution)/shard_map/ppermute | solution.py:17
  198.8 26.0 %collective-permute-start.24 = (f32[1,8,8,128]{3,2,1,0:T(8,128)S(1)}, f32[1,8,8,128]{3,2,1,0:T(8,128)S(1)}, u32[]{:S(2)}, u32[]{:S(2)}) collective-permute-start(f32[1,8,8,128]{3,2,1,0:T(8,128)S(1)} %get-tuple-element.20), channel_id=1, source_target_pairs={{64,0},{65,1},{66,2},{67,3},{68,4},{69,5},{70,6},{71,7},{72,8},{73... | collective-permute-start | bytes 98312 | tf_op jit(solution)/shard_map/ppermute | solution.py:18
  200.1 24.7 %collective-permute-start.25 = (f32[1,8,8,128]{3,2,1,0:T(8,128)S(1)}, f32[1,8,8,128]{3,2,1,0:T(8,128)S(1)}, u32[]{:S(2)}, u32[]{:S(2)}) collective-permute-start(f32[1,8,8,128]{3,2,1,0:T(8,128)S(1)} %get-tuple-element.19), channel_id=1, source_target_pairs={{0,64},{1,65},{2,66},{3,67},{4,68},{5,69},{6,70},{7,71},{8,72},{9,... | collective-permute-start | bytes 98312 | tf_op jit(solution)/shard_map/ppermute | solution.py:17
  234.5 12.2 %collective-permute-start.32 = (f32[128,1,8,128]{3,2,1,0:T(8,128)S(1)}, f32[128,1,8,128]{3,2,1,0:T(8,128)S(1)}, u32[]{:S(2)}, u32[]{:S(2)}) collective-permute-start(f32[128,1,8,128]{3,2,1,0:T(8,128)S(1)} %get-tuple-element.12), channel_id=1, source_target_pairs={{8,0},{16,8},{24,16},{32,24},{40,32},{48,40},{56,48},{9,1},{17,9},... | collective-permute-start | bytes 1572872 | tf_op jit(solution)/shard_map/ppermute | solution.py:18
  236.4 16.4 %collective-permute-start.33 = (f32[128,1,8,128]{3,2,1,0:T(8,128)S(1)}, f32[128,1,8,128]{3,2,1,0:T(8,128)S(1)}, u32[]{:S(2)}, u32[]{:S(2)}) collective-permute-start(f32[128,1,8,128]{3,2,1,0:T(8,128)S(1)} %get-tuple-element.11), channel_id=1, source_target_pairs={{0,8},{8,16},{16,24},{24,32},{32,40},{40,48},{48,56},{1,9},{9,17},... | collective-permute-start | bytes 1572872 | tf_op jit(solution)/shard_map/ppermute | solution.py:17
  239.5 28.9 %collective-permute-start.34 = (f32[128,8,1,128]{3,1,2,0:T(8,128)S(1)}, f32[128,8,1,128]{3,1,2,0:T(8,128)S(1)}, u32[]{:S(2)}, u32[]{:S(2)}) collective-permute-start(f32[128,8,1,128]{3,1,2,0:T(8,128)S(1)} %bitcast.51), channel_id=1, source_target_pairs={{1,0},{2,1},{3,2},{4,3},{5,4},{6,5},{7,6},{9,8},{10,9},{11,10},{12... | collective-permute-start | bytes 1572872 | tf_op jit(solution)/shard_map/ppermute | solution.py:18
  241.4 26.9 %collective-permute-start.35 = (f32[128,8,1,128]{3,1,2,0:T(8,128)S(1)}, f32[128,8,1,128]{3,1,2,0:T(8,128)S(1)}, u32[]{:S(2)}, u32[]{:S(2)}) collective-permute-start(f32[128,8,1,128]{3,1,2,0:T(8,128)S(1)} %bitcast.45), channel_id=1, source_target_pairs={{0,1},{1,2},{2,3},{3,4},{4,5},{5,6},{6,7},{8,9},{9,10},{10,11},{11... | collective-permute-start | bytes 1572872 | tf_op jit(solution)/shard_map/ppermute | solution.py:17
  245.4 23.0 %collective-permute-start.30 = (f32[1,8,8,128]{3,2,1,0:T(8,128)S(1)}, f32[1,8,8,128]{3,2,1,0:T(8,128)S(1)}, u32[]{:S(2)}, u32[]{:S(2)}) collective-permute-start(f32[1,8,8,128]{3,2,1,0:T(8,128)S(1)} %get-tuple-element.14), channel_id=1, source_target_pairs={{64,0},{65,1},{66,2},{67,3},{68,4},{69,5},{70,6},{71,7},{72,8},{73... | collective-permute-start | bytes 98312 | tf_op jit(solution)/shard_map/ppermute | solution.py:18
  246.7 21.7 %collective-permute-start.31 = (f32[1,8,8,128]{3,2,1,0:T(8,128)S(1)}, f32[1,8,8,128]{3,2,1,0:T(8,128)S(1)}, u32[]{:S(2)}, u32[]{:S(2)}) collective-permute-start(f32[1,8,8,128]{3,2,1,0:T(8,128)S(1)} %get-tuple-element.13), channel_id=1, source_target_pairs={{0,64},{1,65},{2,66},{3,67},{4,68},{5,69},{6,70},{7,71},{8,72},{9,... | collective-permute-start | bytes 98312 | tf_op jit(solution)/shard_map/ppermute | solution.py:17
where the time goes:
time: 295 us; the launch traced here: 293 us
  starting transfers between devices  107 us (36%)
  waiting for transfers between devices  96.5 us (33%)
  other arithmetic  66.7 us (23%)
  local copies, waits for them, and re-layouts  13.7 us (5%)
  blocking collectives  8.44 us (3%)
    ppermute x18, waiting for transfers between devices, with_halo(): lax.ppermute(leading, axis, [(b, a) for a, b in up])  81.6 us
    ppermute x18, starting transfers between devices, with_halo(): lax.ppermute(last, axis, up)  72.5 us
    add x5, other arithmetic, advance(): middle - flow_j * slopes[0] - flow_i * slopes[1] - flow_k * slopes[2]  50.3 us
    ppermute x18, starting transfers between devices, with_halo(): lax.ppermute(leading, axis, [(b, a) for a, b in up])  34 us
    ppermute x18, waiting for transfers between devices, with_halo(): lax.ppermute(last, axis, up)  15 us
    reduce_sum x1, other arithmetic, per_device(): jnp.sum(moved, axis=0, keepdims=True)  11.1 us
    slice x16, local copies, waits for them, and re-layouts, with_halo(): last = lax.slice_in_dim(shard, length - width, length, axis=dim)  9.09 us
    all_to_all x1, blocking collectives, sent_to_all(): lax.all_to_all(jnp.broadcast_to(shard[None], (devices, *shard.shape)), ax...  8.44 us
  transfers between devices with their start and end apart: 36, of which 7 were waited for; matrix products, arithmetic and copies ran while one was open for 4% of the time, Pallas kernels for 0%

commit v1 on v0

v1 whole, which is shorter than its diff:
```python
import jax
import jax.numpy as jnp
from jax import lax
from jax.experimental import pallas as pl
from jax.experimental.pallas import tpu as pltpu
from jax.sharding import PartitionSpec as P


STEPS = 6
RATE = 0.05
F32 = jnp.float32
VMEM = pltpu.VMEM
SMEM = pltpu.SMEM


def swap_pairs(devices, first):
    pairs = []
    for a in range(first, devices - 1, 2):
        pairs += [(a, a + 1), (a + 1, a)]
    return pairs


def combine(c, jl, ju, il, iu, kl, ku, fj, fi, fk):
    total = (jl + ju) + (il + iu) + (kl + ku)
    return (
        c * (1.0 - 6.0 * RATE)
        + RATE * total
        - fj * (ju - jl)
        - fi * (iu - il)
        - fk * (ku - kl)
    )


def face_body(side, flags, f, fj, fi, fk, halo, e1, e2, s, out):
    rows, ni, nl = out.shape
    nk = f.shape[1] // ni
    last = flags[0] == side
    k = jnp.where(last, nk - 1, 0)
    kin = jnp.where(last, nk - 2, 1)
    sign = jnp.where(last, F32(1), F32(-1))
    i_even = flags[1] == 0
    low_south = flags[2] == 0
    sub = lax.broadcasted_iota(jnp.int32, (ni, nl), 0)
    e1_edge = sub == jnp.where(i_even, ni - 1, 0)
    first_i = sub == 0
    last_i = sub == ni - 1

    def at(ref, j, kk):
        return ref[j, pl.ds(kk, ni, stride=nk), :]

    beyond = s[pl.ds(k, ni, stride=nk), :]
    zero = jnp.zeros_like(beyond)

    def row(j, prev, cur, nxt):
        r1 = jnp.broadcast_to(e1[j, pl.ds(k, 1), :], (ni, nl))
        r2 = jnp.broadcast_to(e2[j, pl.ds(k, 1), :], (ni, nl))
        edge = jnp.where(e1_edge, r1, r2)
        il = jnp.where(first_i, edge, pltpu.roll(cur, 1, 0))
        iu = jnp.where(last_i, edge, pltpu.roll(cur, ni - 1, 0))
        h = halo[j]
        inner = at(f, j, kin)
        out[j] = combine(
            cur, prev, nxt, il, iu, inner, h,
            at(fj, j, k), at(fi, j, k), sign * at(fk, j, k),
        )

    def body(j, carry):
        prev, cur = carry
        nxt = at(f, j + 1, k)
        row(j, prev, cur, nxt)
        return cur, nxt

    prev, cur = lax.fori_loop(
        0, rows - 1, body, (jnp.where(low_south, zero, beyond), at(f, 0, k)), unroll=False
    )
    row(rows - 1, prev, cur, jnp.where(low_south, beyond, zero))


def update_rows(flags, f, fj, fi, fk, ha, hb, e1, e2, s, emit):
    rows, ni, nk, nl = f.shape
    i_even = flags[1] == 0
    low_south = flags[2] == 0
    sub = lax.broadcasted_iota(jnp.int32, (nk, nl), 0)
    a_edge = sub == jnp.where(flags[0] == 0, nk - 1, 0)
    first_k = sub == 0
    last_k = sub == nk - 1

    def row(j, prev, cur, nxt):
        x1 = e1[j]
        x2 = e2[j]
        below = jnp.where(i_even, x2, x1)
        above = jnp.where(i_even, x1, x2)
        new = []
        for i in range(ni):
            c = cur[i]
            ra = jnp.broadcast_to(ha[j, pl.ds(i, 1), :], (nk, nl))
            rb = jnp.broadcast_to(hb[j, pl.ds(i, 1), :], (nk, nl))
            edge = jnp.where(a_edge, ra, rb)
            kl = jnp.where(first_k, edge, pltpu.roll(c, 1, 0))
            ku = jnp.where(last_k, edge, pltpu.roll(c, nk - 1, 0))
            il = below if i == 0 else cur[i - 1]
            iu = above if i == ni - 1 else cur[i + 1]
            new.append(
                combine(c, prev[i], nxt[i], il, iu, kl, ku, fj[j, i], fi[j, i], fk[j, i])
            )
        emit(j, new)

    def body(j, carry):
        prev, cur = carry
        nxt = tuple(f[j + 1, i] for i in range(ni))
        row(j, prev, cur, nxt)
        return cur, nxt

    zero = jnp.zeros((nk, nl), F32)
    start = (
        tuple(jnp.where(low_south, zero, s[i]) for i in range(ni)),
        tuple(f[0, i] for i in range(ni)),
    )
    prev, cur = lax.fori_loop(0, rows - 1, body, start, unroll=False)
    row(rows - 1, prev, cur, tuple(jnp.where(low_south, s[i], zero) for i in range(ni)))


def full_body(flags, f, fj, fi, fk, ha, hb, e1, e2, s, order, out, g1, g2, gs):
    rows, ni, _, _ = f.shape
    i_even = flags[1] == 0

    def emit(j, new):
        for i in range(ni):
            out[j, i] = new[i]
        g1[j] = jnp.where(i_even, new[-1], new[0])
        g2[j] = jnp.where(i_even, new[0], new[-1])

    update_rows(flags, f, fj, fi, fk, ha, hb, e1, e2, s, emit)
    gs[...] = out[jnp.where(flags[2] == 0, rows - 1, 0)]


def final_body(flags, f, fj, fi, fk, ha, hb, e1, e2, s, out, stats):
    rows, ni, nk, nl = f.shape

    def emit(j, new):
        for i in range(ni):
            out[j, i] = new[i]

    update_rows(flags, f, fj, fi, fk, ha, hb, e1, e2, s, emit)
    zero = tuple(jnp.zeros((nk, nl), F32) for _ in range(ni))

    def add(j, sums):
        return tuple(a + out[j, i] for i, a in enumerate(sums))

    means = tuple(a * (1.0 / rows) for a in lax.fori_loop(0, rows, add, zero, unroll=2))

    def add_square(j, sums):
        new = []
        for i, a in enumerate(sums):
            d = out[j, i] - means[i]
            new.append(a + d * d)
        return tuple(new)

    spread = lax.fori_loop(0, rows, add_square, zero, unroll=2)
    for i in range(ni):
        stats[0, i] = means[i]
        stats[1, i] = spread[i]


def scale_body(f, mine, other, out):
    rows, ni, _, _ = f.shape
    mean = []
    scale = []
    for i in range(ni):
        apart = mine[0, i] - other[0, i]
        mean.append(0.5 * (mine[0, i] + other[0, i]))
        squares = mine[1, i] + other[1, i] + (0.5 * rows) * (apart * apart)
        scale.append(lax.rsqrt(squares * (0.5 / rows) + 0.0001))

    def body(j, _):
        for i in range(ni):
            out[j, i] = (f[j, i] - mean[i]) * scale[i]
        return 0

    lax.fori_loop(0, rows, body, 0, unroll=2)


def edges_body(flags, f, g1, g2, ga, gb, gs):
    rows, ni, nk, _ = f.shape
    i_even = flags[1] == 0
    a_last = flags[0] == 0

    def body(j, _):
        g1[j] = jnp.where(i_even, f[j, ni - 1], f[j, 0])
        g2[j] = jnp.where(i_even, f[j, 0], f[j, ni - 1])
        lo = f[j, :, 0, :]
        hi = f[j, :, nk - 1, :]
        ga[j] = jnp.where(a_last, hi, lo)
        gb[j] = jnp.where(a_last, lo, hi)
        return 0

    lax.fori_loop(0, rows, body, 0)
    gs[...] = f[jnp.where(flags[2] == 0, rows - 1, 0)]


def call(body, args, outs, mib=2):
    flagged = args[0].dtype == jnp.int32
    specs = [pl.BlockSpec(memory_space=VMEM) for _ in args]
    if flagged:
        specs[0] = pl.BlockSpec(memory_space=SMEM)
    return pl.pallas_call(
        body,
        out_shape=[jax.ShapeDtypeStruct(o, F32) for o in outs],
        in_specs=specs,
        out_specs=[pl.BlockSpec(memory_space=VMEM) for _ in outs],
        compiler_params=pltpu.CompilerParams(vmem_limit_bytes=mib << 20),
    )(*args)


def per_device(field, fj, fi, fk):
    import functools

    rows, ni, nk, nl = field.shape
    flags = jnp.stack(
        [
            lax.axis_index("down") % 2,
            lax.axis_index("east") % 2,
            lax.axis_index("south"),
        ]
    ).astype(jnp.int32)

    def swap(x, axis, first):
        return lax.ppermute(x, axis, swap_pairs(lax.axis_size(axis), first))

    flat = (rows, ni * nk, nl)
    kface, iface, jface = (rows, ni, nl), (rows, nk, nl), (ni, nk, nl)
    fjr, fir, fkr = (x.reshape(flat) for x in (fj, fi, fk))

    g1, g2, ga, gb, gs = call(edges_body, [flags, field], [iface, iface, kface, kface, jface])
    ha = swap(ga, "down", 0)
    hb = swap(gb, "down", 1)
    e2 = swap(g2, "east", 1)
    e1 = swap(g1, "east", 0)
    s = swap(gs, "south", 0)
    for _ in range(STEPS - 1):
        fr = field.reshape(flat)
        sr = s.reshape(ni * nk, nl)
        (ga,) = call(functools.partial(face_body, 0), [flags, fr, fjr, fir, fkr, ha, e1, e2, sr], [kface])
        (gb,) = call(functools.partial(face_body, 1), [flags, fr, fjr, fir, fkr, hb, e1, e2, sr], [kface])
        ha_next = swap(ga, "down", 0)
        hb_next = swap(gb, "down", 1)
        field, g1, g2, gs = call(
            full_body, [flags, field, fj, fi, fk, ha, hb, e1, e2, s, gb],
            [field.shape, iface, iface, jface],
        )
        ha, hb = ha_next, hb_next
        e2 = swap(g2, "east", 1)
        e1 = swap(g1, "east", 0)
        s = swap(gs, "south", 0)
    field, stats = call(
        final_body, [flags, field, fj, fi, fk, ha, hb, e1, e2, s],
        [field.shape, (2, ni, nk, nl)], 12,
    )
    other = swap(stats, "south", 0)
    (standardized,) = call(scale_body, [field, stats, other], [field.shape], 12)
    return (standardized, field)


def solution(mesh):
    spec = P("south", "east", "down", None)
    return jax.shard_map(
        per_device,
        mesh=mesh,
        in_specs=(spec,) * 4,
        out_specs=(spec, spec),
        check_vma=False,
    )
```

time: 295 us -> 210 us (0.71)
  the two profiles are of different devices: /device:TPU:96 before, /device:TPU:46 now
where the time goes in v1:
time: 210 us; the launch traced here: 209 us
  waiting for transfers between devices  85.8 us (41%)
  Pallas kernels  60.7 us (29%)
  starting transfers between devices  52.8 us (25%)
  local copies, waits for them, and re-layouts  8.91 us (4%)
    ppermute x31, waiting for transfers between devices, swap(): return lax.ppermute(x, axis, swap_pairs(lax.axis_size(axis), first))  85.8 us
    pallas_call x18, Pallas kernels, call(): pl.pallas_call(body, out_shape=[jax.ShapeDtypeStruct(o, F32) for o in out...  60.7 us
    ppermute x31, starting transfers between devices, swap(): return lax.ppermute(x, axis, swap_pairs(lax.axis_size(axis), first))  52.8 us
    unnamed x14, local copies, waits for them, and re-layouts  8.91 us
  transfers between devices with their start and end apart: 31, of which 7 were waited for; matrix products, arithmetic and copies ran while one was open for 0% of the time, Pallas kernels for 23%

profile of v1, /device:TPU:46, one launch (start us, length us, event | category | flops | bytes accessed | tf_op | source)
XLA Modules:
  0.0 209.2 jit_solution(6972708903943834973)
XLA Ops:
  0.7 2.3 %copy-done.5 = f32[128,8,8,128]{3,2,1,0:T(8,128)S(1)} copy-done((f32[128,8,8,128]{3,2,1,0:T(8,128)S(1)}, f32[128,8,8,128]{3,2,1,0:T(8,128)}, u32[]{:S(2)}) %copy-start.5) | copy-done | bytes 4194328
  3.1 2.3 %shard_map.59 = (f32[128,8,128]{2,1,0:T(8,128)S(1)}, f32[128,8,128]{2,1,0:T(8,128)S(1)}, f32[128,8,128]{2,1,0:T(8,128)S(1)}, f32[128,8,128]{2,1,0:T(8,128)S(1)}, f32[8,8,128]{2,1,0:T(8,128)S(1)}) custom-call(s32[3]{0:T(128)S(1)} %pad_add_fusion.flags, f32[128,8,8,128]{3,2,1,0:T(8,128)S(1)} %copy-done.5), custom_call_target="tpu_custom_call" | custom-call | tf_op jit(solution)/shard_map/pallas_call | solution.py:206
  5.4 0.9 collective-permute-start
  6.3 2.5 %collective-permute-start.3 = (f32[128,8,128]{2,1,0:T(8,128)S(1)}, f32[128,8,128]{2,1,0:T(8,128)S(1)}, u32[]{:S(2)}, u32[]{:S(2)}) collective-permute-start(f32[128,8,128]{2,1,0:T(8,128)S(1)} %get-tuple-element.32), channel_id=1, source_target_pairs={{8,16},{16,8},{24,32},{32,24},{40,48},{48,40},{9,17},{17,9},{25,33... | collective-permute-start | bytes 1572872 | tf_op jit(solution)/shard_map/ppermute | solution.py:228
  8.8 4.5 %collective-permute-start.1 = (f32[128,8,128]{2,1,0:T(8,128)S(1)}, f32[128,8,128]{2,1,0:T(8,128)S(1)}, u32[]{:S(2)}, u32[]{:S(2)}) collective-permute-start(f32[128,8,128]{2,1,0:T(8,128)S(1)} %get-tuple-element.30), channel_id=1, source_target_pairs={{1,2},{2,1},{3,4},{4,3},{5,6},{6,5},{9,10},{10,9},{11,12},{12,11},... | collective-permute-start | bytes 1572872 | tf_op jit(solution)/shard_map/ppermute | solution.py:228
  13.2 1.5 collective-permute-start.4
  14.7 16.3 %collective-permute-done.4.s = f32[8,8,128]{2,1,0:T(8,128)S(1)} collective-permute-done((f32[8,8,128]{2,1,0:T(8,128)S(1)}, f32[8,8,128]{2,1,0:T(8,128)S(1)}, u32[]{:S(2)}, u32[]{:S(2)}) %collective-permute-start.4) | collective-permute-done | bytes 32800 | tf_op jit(solution)/shard_map/ppermute | solution.py:228
  31.0 2.2 %copy-done.1 = f32[128,8,8,128]{3,2,1,0:T(8,128)S(1)} copy-done((f32[128,8,8,128]{3,2,1,0:T(8,128)S(1)}, f32[128,8,8,128]{3,2,1,0:T(8,128)}, u32[]{:S(2)}) %copy-start.1) | copy-done | bytes 4194328
  33.2 2.2 %copy-done.3 = f32[128,8,8,128]{3,2,1,0:T(8,128)S(1)} copy-done((f32[128,8,8,128]{3,2,1,0:T(8,128)S(1)}, f32[128,8,8,128]{3,2,1,0:T(8,128)}, u32[]{:S(2)}) %copy-start.3) | copy-done | bytes 4194328
  35.4 2.4 %shard_map.62 = f32[128,8,128]{2,1,0:T(8,128)S(1)} custom-call(s32[3]{0:T(128)S(1)} %pad_add_fusion.flags, f32[128,64,128]{2,1,0:T(8,128)S(1)} %bitcast.46, f32[128,64,128]{2,1,0:T(8,128)S(1)} %bitcast.16, f32[128,64,128]{2,1,0:T(8,128)S(1)} %bitcast.26, f32[128,64,128]{2,1,0:T(8,128)S(1)} %bitcast.36, f32[128,8,128]{2,1,0:T(8,128)S(1)} %collective-permute-done.ha.halo, ...), custom_call_target="tpu_custom_call" | custom-call | tf_op jit(solution)/shard_map/pallas_call | solution.py:206
  37.8 1.0 collective-permute-start.5
  38.8 2.4 %shard_map.60.order = f32[128,8,128]{2,1,0:T(8,128)S(1)} custom-call(s32[3]{0:T(128)S(1)} %pad_add_fusion.flags, f32[128,64,128]{2,1,0:T(8,128)S(1)} %bitcast.47, f32[128,64,128]{2,1,0:T(8,128)S(1)} %bitcast.17, f32[128,64,128]{2,1,0:T(8,128)S(1)} %bitcast.27, f32[128,64,128]{2,1,0:T(8,128)S(1)} %bitcast.37, ...), custom_call_target="tpu_custom_call" | custom-call | tf_op jit(solution)/shard_map/pallas_call | solution.py:206
  41.2 4.7 %shard_map.61 = (f32[128,8,8,128]{3,2,1,0:T(8,128)S(1)}, f32[128,8,128]{2,1,0:T(8,128)S(1)}, f32[128,8,128]{2,1,0:T(8,128)S(1)}, f32[8,8,128]{2,1,0:T(8,128)S(1)}) custom-call(s32[3]{0:T(128)S(1)} %pad_add_fusion.flags, f32[128,8,8,128]{3,2,1,0:T(8,128)S(1)} %copy-done.5, f32[128,8,8,128]{3,2,1,0:T(8,128)S(1)} %copy-done, f32[128,8,8,128]{3,2,1,0:T(8,128)S(1)} %copy-done.1, ...), custom_call_target="tpu_custom_call" | custom-call | tf_op jit(solution)/shard_map/pallas_call | solution.py:206
  46.0 2.4 %collective-permute-start.8 = (f32[128,8,128]{2,1,0:T(8,128)S(1)}, f32[128,8,128]{2,1,0:T(8,128)S(1)}, u32[]{:S(2)}, u32[]{:S(2)}) collective-permute-start(f32[128,8,128]{2,1,0:T(8,128)S(1)} %get-tuple-element.36), channel_id=1, source_target_pairs={{8,16},{16,8},{24,32},{32,24},{40,48},{48,40},{9,17},{17,9},{25,33... | collective-permute-start | bytes 1572872 | tf_op jit(solution)/shard_map/ppermute | solution.py:228
  48.5 4.4 %collective-permute-start.6 = (f32[128,8,128]{2,1,0:T(8,128)S(1)}, f32[128,8,128]{2,1,0:T(8,128)S(1)}, u32[]{:S(2)}, u32[]{:S(2)}) collective-permute-start(f32[128,8,128]{2,1,0:T(8,128)S(1)} %shard_map.60.order), channel_id=1, source_target_pairs={{1,2},{2,1},{3,4},{4,3},{5,6},{6,5},{9,10},{10,9},{11,12},{12,11},... | collective-permute-start | bytes 1572872 | tf_op jit(solution)/shard_map/ppermute | solution.py:228
  52.9 2.5 %collective-permute-start.9 = (f32[8,8,128]{2,1,0:T(8,128)S(1)}, f32[8,8,128]{2,1,0:T(8,128)S(1)}, u32[]{:S(2)}, u32[]{:S(2)}) collective-permute-start(f32[8,8,128]{2,1,0:T(8,128)S(1)} %get-tuple-element.37), channel_id=1, source_target_pairs={{0,64},{64,0},{1,65},{65,1},{2,66},{66,2},{3,67},{67,3},{4,68},{68... | collective-permute-start | bytes 98312 | tf_op jit(solution)/shard_map/ppermute | solution.py:228
  55.4 13.2 %collective-permute-done.9.s = f32[8,8,128]{2,1,0:T(8,128)S(1)} collective-permute-done((f32[8,8,128]{2,1,0:T(8,128)S(1)}, f32[8,8,128]{2,1,0:T(8,128)S(1)}, u32[]{:S(2)}, u32[]{:S(2)}) %collective-permute-start.9) | collective-permute-done | bytes 32800 | tf_op jit(solution)/shard_map/ppermute | solution.py:228
  68.6 2.4 %shard_map.65 = f32[128,8,128]{2,1,0:T(8,128)S(1)} custom-call(s32[3]{0:T(128)S(1)} %pad_add_fusion.flags, f32[128,64,128]{2,1,0:T(8,128)S(1)} %bitcast.54, f32[128,64,128]{2,1,0:T(8,128)S(1)} %bitcast.18, f32[128,64,128]{2,1,0:T(8,128)S(1)} %bitcast.28, f32[128,64,128]{2,1,0:T(8,128)S(1)} %bitcast.38, f32[128,8,128]{2,1,0:T(8,128)S(1)} %collective-permute-done.5.ha.halo, ...), custom_call_target="tpu_custom_call" | custom-call | tf_op jit(solution)/shard_map/pallas_call | solution.py:206
  71.1 2.4 %shard_map.63.order = f32[128,8,128]{2,1,0:T(8,128)S(1)} custom-call(s32[3]{0:T(128)S(1)} %pad_add_fusion.flags, f32[128,64,128]{2,1,0:T(8,128)S(1)} %bitcast.55, f32[128,64,128]{2,1,0:T(8,128)S(1)} %bitcast.19, f32[128,64,128]{2,1,0:T(8,128)S(1)} %bitcast.29, f32[128,64,128]{2,1,0:T(8,128)S(1)} %bitcast.39, ...), custom_call_target="tpu_custom_call" | custom-call | tf_op jit(solution)/shard_map/pallas_call | solution.py:206
  73.6 4.7 %shard_map.64 = (f32[128,8,8,128]{3,2,1,0:T(8,128)S(1)}, f32[128,8,128]{2,1,0:T(8,128)S(1)}, f32[128,8,128]{2,1,0:T(8,128)S(1)}, f32[8,8,128]{2,1,0:T(8,128)S(1)}) custom-call(s32[3]{0:T(128)S(1)} %pad_add_fusion.flags, f32[128,8,8,128]{3,2,1,0:T(8,128)S(1)} %get-tuple-element.34.f, f32[128,8,8,128]{3,2,1,0:T(8,128)S(1)} %copy-done, ...), custom_call_target="tpu_custom_call" | custom-call | tf_op jit(solution)/shard_map/pallas_call | solution.py:206
  78.5 1.9 collective-permute-start.13
  80.4 4.7 %collective-permute-start.11 = (f32[128,8,128]{2,1,0:T(8,128)S(1)}, f32[128,8,128]{2,1,0:T(8,128)S(1)}, u32[]{:S(2)}, u32[]{:S(2)}) collective-permute-start(f32[128,8,128]{2,1,0:T(8,128)S(1)} %shard_map.63.order), channel_id=1, source_target_pairs={{1,2},{2,1},{3,4},{4,3},{5,6},{6,5},{9,10},{10,9},{11,12},{12,11},... | collective-permute-start | bytes 1572872 | tf_op jit(solution)/shard_map/ppermute | solution.py:228
  85.4 12.6 %collective-permute-done.14.s = f32[8,8,128]{2,1,0:T(8,128)S(1)} collective-permute-done((f32[8,8,128]{2,1,0:T(8,128)S(1)}, f32[8,8,128]{2,1,0:T(8,128)S(1)}, u32[]{:S(2)}, u32[]{:S(2)}) %collective-permute-start.14) | collective-permute-done | bytes 32800 | tf_op jit(solution)/shard_map/ppermute | solution.py:228
  98.0 2.4 %shard_map.68 = f32[128,8,128]{2,1,0:T(8,128)S(1)} custom-call(s32[3]{0:T(128)S(1)} %pad_add_fusion.flags, f32[128,64,128]{2,1,0:T(8,128)S(1)} %bitcast.50, f32[128,64,128]{2,1,0:T(8,128)S(1)} %bitcast.20, f32[128,64,128]{2,1,0:T(8,128)S(1)} %bitcast.30, f32[128,64,128]{2,1,0:T(8,128)S(1)} %bitcast.40, f32[128,8,128]{2,1,0:T(8,128)S(1)} %collective-permute-done.10.ha.halo, ...), custom_call_target="tpu_custom_call" | custom-call | tf_op jit(solution)/shard_map/pallas_call | solution.py:206
  100.5 2.4 %shard_map.66.order = f32[128,8,128]{2,1,0:T(8,128)S(1)} custom-call(s32[3]{0:T(128)S(1)} %pad_add_fusion.flags, f32[128,64,128]{2,1,0:T(8,128)S(1)} %bitcast.51, f32[128,64,128]{2,1,0:T(8,128)S(1)} %bitcast.21, f32[128,64,128]{2,1,0:T(8,128)S(1)} %bitcast.31, f32[128,64,128]{2,1,0:T(8,128)S(1)} %bitcast.41, ...), custom_call_target="tpu_custom_call" | custom-call | tf_op jit(solution)/shard_map/pallas_call | solution.py:206
  103.0 4.7 %shard_map.67 = (f32[128,8,8,128]{3,2,1,0:T(8,128)S(1)}, f32[128,8,128]{2,1,0:T(8,128)S(1)}, f32[128,8,128]{2,1,0:T(8,128)S(1)}, f32[8,8,128]{2,1,0:T(8,128)S(1)}) custom-call(s32[3]{0:T(128)S(1)} %pad_add_fusion.flags, f32[128,8,8,128]{3,2,1,0:T(8,128)S(1)} %get-tuple-element.38.f, f32[128,8,8,128]{3,2,1,0:T(8,128)S(1)} %copy-done, ...), custom_call_target="tpu_custom_call" | custom-call | tf_op jit(solution)/shard_map/pallas_call | solution.py:206
  107.7 0.7 collective-permute-start.17
  108.4 1.9 collective-permute-start.18
  110.3 4.2 %collective-permute-start.16 = (f32[128,8,128]{2,1,0:T(8,128)S(1)}, f32[128,8,128]{2,1,0:T(8,128)S(1)}, u32[]{:S(2)}, u32[]{:S(2)}) collective-permute-start(f32[128,8,128]{2,1,0:T(8,128)S(1)} %shard_map.66.order), channel_id=1, source_target_pairs={{1,2},{2,1},{3,4},{4,3},{5,6},{6,5},{9,10},{10,9},{11,12},{12,11},... | collective-permute-start | bytes 1572872 | tf_op jit(solution)/shard_map/ppermute | solution.py:228
  114.5 2.2 %collective-permute-start.19 = (f32[8,8,128]{2,1,0:T(8,128)S(1)}, f32[8,8,128]{2,1,0:T(8,128)S(1)}, u32[]{:S(2)}, u32[]{:S(2)}) collective-permute-start(f32[8,8,128]{2,1,0:T(8,128)S(1)} %get-tuple-element.45), channel_id=1, source_target_pairs={{0,64},{64,0},{1,65},{65,1},{2,66},{66,2},{3,67},{67,3},{4,68},{68... | collective-permute-start | bytes 98312 | tf_op jit(solution)/shard_map/ppermute | solution.py:228
  116.7 12.7 %collective-permute-done.19.s = f32[8,8,128]{2,1,0:T(8,128)S(1)} collective-permute-done((f32[8,8,128]{2,1,0:T(8,128)S(1)}, f32[8,8,128]{2,1,0:T(8,128)S(1)}, u32[]{:S(2)}, u32[]{:S(2)}) %collective-permute-start.19) | collective-permute-done | bytes 32800 | tf_op jit(solution)/shard_map/ppermute | solution.py:228
  129.4 2.4 %shard_map.71 = f32[128,8,128]{2,1,0:T(8,128)S(1)} custom-call(s32[3]{0:T(128)S(1)} %pad_add_fusion.flags, f32[128,64,128]{2,1,0:T(8,128)S(1)} %bitcast.52, f32[128,64,128]{2,1,0:T(8,128)S(1)} %bitcast.22, f32[128,64,128]{2,1,0:T(8,128)S(1)} %bitcast.32, f32[128,64,128]{2,1,0:T(8,128)S(1)} %bitcast.42, f32[128,8,128]{2,1,0:T(8,128)S(1)} %collective-permute-done.15.ha.halo, ...), custom_call_target="tpu_custom_call" | custom-call | tf_op jit(solution)/shard_map/pallas_call | solution.py:206
  132.3 2.4 %shard_map.69.order = f32[128,8,128]{2,1,0:T(8,128)S(1)} custom-call(s32[3]{0:T(128)S(1)} %pad_add_fusion.flags, f32[128,64,128]{2,1,0:T(8,128)S(1)} %bitcast.53, f32[128,64,128]{2,1,0:T(8,128)S(1)} %bitcast.23, f32[128,64,128]{2,1,0:T(8,128)S(1)} %bitcast.33, f32[128,64,128]{2,1,0:T(8,128)S(1)} %bitcast.43, ...), custom_call_target="tpu_custom_call" | custom-call | tf_op jit(solution)/shard_map/pallas_call | solution.py:206
  134.7 4.7 %shard_map.70 = (f32[128,8,8,128]{3,2,1,0:T(8,128)S(1)}, f32[128,8,128]{2,1,0:T(8,128)S(1)}, f32[128,8,128]{2,1,0:T(8,128)S(1)}, f32[8,8,128]{2,1,0:T(8,128)S(1)}) custom-call(s32[3]{0:T(128)S(1)} %pad_add_fusion.flags, f32[128,8,8,128]{3,2,1,0:T(8,128)S(1)} %get-tuple-element.42.f, f32[128,8,8,128]{3,2,1,0:T(8,128)S(1)} %copy-done, ...), custom_call_target="tpu_custom_call" | custom-call | tf_op jit(solution)/shard_map/pallas_call | solution.py:206
  139.8 1.9 collective-permute-start.23
  141.7 4.2 %collective-permute-start.21 = (f32[128,8,128]{2,1,0:T(8,128)S(1)}, f32[128,8,128]{2,1,0:T(8,128)S(1)}, u32[]{:S(2)}, u32[]{:S(2)}) collective-permute-start(f32[128,8,128]{2,1,0:T(8,128)S(1)} %shard_map.69.order), channel_id=1, source_target_pairs={{1,2},{2,1},{3,4},{4,3},{5,6},{6,5},{9,10},{10,9},{11,12},{12,11},... | collective-permute-start | bytes 1572872 | tf_op jit(solution)/shard_map/ppermute | solution.py:228
  146.3 12.8 %collective-permute-done.24.s = f32[8,8,128]{2,1,0:T(8,128)S(1)} collective-permute-done((f32[8,8,128]{2,1,0:T(8,128)S(1)}, f32[8,8,128]{2,1,0:T(8,128)S(1)}, u32[]{:S(2)}, u32[]{:S(2)}) %collective-permute-start.24) | collective-permute-done | bytes 32800 | tf_op jit(solution)/shard_map/ppermute | solution.py:228
  159.1 2.4 %shard_map.74 = f32[128,8,128]{2,1,0:T(8,128)S(1)} custom-call(s32[3]{0:T(128)S(1)} %pad_add_fusion.flags, f32[128,64,128]{2,1,0:T(8,128)S(1)} %bitcast.48, f32[128,64,128]{2,1,0:T(8,128)S(1)} %bitcast.24, f32[128,64,128]{2,1,0:T(8,128)S(1)} %bitcast.34, f32[128,64,128]{2,1,0:T(8,128)S(1)} %bitcast.44, f32[128,8,128]{2,1,0:T(8,128)S(1)} %collective-permute-done.20.ha.halo, ...), custom_call_target="tpu_custom_call" | custom-call | tf_op jit(solution)/shard_map/pallas_call | solution.py:206
  162.2 2.4 %shard_map.72.order = f32[128,8,128]{2,1,0:T(8,128)S(1)} custom-call(s32[3]{0:T(128)S(1)} %pad_add_fusion.flags, f32[128,64,128]{2,1,0:T(8,128)S(1)} %bitcast.49, f32[128,64,128]{2,1,0:T(8,128)S(1)} %bitcast.25, f32[128,64,128]{2,1,0:T(8,128)S(1)} %bitcast.35, f32[128,64,128]{2,1,0:T(8,128)S(1)} %bitcast.45, ...), custom_call_target="tpu_custom_call" | custom-call | tf_op jit(solution)/shard_map/pallas_call | solution.py:206
  164.6 4.6 %collective-permute-start.26 = (f32[128,8,128]{2,1,0:T(8,128)S(1)}, f32[128,8,128]{2,1,0:T(8,128)S(1)}, u32[]{:S(2)}, u32[]{:S(2)}) collective-permute-start(f32[128,8,128]{2,1,0:T(8,128)S(1)} %shard_map.72.order), channel_id=1, source_target_pairs={{1,2},{2,1},{3,4},{4,3},{5,6},{6,5},{9,10},{10,9},{11,12},{12,11},... | collective-permute-start | bytes 1572872 | tf_op jit(solution)/shard_map/ppermute | solution.py:228
  169.2 4.7 %shard_map.73 = (f32[128,8,8,128]{3,2,1,0:T(8,128)S(1)}, f32[128,8,128]{2,1,0:T(8,128)S(1)}, f32[128,8,128]{2,1,0:T(8,128)S(1)}, f32[8,8,128]{2,1,0:T(8,128)S(1)}) custom-call(s32[3]{0:T(128)S(1)} %pad_add_fusion.flags, f32[128,8,8,128]{3,2,1,0:T(8,128)S(1)} %get-tuple-element.46.f, f32[128,8,8,128]{3,2,1,0:T(8,128)S(1)} %copy-done, ...), custom_call_target="tpu_custom_call" | custom-call | tf_op jit(solution)/shard_map/pallas_call | solution.py:206
  174.0 1.9 collective-permute-start.28
  176.0 2.4 %collective-permute-start.29 = (f32[8,8,128]{2,1,0:T(8,128)S(1)}, f32[8,8,128]{2,1,0:T(8,128)S(1)}, u32[]{:S(2)}, u32[]{:S(2)}) collective-permute-start(f32[8,8,128]{2,1,0:T(8,128)S(1)} %get-tuple-element.53), channel_id=1, source_target_pairs={{0,64},{64,0},{1,65},{65,1},{2,66},{66,2},{3,67},{67,3},{4,68},{68... | collective-permute-start | bytes 98312 | tf_op jit(solution)/shard_map/ppermute | solution.py:228
  178.3 12.4 %collective-permute-done.29.s = f32[8,8,128]{2,1,0:T(8,128)S(1)} collective-permute-done((f32[8,8,128]{2,1,0:T(8,128)S(1)}, f32[8,8,128]{2,1,0:T(8,128)S(1)}, u32[]{:S(2)}, u32[]{:S(2)}) %collective-permute-start.29) | collective-permute-done | bytes 32800 | tf_op jit(solution)/shard_map/ppermute | solution.py:228
  190.8 7.8 %shard_map.75 = (f32[128,8,8,128]{3,2,1,0:T(8,128)}, f32[2,8,8,128]{3,2,1,0:T(8,128)S(1)}) custom-call(s32[3]{0:T(128)S(1)} %pad_add_fusion.flags, f32[128,8,8,128]{3,2,1,0:T(8,128)S(1)} %get-tuple-element.50.f, f32[128,8,8,128]{3,2,1,0:T(8,128)S(1)} %copy-done, f32[128,8,8,128]{3,2,1,0:T(8,128)S(1)} %copy-done.2, f32[128,8,8,128]{3,2,1,0:T(8,128)S(1)} %copy-done.4, ...), custom_call_target="tpu_custom_call" | custom-call | tf_op jit(solution)/shard_map/pallas_call | solution.py:206
  198.7 5.8 %collective-permute-done.30.other = f32[2,8,8,128]{3,2,1,0:T(8,128)S(1)} collective-permute-done((f32[2,8,8,128]{3,2,1,0:T(8,128)S(1)}, f32[2,8,8,128]{3,2,1,0:T(8,128)S(1)}, u32[]{:S(2)}, u32[]{:S(2)}) %collective-permute-start.30) | collective-permute-done | bytes 65568 | tf_op jit(solution)/shard_map/ppermute | solution.py:228
  204.4 2.2 %copy-done.6 = f32[128,8,8,128]{3,2,1,0:T(8,128)S(1)} copy-done((f32[128,8,8,128]{3,2,1,0:T(8,128)S(1)}, f32[128,8,8,128]{3,2,1,0:T(8,128)}, u32[]{:S(2)}) %copy-start.6) | copy-done | bytes 4194328
  206.6 2.6 %shard_map.76 = f32[128,8,8,128]{3,2,1,0:T(8,128)} custom-call(f32[128,8,8,128]{3,2,1,0:T(8,128)S(1)} %copy-done.6, f32[2,8,8,128]{3,2,1,0:T(8,128)S(1)} %get-tuple-element.55.mine, f32[2,8,8,128]{3,2,1,0:T(8,128)S(1)} %collective-permute-done.30.other), custom_call_target="tpu_custom_call" | custom-call | tf_op jit(solution)/shard_map/pallas_call | solution.py:206
  (47 shorter events, 2.8 us)
Async XLA Ops:
  0.6 30.3 %copy-start = (f32[128,8,8,128]{3,2,1,0:T(8,128)S(1)}, f32[128,8,8,128]{3,2,1,0:T(8,128)}, u32[]{:S(2)}) copy-start(f32[128,8,8,128]{3,2,1,0:T(8,128)} %fj.11) | copy-start | bytes 12582916
  0.7 2.3 %copy-start.5 = (f32[128,8,8,128]{3,2,1,0:T(8,128)S(1)}, f32[128,8,8,128]{3,2,1,0:T(8,128)}, u32[]{:S(2)}) copy-start(f32[128,8,8,128]{3,2,1,0:T(8,128)} %f.3) | copy-start | bytes 12582916
  5.4 25.6 %collective-permute-start = (f32[128,8,128]{2,1,0:T(8,128)S(1)}, f32[128,8,128]{2,1,0:T(8,128)S(1)}, u32[]{:S(2)}, u32[]{:S(2)}) collective-permute-start(f32[128,8,128]{2,1,0:T(8,128)S(1)} %get-tuple-element.29), channel_id=1, source_target_pairs={{0,1},{1,0},{2,3},{3,2},{4,5},{5,4},{6,7},{7,6},{8,9},{9,8},{10,11... | collective-permute-start | bytes 1572872 | tf_op jit(solution)/shard_map/ppermute | solution.py:228
  6.3 24.7 %collective-permute-start.2 = (f32[128,8,128]{2,1,0:T(8,128)S(1)}, f32[128,8,128]{2,1,0:T(8,128)S(1)}, u32[]{:S(2)}, u32[]{:S(2)}) collective-permute-start(f32[128,8,128]{2,1,0:T(8,128)S(1)} %get-tuple-element.31), channel_id=1, source_target_pairs={{0,8},{8,0},{16,24},{24,16},{32,40},{40,32},{48,56},{56,48},{1,9},... | collective-permute-start | bytes 1572872 | tf_op jit(solution)/shard_map/ppermute | solution.py:228
  6.3 24.7 %collective-permute-start.3 = (f32[128,8,128]{2,1,0:T(8,128)S(1)}, f32[128,8,128]{2,1,0:T(8,128)S(1)}, u32[]{:S(2)}, u32[]{:S(2)}) collective-permute-start(f32[128,8,128]{2,1,0:T(8,128)S(1)} %get-tuple-element.32), channel_id=1, source_target_pairs={{8,16},{16,8},{24,32},{32,24},{40,48},{48,40},{9,17},{17,9},{25,33... | collective-permute-start | bytes 1572872 | tf_op jit(solution)/shard_map/ppermute | solution.py:228
  8.8 30.0 %collective-permute-start.1 = (f32[128,8,128]{2,1,0:T(8,128)S(1)}, f32[128,8,128]{2,1,0:T(8,128)S(1)}, u32[]{:S(2)}, u32[]{:S(2)}) collective-permute-start(f32[128,8,128]{2,1,0:T(8,128)S(1)} %get-tuple-element.30), channel_id=1, source_target_pairs={{1,2},{2,1},{3,4},{4,3},{5,6},{6,5},{9,10},{10,9},{11,12},{12,11},... | collective-permute-start | bytes 1572872 | tf_op jit(solution)/shard_map/ppermute | solution.py:228
  13.2 17.7 %collective-permute-start.4 = (f32[8,8,128]{2,1,0:T(8,128)S(1)}, f32[8,8,128]{2,1,0:T(8,128)S(1)}, u32[]{:S(2)}, u32[]{:S(2)}) collective-permute-start(f32[8,8,128]{2,1,0:T(8,128)S(1)} %get-tuple-element.33), channel_id=1, source_target_pairs={{0,64},{64,0},{1,65},{65,1},{2,66},{66,2},{3,67},{67,3},{4,68},{68... | collective-permute-start | bytes 98312 | tf_op jit(solution)/shard_map/ppermute | solution.py:228
  31.0 2.2 %copy-start.1 = (f32[128,8,8,128]{3,2,1,0:T(8,128)S(1)}, f32[128,8,8,128]{3,2,1,0:T(8,128)}, u32[]{:S(2)}) copy-start(f32[128,8,8,128]{3,2,1,0:T(8,128)} %fi.11) | copy-start | bytes 12582916
  33.2 2.2 %copy-start.3 = (f32[128,8,8,128]{3,2,1,0:T(8,128)S(1)}, f32[128,8,8,128]{3,2,1,0:T(8,128)}, u32[]{:S(2)}) copy-start(f32[128,8,8,128]{3,2,1,0:T(8,128)} %fk.11) | copy-start | bytes 12582916
  37.8 30.8 %collective-permute-start.5 = (f32[128,8,128]{2,1,0:T(8,128)S(1)}, f32[128,8,128]{2,1,0:T(8,128)S(1)}, u32[]{:S(2)}, u32[]{:S(2)}) collective-permute-start(f32[128,8,128]{2,1,0:T(8,128)S(1)} %shard_map.62), channel_id=1, source_target_pairs={{0,1},{1,0},{2,3},{3,2},{4,5},{5,4},{6,7},{7,6},{8,9},{9,8},{10,11... | collective-permute-start | bytes 1572872 | tf_op jit(solution)/shard_map/ppermute | solution.py:228
  45.9 22.7 %collective-permute-start.7 = (f32[128,8,128]{2,1,0:T(8,128)S(1)}, f32[128,8,128]{2,1,0:T(8,128)S(1)}, u32[]{:S(2)}, u32[]{:S(2)}) collective-permute-start(f32[128,8,128]{2,1,0:T(8,128)S(1)} %get-tuple-element.35), channel_id=1, source_target_pairs={{0,8},{8,0},{16,24},{24,16},{32,40},{40,32},{48,56},{56,48},{1,9},... | collective-permute-start | bytes 1572872 | tf_op jit(solution)/shard_map/ppermute | solution.py:228
  46.0 22.6 %collective-permute-start.8 = (f32[128,8,128]{2,1,0:T(8,128)S(1)}, f32[128,8,128]{2,1,0:T(8,128)S(1)}, u32[]{:S(2)}, u32[]{:S(2)}) collective-permute-start(f32[128,8,128]{2,1,0:T(8,128)S(1)} %get-tuple-element.36), channel_id=1, source_target_pairs={{8,16},{16,8},{24,32},{32,24},{40,48},{48,40},{9,17},{17,9},{25,33... | collective-permute-start | bytes 1572872 | tf_op jit(solution)/shard_map/ppermute | solution.py:228
  48.5 22.6 %collective-permute-start.6 = (f32[128,8,128]{2,1,0:T(8,128)S(1)}, f32[128,8,128]{2,1,0:T(8,128)S(1)}, u32[]{:S(2)}, u32[]{:S(2)}) collective-permute-start(f32[128,8,128]{2,1,0:T(8,128)S(1)} %shard_map.60.order), channel_id=1, source_target_pairs={{1,2},{2,1},{3,4},{4,3},{5,6},{6,5},{9,10},{10,9},{11,12},{12,11},... | collective-permute-start | bytes 1572872 | tf_op jit(solution)/shard_map/ppermute | solution.py:228
  52.9 15.7 %collective-permute-start.9 = (f32[8,8,128]{2,1,0:T(8,128)S(1)}, f32[8,8,128]{2,1,0:T(8,128)S(1)}, u32[]{:S(2)}, u32[]{:S(2)}) collective-permute-start(f32[8,8,128]{2,1,0:T(8,128)S(1)} %get-tuple-element.37), channel_id=1, source_target_pairs={{0,64},{64,0},{1,65},{65,1},{2,66},{66,2},{3,67},{67,3},{4,68},{68... | collective-permute-start | bytes 98312 | tf_op jit(solution)/shard_map/ppermute | solution.py:228
  71.0 26.9 %collective-permute-start.10 = (f32[128,8,128]{2,1,0:T(8,128)S(1)}, f32[128,8,128]{2,1,0:T(8,128)S(1)}, u32[]{:S(2)}, u32[]{:S(2)}) collective-permute-start(f32[128,8,128]{2,1,0:T(8,128)S(1)} %shard_map.65), channel_id=1, source_target_pairs={{0,1},{1,0},{2,3},{3,2},{4,5},{5,4},{6,7},{7,6},{8,9},{9,8},{10,11... | collective-permute-start | bytes 1572872 | tf_op jit(solution)/shard_map/ppermute | solution.py:228
  78.3 19.7 %collective-permute-start.12 = (f32[128,8,128]{2,1,0:T(8,128)S(1)}, f32[128,8,128]{2,1,0:T(8,128)S(1)}, u32[]{:S(2)}, u32[]{:S(2)}) collective-permute-start(f32[128,8,128]{2,1,0:T(8,128)S(1)} %get-tuple-element.39), channel_id=1, source_target_pairs={{0,8},{8,0},{16,24},{24,16},{32,40},{40,32},{48,56},{56,48},{1,9},... | collective-permute-start | bytes 1572872 | tf_op jit(solution)/shard_map/ppermute | solution.py:228
  78.5 19.5 %collective-permute-start.13 = (f32[128,8,128]{2,1,0:T(8,128)S(1)}, f32[128,8,128]{2,1,0:T(8,128)S(1)}, u32[]{:S(2)}, u32[]{:S(2)}) collective-permute-start(f32[128,8,128]{2,1,0:T(8,128)S(1)} %get-tuple-element.40), channel_id=1, source_target_pairs={{8,16},{16,8},{24,32},{32,24},{40,48},{48,40},{9,17},{17,9},{25,33... | collective-permute-start | bytes 1572872 | tf_op jit(solution)/shard_map/ppermute | solution.py:228
  80.4 20.1 %collective-permute-start.11 = (f32[128,8,128]{2,1,0:T(8,128)S(1)}, f32[128,8,128]{2,1,0:T(8,128)S(1)}, u32[]{:S(2)}, u32[]{:S(2)}) collective-permute-start(f32[128,8,128]{2,1,0:T(8,128)S(1)} %shard_map.63.order), channel_id=1, source_target_pairs={{1,2},{2,1},{3,4},{4,3},{5,6},{6,5},{9,10},{10,9},{11,12},{12,11},... | collective-permute-start | bytes 1572872 | tf_op jit(solution)/shard_map/ppermute | solution.py:228
  85.1 12.9 %collective-permute-start.14 = (f32[8,8,128]{2,1,0:T(8,128)S(1)}, f32[8,8,128]{2,1,0:T(8,128)S(1)}, u32[]{:S(2)}, u32[]{:S(2)}) collective-permute-start(f32[8,8,128]{2,1,0:T(8,128)S(1)} %get-tuple-element.41), channel_id=1, source_target_pairs={{0,64},{64,0},{1,65},{65,1},{2,66},{66,2},{3,67},{67,3},{4,68},{68... | collective-permute-start | bytes 98312 | tf_op jit(solution)/shard_map/ppermute | solution.py:228
  100.4 28.9 %collective-permute-start.15 = (f32[128,8,128]{2,1,0:T(8,128)S(1)}, f32[128,8,128]{2,1,0:T(8,128)S(1)}, u32[]{:S(2)}, u32[]{:S(2)}) collective-permute-start(f32[128,8,128]{2,1,0:T(8,128)S(1)} %shard_map.68), channel_id=1, source_target_pairs={{0,1},{1,0},{2,3},{3,2},{4,5},{5,4},{6,7},{7,6},{8,9},{9,8},{10,11... | collective-permute-start | bytes 1572872 | tf_op jit(solution)/shard_map/ppermute | solution.py:228
  107.7 21.7 %collective-permute-start.17 = (f32[128,8,128]{2,1,0:T(8,128)S(1)}, f32[128,8,128]{2,1,0:T(8,128)S(1)}, u32[]{:S(2)}, u32[]{:S(2)}) collective-permute-start(f32[128,8,128]{2,1,0:T(8,128)S(1)} %get-tuple-element.43), channel_id=1, source_target_pairs={{0,8},{8,0},{16,24},{24,16},{32,40},{40,32},{48,56},{56,48},{1,9},... | collective-permute-start | bytes 1572872 | tf_op jit(solution)/shard_map/ppermute | solution.py:228
  108.4 21.0 %collective-permute-start.18 = (f32[128,8,128]{2,1,0:T(8,128)S(1)}, f32[128,8,128]{2,1,0:T(8,128)S(1)}, u32[]{:S(2)}, u32[]{:S(2)}) collective-permute-start(f32[128,8,128]{2,1,0:T(8,128)S(1)} %get-tuple-element.44), channel_id=1, source_target_pairs={{8,16},{16,8},{24,32},{32,24},{40,48},{48,40},{9,17},{17,9},{25,33... | collective-permute-start | bytes 1572872 | tf_op jit(solution)/shard_map/ppermute | solution.py:228
  110.3 22.0 %collective-permute-start.16 = (f32[128,8,128]{2,1,0:T(8,128)S(1)}, f32[128,8,128]{2,1,0:T(8,128)S(1)}, u32[]{:S(2)}, u32[]{:S(2)}) collective-permute-start(f32[128,8,128]{2,1,0:T(8,128)S(1)} %shard_map.66.order), channel_id=1, source_target_pairs={{1,2},{2,1},{3,4},{4,3},{5,6},{6,5},{9,10},{10,9},{11,12},{12,11},... | collective-permute-start | bytes 1572872 | tf_op jit(solution)/shard_map/ppermute | solution.py:228
  114.5 14.9 %collective-permute-start.19 = (f32[8,8,128]{2,1,0:T(8,128)S(1)}, f32[8,8,128]{2,1,0:T(8,128)S(1)}, u32[]{:S(2)}, u32[]{:S(2)}) collective-permute-start(f32[8,8,128]{2,1,0:T(8,128)S(1)} %get-tuple-element.45), channel_id=1, source_target_pairs={{0,64},{64,0},{1,65},{65,1},{2,66},{66,2},{3,67},{67,3},{4,68},{68... | collective-permute-start | bytes 98312 | tf_op jit(solution)/shard_map/ppermute | solution.py:228
  131.8 27.3 %collective-permute-start.20 = (f32[128,8,128]{2,1,0:T(8,128)S(1)}, f32[128,8,128]{2,1,0:T(8,128)S(1)}, u32[]{:S(2)}, u32[]{:S(2)}) collective-permute-start(f32[128,8,128]{2,1,0:T(8,128)S(1)} %shard_map.71), channel_id=1, source_target_pairs={{0,1},{1,0},{2,3},{3,2},{4,5},{5,4},{6,7},{7,6},{8,9},{9,8},{10,11... | collective-permute-start | bytes 1572872 | tf_op jit(solution)/shard_map/ppermute | solution.py:228
  139.4 19.7 %collective-permute-start.22 = (f32[128,8,128]{2,1,0:T(8,128)S(1)}, f32[128,8,128]{2,1,0:T(8,128)S(1)}, u32[]{:S(2)}, u32[]{:S(2)}) collective-permute-start(f32[128,8,128]{2,1,0:T(8,128)S(1)} %get-tuple-element.47), channel_id=1, source_target_pairs={{0,8},{8,0},{16,24},{24,16},{32,40},{40,32},{48,56},{56,48},{1,9},... | collective-permute-start | bytes 1572872 | tf_op jit(solution)/shard_map/ppermute | solution.py:228
  139.8 19.3 %collective-permute-start.23 = (f32[128,8,128]{2,1,0:T(8,128)S(1)}, f32[128,8,128]{2,1,0:T(8,128)S(1)}, u32[]{:S(2)}, u32[]{:S(2)}) collective-permute-start(f32[128,8,128]{2,1,0:T(8,128)S(1)} %get-tuple-element.48), channel_id=1, source_target_pairs={{8,16},{16,8},{24,32},{32,24},{40,48},{48,40},{9,17},{17,9},{25,33... | collective-permute-start | bytes 1572872 | tf_op jit(solution)/shard_map/ppermute | solution.py:228
  141.7 20.5 %collective-permute-start.21 = (f32[128,8,128]{2,1,0:T(8,128)S(1)}, f32[128,8,128]{2,1,0:T(8,128)S(1)}, u32[]{:S(2)}, u32[]{:S(2)}) collective-permute-start(f32[128,8,128]{2,1,0:T(8,128)S(1)} %shard_map.69.order), channel_id=1, source_target_pairs={{1,2},{2,1},{3,4},{4,3},{5,6},{6,5},{9,10},{10,9},{11,12},{12,11},... | collective-permute-start | bytes 1572872 | tf_op jit(solution)/shard_map/ppermute | solution.py:228
  145.9 13.2 %collective-permute-start.24 = (f32[8,8,128]{2,1,0:T(8,128)S(1)}, f32[8,8,128]{2,1,0:T(8,128)S(1)}, u32[]{:S(2)}, u32[]{:S(2)}) collective-permute-start(f32[8,8,128]{2,1,0:T(8,128)S(1)} %get-tuple-element.49), channel_id=1, source_target_pairs={{0,64},{64,0},{1,65},{65,1},{2,66},{66,2},{3,67},{67,3},{4,68},{68... | collective-permute-start | bytes 98312 | tf_op jit(solution)/shard_map/ppermute | solution.py:228
  161.5 29.2 %collective-permute-start.25 = (f32[128,8,128]{2,1,0:T(8,128)S(1)}, f32[128,8,128]{2,1,0:T(8,128)S(1)}, u32[]{:S(2)}, u32[]{:S(2)}) collective-permute-start(f32[128,8,128]{2,1,0:T(8,128)S(1)} %shard_map.74), channel_id=1, source_target_pairs={{0,1},{1,0},{2,3},{3,2},{4,5},{5,4},{6,7},{7,6},{8,9},{9,8},{10,11... | collective-permute-start | bytes 1572872 | tf_op jit(solution)/shard_map/ppermute | solution.py:228
  164.6 26.2 %copy-start.2 = (f32[128,8,8,128]{3,2,1,0:T(8,128)S(1)}, f32[128,8,8,128]{3,2,1,0:T(8,128)}, u32[]{:S(2)}) copy-start(f32[128,8,8,128]{3,2,1,0:T(8,128)} %fi.11) | copy-start | bytes 12582916
  164.6 26.2 %copy-start.4 = (f32[128,8,8,128]{3,2,1,0:T(8,128)S(1)}, f32[128,8,8,128]{3,2,1,0:T(8,128)}, u32[]{:S(2)}) copy-start(f32[128,8,8,128]{3,2,1,0:T(8,128)} %fk.11) | copy-start | bytes 12582916
  164.6 26.2 %collective-permute-start.26 = (f32[128,8,128]{2,1,0:T(8,128)S(1)}, f32[128,8,128]{2,1,0:T(8,128)S(1)}, u32[]{:S(2)}, u32[]{:S(2)}) collective-permute-start(f32[128,8,128]{2,1,0:T(8,128)S(1)} %shard_map.72.order), channel_id=1, source_target_pairs={{1,2},{2,1},{3,4},{4,3},{5,6},{6,5},{9,10},{10,9},{11,12},{12,11},... | collective-permute-start | bytes 1572872 | tf_op jit(solution)/shard_map/ppermute | solution.py:228
  174.0 16.8 %collective-permute-start.27 = (f32[128,8,128]{2,1,0:T(8,128)S(1)}, f32[128,8,128]{2,1,0:T(8,128)S(1)}, u32[]{:S(2)}, u32[]{:S(2)}) collective-permute-start(f32[128,8,128]{2,1,0:T(8,128)S(1)} %get-tuple-element.51), channel_id=1, source_target_pairs={{0,8},{8,0},{16,24},{24,16},{32,40},{40,32},{48,56},{56,48},{1,9},... | collective-permute-start | bytes 1572872 | tf_op jit(solution)/shard_map/ppermute | solution.py:228
  174.0 16.7 %collective-permute-start.28 = (f32[128,8,128]{2,1,0:T(8,128)S(1)}, f32[128,8,128]{2,1,0:T(8,128)S(1)}, u32[]{:S(2)}, u32[]{:S(2)}) collective-permute-start(f32[128,8,128]{2,1,0:T(8,128)S(1)} %get-tuple-element.52), channel_id=1, source_target_pairs={{8,16},{16,8},{24,32},{32,24},{40,48},{48,40},{9,17},{17,9},{25,33... | collective-permute-start | bytes 1572872 | tf_op jit(solution)/shard_map/ppermute | solution.py:228
  176.0 14.8 %collective-permute-start.29 = (f32[8,8,128]{2,1,0:T(8,128)S(1)}, f32[8,8,128]{2,1,0:T(8,128)S(1)}, u32[]{:S(2)}, u32[]{:S(2)}) collective-permute-start(f32[8,8,128]{2,1,0:T(8,128)S(1)} %get-tuple-element.53), channel_id=1, source_target_pairs={{0,64},{64,0},{1,65},{65,1},{2,66},{66,2},{3,67},{67,3},{4,68},{68... | collective-permute-start | bytes 98312 | tf_op jit(solution)/shard_map/ppermute | solution.py:228
  198.7 5.8 %collective-permute-start.30 = (f32[2,8,8,128]{3,2,1,0:T(8,128)S(1)}, f32[2,8,8,128]{3,2,1,0:T(8,128)S(1)}, u32[]{:S(2)}, u32[]{:S(2)}) collective-permute-start(f32[2,8,8,128]{3,2,1,0:T(8,128)S(1)} %get-tuple-element.55.mine), channel_id=1, source_target_pairs={{0,64},{64,0},{1,65},{65,1},{2,66},{66,2},{3,67},{67,3},{4,68},{68... | collective-permute-start | bytes 196616 | tf_op jit(solution)/shard_map/ppermute | solution.py:228
  204.4 2.2 %copy-start.6 = (f32[128,8,8,128]{3,2,1,0:T(8,128)S(1)}, f32[128,8,8,128]{3,2,1,0:T(8,128)}, u32[]{:S(2)}) copy-start(f32[128,8,8,128]{3,2,1,0:T(8,128)} %get-tuple-element.28.f) | copy-start | bytes 12582916

commit v2 on v1

--- a/solution.py
+++ b/solution.py
@@ -11,6 +11,8 @@
 F32 = jnp.float32
 VMEM = pltpu.VMEM
 SMEM = pltpu.SMEM
+HBM = pltpu.HBM
+ROWS = 8
 
 
 def swap_pairs(devices, first):
@@ -50,30 +52,84 @@
 
     beyond = s[pl.ds(k, ni, stride=nk), :]
     zero = jnp.zeros_like(beyond)
-
-    def row(j, prev, cur, nxt):
-        r1 = jnp.broadcast_to(e1[j, pl.ds(k, 1), :], (ni, nl))
-        r2 = jnp.broadcast_to(e2[j, pl.ds(k, 1), :], (ni, nl))
-        edge = jnp.where(e1_edge, r1, r2)
-        il = jnp.where(first_i, edge, pltpu.roll(cur, 1, 0))
-        iu = jnp.where(last_i, edge, pltpu.roll(cur, ni - 1, 0))
-        h = halo[j]
-        inner = at(f, j, kin)
-        out[j] = combine(
-            cur, prev, nxt, il, iu, inner, h,
-            at(fj, j, k), at(fi, j, k), sign * at(fk, j, k),
+    before = jnp.where(low_south, zero, beyond)
+    after = jnp.where(low_south, beyond, zero)
+
+    def body(t, prev):
+        j0 = t * ROWS
+        cur = [at(f, j0 + r, k) for r in range(ROWS)]
+        nxt = jnp.where(j0 + ROWS == rows, after, at(f, jnp.minimum(j0 + ROWS, rows - 1), k))
+        for r in range(ROWS):
+            j, c = j0 + r, cur[r]
+            r1 = jnp.broadcast_to(e1[j, pl.ds(k, 1), :], (ni, nl))
+            r2 = jnp.broadcast_to(e2[j, pl.ds(k, 1), :], (ni, nl))
+            edge = jnp.where(e1_edge, r1, r2)
+            il = jnp.where(first_i, edge, pltpu.roll(c, 1, 0))
+            iu = jnp.where(last_i, edge, pltpu.roll(c, ni - 1, 0))
+            out[j] = combine(
+                c, cur[r - 1] if r else prev, cur[r + 1] if r + 1 < ROWS else nxt,
+                il, iu, at(f, j, kin), halo[j],
+                at(fj, j, k), at(fi, j, k), sign * at(fk, j, k),
+            )
+        return cur[-1]
+
+    lax.fori_loop(0, rows // ROWS, body, before)
+
+
+def edge_body(flags, f, fj, fi, fk, ha, hb, e1, e2, s, order, g1, g2, gs):
+    rows, ni, nk, nl = f.shape
+    i_even = flags[1] == 0
+    low_south = flags[2] == 0
+    sub = lax.broadcasted_iota(jnp.int32, (nk, nl), 0)
+    a_edge = sub == jnp.where(flags[0] == 0, nk - 1, 0)
+    first_k = sub == 0
+    last_k = sub == nk - 1
+    zero = jnp.zeros((nk, nl), F32)
+
+    def cell(j, i, c, prev, nxt, il, iu):
+        ra = jnp.broadcast_to(ha[j, pl.ds(i, 1), :], (nk, nl))
+        rb = jnp.broadcast_to(hb[j, pl.ds(i, 1), :], (nk, nl))
+        edge = jnp.where(a_edge, ra, rb)
+        kl = jnp.where(first_k, edge, pltpu.roll(c, 1, 0))
+        ku = jnp.where(last_k, edge, pltpu.roll(c, nk - 1, 0))
+        return combine(c, prev, nxt, il, iu, kl, ku, fj[j, i], fi[j, i], fk[j, i])
+
+    def sides(j):
+        x1, x2 = e1[j], e2[j]
+        return jnp.where(i_even, x2, x1), jnp.where(i_even, x1, x2)
+
+    js = jnp.where(low_south, rows - 1, 0)
+    jin = jnp.where(low_south, rows - 2, 1)
+    below, above = sides(js)
+    row = [f[js, i] for i in range(ni)]
+    for i in range(ni):
+        inner = f[jin, i]
+        gs[i] = cell(
+            js, i, row[i], jnp.where(low_south, inner, s[i]), jnp.where(low_south, s[i], inner),
+            row[i - 1] if i else below, row[i + 1] if i + 1 < ni else above,
         )
 
-    def body(j, carry):
-        prev, cur = carry
-        nxt = at(f, j + 1, k)
-        row(j, prev, cur, nxt)
-        return cur, nxt
-
-    prev, cur = lax.fori_loop(
-        0, rows - 1, body, (jnp.where(low_south, zero, beyond), at(f, 0, k)), unroll=False
-    )
-    row(rows - 1, prev, cur, jnp.where(low_south, beyond, zero))
+    before = tuple(jnp.where(low_south, zero, s[i]) for i in (0, ni - 1))
+    after = tuple(jnp.where(low_south, s[i], zero) for i in (0, ni - 1))
+    n = ROWS // 2
+
+    def body(t, prev):
+        j0 = t * n
+        end = j0 + n == rows
+        jn = jnp.minimum(j0 + n, rows - 1)
+        cur = [(f[j0 + r, 0], f[j0 + r, ni - 1]) for r in range(n)]
+        cur.append(tuple(jnp.where(end, a, f[jn, i]) for a, i in zip(after, (0, ni - 1))))
+        cur.insert(0, prev)
+        for r in range(n):
+            j = j0 + r
+            below, above = sides(j)
+            lo = cell(j, 0, cur[r + 1][0], cur[r][0], cur[r + 2][0], below, f[j, 1])
+            hi = cell(j, ni - 1, cur[r + 1][1], cur[r][1], cur[r + 2][1], f[j, ni - 2], above)
+            g1[j] = jnp.where(i_even, hi, lo)
+            g2[j] = jnp.where(i_even, lo, hi)
+        return cur[n]
+
+    lax.fori_loop(0, rows // n, body, before)
 
 
 def update_rows(flags, f, fj, fi, fk, ha, hb, e1, e2, s, emit):
@@ -120,18 +176,14 @@
     row(rows - 1, prev, cur, tuple(jnp.where(low_south, s[i], zero) for i in range(ni)))
 
 
-def full_body(flags, f, fj, fi, fk, ha, hb, e1, e2, s, order, out, g1, g2, gs):
-    rows, ni, _, _ = f.shape
-    i_even = flags[1] == 0
+def full_body(flags, f, fj, fi, fk, ha, hb, e1, e2, s, order, out):
+    _, ni, _, _ = f.shape
 
     def emit(j, new):
         for i in range(ni):
             out[j, i] = new[i]
-        g1[j] = jnp.where(i_even, new[-1], new[0])
-        g2[j] = jnp.where(i_even, new[0], new[-1])
 
     update_rows(flags, f, fj, fi, fk, ha, hb, e1, e2, s, emit)
-    gs[...] = out[jnp.where(flags[2] == 0, rows - 1, 0)]
 
 
 def final_body(flags, f, fj, fi, fk, ha, hb, e1, e2, s, out, stats):
@@ -180,34 +232,54 @@
     lax.fori_loop(0, rows, body, 0, unroll=2)
 
 
-def edges_body(flags, f, g1, g2, ga, gb, gs):
-    rows, ni, nk, _ = f.shape
-    i_even = flags[1] == 0
-    a_last = flags[0] == 0
-
-    def body(j, _):
-        g1[j] = jnp.where(i_even, f[j, ni - 1], f[j, 0])
-        g2[j] = jnp.where(i_even, f[j, 0], f[j, ni - 1])
-        lo = f[j, :, 0, :]
-        hi = f[j, :, nk - 1, :]
-        ga[j] = jnp.where(a_last, hi, lo)
-        gb[j] = jnp.where(a_last, lo, hi)
-        return 0
-
-    lax.fori_loop(0, rows, body, 0)
-    gs[...] = f[jnp.where(flags[2] == 0, rows - 1, 0)]
-
-
-def call(body, args, outs, mib=2):
-    flagged = args[0].dtype == jnp.int32
-    specs = [pl.BlockSpec(memory_space=VMEM) for _ in args]
-    if flagged:
-        specs[0] = pl.BlockSpec(memory_space=SMEM)
+def first_a_body(flags, f, ga, sem):
+    nk = f.shape[2]
+    copy = pltpu.make_async_copy(f.at[:, :, jnp.where(flags[0] == 0, nk - 1, 0)], ga, sem)
+    copy.start()
+    copy.wait()
+
+
+def first_rest_body(flags, f, order, gb, g1, g2, gs, sems):
+    rows, ni, nk = f.shape[:3]
+    i1 = jnp.where(flags[1] == 0, ni - 1, 0)
+    copies = [
+        pltpu.make_async_copy(src, dst, sems.at[n])
+        for n, (src, dst) in enumerate(
+            [
+                (f.at[:, :, jnp.where(flags[0] == 0, 0, nk - 1)], gb),
+                (f.at[:, ni - 1 - i1], g2),
+                (f.at[:, i1], g1),
+                (f.at[jnp.where(flags[2] == 0, rows - 1, 0)], gs),
+            ]
+        )
+    ]
+    for c in copies:
+        c.start()
+    for c in copies:
+        c.wait()
+
+
+def load_body(*refs):
+    n = (len(refs) - 2) // 2
+    copies = [
+        pltpu.make_async_copy(refs[i], refs[n + 1 + i], refs[-1].at[i]) for i in range(n)
+    ]
+    for c in copies:
+        c.start()
+    for c in copies:
+        c.wait()
+
+
+def call(body, args, outs, mib=2, spaces=None, scratch=()):
+    spaces = spaces or [VMEM] * len(args)
+    if args[0].dtype == jnp.int32:
+        spaces = [SMEM, *spaces[1:]]
     return pl.pallas_call(
         body,
         out_shape=[jax.ShapeDtypeStruct(o, F32) for o in outs],
-        in_specs=specs,
+        in_specs=[pl.BlockSpec(memory_space=m) for m in spaces],
         out_specs=[pl.BlockSpec(memory_space=VMEM) for _ in outs],
+        scratch_shapes=scratch,
         compiler_params=pltpu.CompilerParams(vmem_limit_bytes=mib << 20),
     )(*args)
 
@@ -229,29 +301,39 @@
 
     flat = (rows, ni * nk, nl)
     kface, iface, jface = (rows, ni, nl), (rows, nk, nl), (ni, nk, nl)
+    sem = pltpu.SemaphoreType.DMA
+    lines = field.reshape(rows, ni, nk, 1, nl)
+    (ga,) = call(first_a_body, [flags, lines], [(rows, ni, 1, nl)], 51, [SMEM, HBM], [sem])
+    ha = swap(ga.reshape(kface), "down", 0)
+    gb, g1, g2, gs = call(
+        first_rest_body, [flags, lines, ga],
+        [(rows, ni, 1, nl), (rows, nk, 1, nl), (rows, nk, 1, nl), (ni, nk, 1, nl)],
+        51, [SMEM, HBM, VMEM], [sem((4,))],
+    )
+    hb = swap(gb.reshape(kface), "down", 1)
+    e2 = swap(g2.reshape(iface), "east", 1)
+    s = swap(gs.reshape(jface), "south", 0)
+    e1 = swap(g1.reshape(iface), "east", 0)
+    field, fj, fi, fk = call(
+        load_body, [field, fj, fi, fk, gs], [field.shape] * 4,
+        32, [HBM] * 4 + [VMEM], [sem((4,))],
+    )
+
     fjr, fir, fkr = (x.reshape(flat) for x in (fj, fi, fk))
-
-    g1, g2, ga, gb, gs = call(edges_body, [flags, field], [iface, iface, kface, kface, jface])
-    ha = swap(ga, "down", 0)
-    hb = swap(gb, "down", 1)
-    e2 = swap(g2, "east", 1)
-    e1 = swap(g1, "east", 0)
-    s = swap(gs, "south", 0)
     for _ in range(STEPS - 1):
         fr = field.reshape(flat)
         sr = s.reshape(ni * nk, nl)
         (ga,) = call(functools.partial(face_body, 0), [flags, fr, fjr, fir, fkr, ha, e1, e2, sr], [kface])
+        ha_next = swap(ga, "down", 0)
         (gb,) = call(functools.partial(face_body, 1), [flags, fr, fjr, fir, fkr, hb, e1, e2, sr], [kface])
-        ha_next = swap(ga, "down", 0)
         hb_next = swap(gb, "down", 1)
-        field, g1, g2, gs = call(
-            full_body, [flags, field, fj, fi, fk, ha, hb, e1, e2, s, gb],
-            [field.shape, iface, iface, jface],
-        )
+        halos = [flags, field, fj, fi, fk, ha, hb, e1, e2, s]
+        g1, g2, gs = call(edge_body, [*halos, gb], [iface, iface, jface])
+        e2 = swap(g2, "east", 1)
+        s = swap(gs, "south", 0)
+        e1 = swap(g1, "east", 0)
+        (field,) = call(full_body, [*halos, gs], [field.shape])
         ha, hb = ha_next, hb_next
-        e2 = swap(g2, "east", 1)
-        e1 = swap(g1, "east", 0)
-        s = swap(gs, "south", 0)
     field, stats = call(
         final_body, [flags, field, fj, fi, fk, ha, hb, e1, e2, s],
         [field.shape, (2, ni, nk, nl)], 12,

time: 210 us -> 187 us (0.89)
  the two profiles are of different devices: /device:TPU:46 before, /device:TPU:96 now
where the time goes in v2:
time: 187 us; the launch traced here: 184 us
  waiting for transfers between devices  69.5 us (37%)
  Pallas kernels  65.4 us (35%)
  starting transfers between devices  46.3 us (25%)
  local copies, waits for them, and re-layouts  2.19 us (1%)
    ppermute x31, waiting for transfers between devices, swap(): return lax.ppermute(x, axis, swap_pairs(lax.axis_size(axis), first))  69.5 us
    pallas_call x25, Pallas kernels, call(): pl.pallas_call(body, out_shape=[jax.ShapeDtypeStruct(o, F32) for o in out...  65.4 us
    ppermute x31, starting transfers between devices, swap(): return lax.ppermute(x, axis, swap_pairs(lax.axis_size(axis), first))  46.3 us
  transfers between devices with their start and end apart: 31, of which 9 were waited for; matrix products, arithmetic and copies ran while one was open for 0% of the time, Pallas kernels for 29%

profile of v2, /device:TPU:96, one launch (start us, length us, event | category | flops | bytes accessed | tf_op | source)
XLA Modules:
  0.0 184.4 jit_solution(3877150896703699532)
XLA Ops:
  0.7 1.9 %shard_map.59.order = f32[128,8,1,128]{3,2,1,0:T(1,128)S(1)} custom-call(s32[3]{0:T(128)S(1)} %pad_add_fusion.flags, f32[128,8,8,1,128]{4,3,2,1,0:T(1,128)} %bitcast.62), custom_call_target="tpu_custom_call" | custom-call | tf_op jit(solution)/shard_map/pallas_call | solution.py:277
  2.6 1.6 collective-permute-start
  4.2 1.9 %shard_map.60 = (f32[128,8,1,128]{3,2,1,0:T(1,128)S(1)}, f32[128,8,1,128]{3,2,1,0:T(1,128)S(1)}, f32[128,8,1,128]{3,2,1,0:T(1,128)S(1)}, f32[8,8,1,128]{3,2,1,0:T(1,128)S(1)}) custom-call(s32[3]{0:T(128)S(1)} %pad_add_fusion.flags, f32[128,8,8,1,128]{4,3,2,1,0:T(1,128)} %bitcast.63, f32[128,8,1,128]{3,2,1,0:T(1,128)S(1)} %shard_map.59.order), custom_call_target="tpu_custom_call" | custom-call | tf_op jit(solution)/shard_map/pallas_call | solution.py:277
  6.2 0.7 collective-permute-start.3
  6.9 2.3 %collective-permute-start.1 = (f32[128,8,128]{2,1,0:T(8,128)S(1)}, f32[128,8,128]{2,1,0:T(8,128)S(1)}, u32[]{:S(2)}, u32[]{:S(2)}) collective-permute-start(f32[128,8,128]{2,1,0:T(8,128)S(1)} %bitcast.76), channel_id=1, source_target_pairs={{1,2},{2,1},{3,4},{4,3},{5,6},{6,5},{9,10},{10,9},{11,12},{12,11},... | collective-permute-start | bytes 1572872 | tf_op jit(solution)/shard_map/ppermute | solution.py:300
  9.2 3.1 %collective-permute-start.4 = (f32[8,8,128]{2,1,0:T(8,128)S(1)}, f32[8,8,128]{2,1,0:T(8,128)S(1)}, u32[]{:S(2)}, u32[]{:S(2)}) collective-permute-start(f32[8,8,128]{2,1,0:T(8,128)S(1)} %bitcast.75), channel_id=1, source_target_pairs={{0,64},{64,0},{1,65},{65,1},{2,66},{66,2},{3,67},{67,3},{4,68},{68... | collective-permute-start | bytes 98312 | tf_op jit(solution)/shard_map/ppermute | solution.py:300
  12.4 5.0 %shard_map.61 = (f32[128,8,8,128]{3,2,1,0:T(8,128)S(1)}, f32[128,8,8,128]{3,2,1,0:T(8,128)S(1)}, f32[128,8,8,128]{3,2,1,0:T(8,128)S(1)}, f32[128,8,8,128]{3,2,1,0:T(8,128)S(1)}) custom-call(f32[128,8,8,128]{3,2,1,0:T(8,128)S(1)} %copy-done, f32[128,8,8,128]{3,2,1,0:T(8,128)} %refs_1_.1, f32[128,8,8,128]{3,2,1,0:T(8,128)} %refs_2_.1, ...), custom_call_target="tpu_custom_call" | custom-call | tf_op jit(solution)/shard_map/pallas_call | solution.py:277
  17.3 13.1 %collective-permute-done.4.s = f32[8,8,128]{2,1,0:T(8,128)S(1)} collective-permute-done((f32[8,8,128]{2,1,0:T(8,128)S(1)}, f32[8,8,128]{2,1,0:T(8,128)S(1)}, u32[]{:S(2)}, u32[]{:S(2)}) %collective-permute-start.4) | collective-permute-done | bytes 32800 | tf_op jit(solution)/shard_map/ppermute | solution.py:300
  30.5 1.5 shard_map.65
  32.1 1.5 shard_map.62.order
  33.6 1.7 shard_map.63
  36.0 3.8 %collective-permute-start.6 = (f32[128,8,128]{2,1,0:T(8,128)S(1)}, f32[128,8,128]{2,1,0:T(8,128)S(1)}, u32[]{:S(2)}, u32[]{:S(2)}) collective-permute-start(f32[128,8,128]{2,1,0:T(8,128)S(1)} %shard_map.62.order), channel_id=1, source_target_pairs={{1,2},{2,1},{3,4},{4,3},{5,6},{6,5},{9,10},{10,9},{11,12},{12,11},... | collective-permute-start | bytes 1572872 | tf_op jit(solution)/shard_map/ppermute | solution.py:300
  39.8 0.9 collective-permute-start.9
  40.7 4.6 %shard_map.64.f = f32[128,8,8,128]{3,2,1,0:T(8,128)S(1)} custom-call(s32[3]{0:T(128)S(1)} %pad_add_fusion.flags, f32[128,8,8,128]{3,2,1,0:T(8,128)S(1)} %get-tuple-element.28.f, f32[128,8,8,128]{3,2,1,0:T(8,128)S(1)} %get-tuple-element.29.fj, f32[128,8,8,128]{3,2,1,0:T(8,128)S(1)} %get-tuple-element.30.fi, f32[128,8,8,128]{3,2,1,0:T(8,128)S(1)} %get-tuple-element.31.fk, ...), custom_call_target="tpu_custom_call" | custom-call | tf_op jit(solution)/shard_map/pallas_call | solution.py:277
  45.3 10.5 %collective-permute-done.9.s = f32[8,8,128]{2,1,0:T(8,128)S(1)} collective-permute-done((f32[8,8,128]{2,1,0:T(8,128)S(1)}, f32[8,8,128]{2,1,0:T(8,128)S(1)}, u32[]{:S(2)}, u32[]{:S(2)}) %collective-permute-start.9) | collective-permute-done | bytes 32800 | tf_op jit(solution)/shard_map/ppermute | solution.py:300
  55.8 1.5 shard_map.69
  57.4 1.5 shard_map.66.order
  58.8 1.7 shard_map.67
  61.4 4.5 %collective-permute-start.11 = (f32[128,8,128]{2,1,0:T(8,128)S(1)}, f32[128,8,128]{2,1,0:T(8,128)S(1)}, u32[]{:S(2)}, u32[]{:S(2)}) collective-permute-start(f32[128,8,128]{2,1,0:T(8,128)S(1)} %shard_map.66.order), channel_id=1, source_target_pairs={{1,2},{2,1},{3,4},{4,3},{5,6},{6,5},{9,10},{10,9},{11,12},{12,11},... | collective-permute-start | bytes 1572872 | tf_op jit(solution)/shard_map/ppermute | solution.py:300
  65.9 2.1 %collective-permute-start.14 = (f32[8,8,128]{2,1,0:T(8,128)S(1)}, f32[8,8,128]{2,1,0:T(8,128)S(1)}, u32[]{:S(2)}, u32[]{:S(2)}) collective-permute-start(f32[8,8,128]{2,1,0:T(8,128)S(1)} %get-tuple-element.38.order), channel_id=1, source_target_pairs={{0,64},{64,0},{1,65},{65,1},{2,66},{66,2},{3,67},{67,3},{4,68},{68... | collective-permute-start | bytes 98312 | tf_op jit(solution)/shard_map/ppermute | solution.py:300
  68.0 4.6 %shard_map.68.f = f32[128,8,8,128]{3,2,1,0:T(8,128)S(1)} custom-call(s32[3]{0:T(128)S(1)} %pad_add_fusion.flags, f32[128,8,8,128]{3,2,1,0:T(8,128)S(1)} %shard_map.64.f, f32[128,8,8,128]{3,2,1,0:T(8,128)S(1)} %get-tuple-element.29.fj, f32[128,8,8,128]{3,2,1,0:T(8,128)S(1)} %get-tuple-element.30.fi, f32[128,8,8,128]{3,2,1,0:T(8,128)S(1)} %get-tuple-element.31.fk, ...), custom_call_target="tpu_custom_call" | custom-call | tf_op jit(solution)/shard_map/pallas_call | solution.py:277
  72.7 11.1 %collective-permute-done.14.s = f32[8,8,128]{2,1,0:T(8,128)S(1)} collective-permute-done((f32[8,8,128]{2,1,0:T(8,128)S(1)}, f32[8,8,128]{2,1,0:T(8,128)S(1)}, u32[]{:S(2)}, u32[]{:S(2)}) %collective-permute-start.14) | collective-permute-done | bytes 32800 | tf_op jit(solution)/shard_map/ppermute | solution.py:300
  83.7 1.5 shard_map.73
  85.3 1.5 shard_map.70.order
  86.8 1.7 shard_map.71
  89.2 6.0 %collective-permute-start.16 = (f32[128,8,128]{2,1,0:T(8,128)S(1)}, f32[128,8,128]{2,1,0:T(8,128)S(1)}, u32[]{:S(2)}, u32[]{:S(2)}) collective-permute-start(f32[128,8,128]{2,1,0:T(8,128)S(1)} %shard_map.70.order), channel_id=1, source_target_pairs={{1,2},{2,1},{3,4},{4,3},{5,6},{6,5},{9,10},{10,9},{11,12},{12,11},... | collective-permute-start | bytes 1572872 | tf_op jit(solution)/shard_map/ppermute | solution.py:300
  95.3 4.6 %shard_map.72.f = f32[128,8,8,128]{3,2,1,0:T(8,128)S(1)} custom-call(s32[3]{0:T(128)S(1)} %pad_add_fusion.flags, f32[128,8,8,128]{3,2,1,0:T(8,128)S(1)} %shard_map.68.f, f32[128,8,8,128]{3,2,1,0:T(8,128)S(1)} %get-tuple-element.29.fj, f32[128,8,8,128]{3,2,1,0:T(8,128)S(1)} %get-tuple-element.30.fi, f32[128,8,8,128]{3,2,1,0:T(8,128)S(1)} %get-tuple-element.31.fk, ...), custom_call_target="tpu_custom_call" | custom-call | tf_op jit(solution)/shard_map/pallas_call | solution.py:277
  100.0 10.5 %collective-permute-done.19.s = f32[8,8,128]{2,1,0:T(8,128)S(1)} collective-permute-done((f32[8,8,128]{2,1,0:T(8,128)S(1)}, f32[8,8,128]{2,1,0:T(8,128)S(1)}, u32[]{:S(2)}, u32[]{:S(2)}) %collective-permute-start.19) | collective-permute-done | bytes 32800 | tf_op jit(solution)/shard_map/ppermute | solution.py:300
  110.5 1.5 shard_map.77
  112.1 1.5 shard_map.74.order
  113.5 1.7 shard_map.75
  116.0 4.2 %collective-permute-start.21 = (f32[128,8,128]{2,1,0:T(8,128)S(1)}, f32[128,8,128]{2,1,0:T(8,128)S(1)}, u32[]{:S(2)}, u32[]{:S(2)}) collective-permute-start(f32[128,8,128]{2,1,0:T(8,128)S(1)} %shard_map.74.order), channel_id=1, source_target_pairs={{1,2},{2,1},{3,4},{4,3},{5,6},{6,5},{9,10},{10,9},{11,12},{12,11},... | collective-permute-start | bytes 1572872 | tf_op jit(solution)/shard_map/ppermute | solution.py:300
  120.2 3.4 %collective-permute-start.24 = (f32[8,8,128]{2,1,0:T(8,128)S(1)}, f32[8,8,128]{2,1,0:T(8,128)S(1)}, u32[]{:S(2)}, u32[]{:S(2)}) collective-permute-start(f32[8,8,128]{2,1,0:T(8,128)S(1)} %get-tuple-element.44.order), channel_id=1, source_target_pairs={{0,64},{64,0},{1,65},{65,1},{2,66},{66,2},{3,67},{67,3},{4,68},{68... | collective-permute-start | bytes 98312 | tf_op jit(solution)/shard_map/ppermute | solution.py:300
  123.6 4.6 %shard_map.76.f = f32[128,8,8,128]{3,2,1,0:T(8,128)S(1)} custom-call(s32[3]{0:T(128)S(1)} %pad_add_fusion.flags, f32[128,8,8,128]{3,2,1,0:T(8,128)S(1)} %shard_map.72.f, f32[128,8,8,128]{3,2,1,0:T(8,128)S(1)} %get-tuple-element.29.fj, f32[128,8,8,128]{3,2,1,0:T(8,128)S(1)} %get-tuple-element.30.fi, f32[128,8,8,128]{3,2,1,0:T(8,128)S(1)} %get-tuple-element.31.fk, ...), custom_call_target="tpu_custom_call" | custom-call | tf_op jit(solution)/shard_map/pallas_call | solution.py:277
  128.2 7.2 %collective-permute-done.24.s = f32[8,8,128]{2,1,0:T(8,128)S(1)} collective-permute-done((f32[8,8,128]{2,1,0:T(8,128)S(1)}, f32[8,8,128]{2,1,0:T(8,128)S(1)}, u32[]{:S(2)}, u32[]{:S(2)}) %collective-permute-start.24) | collective-permute-done | bytes 32800 | tf_op jit(solution)/shard_map/ppermute | solution.py:300
  135.5 1.5 shard_map.81
  137.0 0.8 collective-permute-done.21.halo.hb
  137.9 1.5 shard_map.78.order
  139.3 7.8 %collective-permute-start.26 = (f32[128,8,128]{2,1,0:T(8,128)S(1)}, f32[128,8,128]{2,1,0:T(8,128)S(1)}, u32[]{:S(2)}, u32[]{:S(2)}) collective-permute-start(f32[128,8,128]{2,1,0:T(8,128)S(1)} %shard_map.78.order), channel_id=1, source_target_pairs={{1,2},{2,1},{3,4},{4,3},{5,6},{6,5},{9,10},{10,9},{11,12},{12,11},... | collective-permute-start | bytes 1572872 | tf_op jit(solution)/shard_map/ppermute | solution.py:300
  147.1 1.7 shard_map.79
  149.8 4.6 %shard_map.80.f = f32[128,8,8,128]{3,2,1,0:T(8,128)S(1)} custom-call(s32[3]{0:T(128)S(1)} %pad_add_fusion.flags, f32[128,8,8,128]{3,2,1,0:T(8,128)S(1)} %shard_map.76.f, f32[128,8,8,128]{3,2,1,0:T(8,128)S(1)} %get-tuple-element.29.fj, f32[128,8,8,128]{3,2,1,0:T(8,128)S(1)} %get-tuple-element.30.fi, f32[128,8,8,128]{3,2,1,0:T(8,128)S(1)} %get-tuple-element.31.fk, ...), custom_call_target="tpu_custom_call" | custom-call | tf_op jit(solution)/shard_map/pallas_call | solution.py:277
  154.5 10.4 %collective-permute-done.29.s = f32[8,8,128]{2,1,0:T(8,128)S(1)} collective-permute-done((f32[8,8,128]{2,1,0:T(8,128)S(1)}, f32[8,8,128]{2,1,0:T(8,128)S(1)}, u32[]{:S(2)}, u32[]{:S(2)}) %collective-permute-start.29) | collective-permute-done | bytes 32800 | tf_op jit(solution)/shard_map/ppermute | solution.py:300
  164.9 1.1 collective-permute-done.26.hb
  166.0 7.8 %shard_map.82 = (f32[128,8,8,128]{3,2,1,0:T(8,128)}, f32[2,8,8,128]{3,2,1,0:T(8,128)S(1)}) custom-call(s32[3]{0:T(128)S(1)} %pad_add_fusion.flags, f32[128,8,8,128]{3,2,1,0:T(8,128)S(1)} %shard_map.80.f, f32[128,8,8,128]{3,2,1,0:T(8,128)S(1)} %get-tuple-element.29.fj, f32[128,8,8,128]{3,2,1,0:T(8,128)S(1)} %get-tuple-element.30.fi, ...), custom_call_target="tpu_custom_call" | custom-call | tf_op jit(solution)/shard_map/pallas_call | solution.py:277
  173.8 1.1 collective-permute-start.30
  174.9 4.7 %collective-permute-done.30.other = f32[2,8,8,128]{3,2,1,0:T(8,128)S(1)} collective-permute-done((f32[2,8,8,128]{3,2,1,0:T(8,128)S(1)}, f32[2,8,8,128]{3,2,1,0:T(8,128)S(1)}, u32[]{:S(2)}, u32[]{:S(2)}) %collective-permute-start.30) | collective-permute-done | bytes 65568 | tf_op jit(solution)/shard_map/ppermute | solution.py:300
  179.6 2.2 %copy-done.1 = f32[128,8,8,128]{3,2,1,0:T(8,128)S(1)} copy-done((f32[128,8,8,128]{3,2,1,0:T(8,128)S(1)}, f32[128,8,8,128]{3,2,1,0:T(8,128)}, u32[]{:S(2)}) %copy-start.1) | copy-done | bytes 4194328
  181.8 2.6 %shard_map.83 = f32[128,8,8,128]{3,2,1,0:T(8,128)} custom-call(f32[128,8,8,128]{3,2,1,0:T(8,128)S(1)} %copy-done.1, f32[2,8,8,128]{3,2,1,0:T(8,128)S(1)} %get-tuple-element.51.mine, f32[2,8,8,128]{3,2,1,0:T(8,128)S(1)} %collective-permute-done.30.other), custom_call_target="tpu_custom_call" | custom-call | tf_op jit(solution)/shard_map/pallas_call | solution.py:277
  (44 shorter events, 5.0 us)
Async XLA Ops:
  0.7 11.6 %copy-start = (f32[128,8,8,128]{3,2,1,0:T(8,128)S(1)}, f32[128,8,8,128]{3,2,1,0:T(8,128)}, u32[]{:S(2)}) copy-start(f32[128,8,8,128]{3,2,1,0:T(8,128)} %refs_0_.1) | copy-start | bytes 12582916
  2.6 27.9 %collective-permute-start = (f32[128,8,128]{2,1,0:T(8,128)S(1)}, f32[128,8,128]{2,1,0:T(8,128)S(1)}, u32[]{:S(2)}, u32[]{:S(2)}) collective-permute-start(f32[128,8,128]{2,1,0:T(8,128)S(1)} %bitcast.64), channel_id=1, source_target_pairs={{0,1},{1,0},{2,3},{3,2},{4,5},{5,4},{6,7},{7,6},{8,9},{9,8},{10,11... | collective-permute-start | bytes 1572872 | tf_op jit(solution)/shard_map/ppermute | solution.py:300
  6.1 24.4 %collective-permute-start.2 = (f32[128,8,128]{2,1,0:T(8,128)S(1)}, f32[128,8,128]{2,1,0:T(8,128)S(1)}, u32[]{:S(2)}, u32[]{:S(2)}) collective-permute-start(f32[128,8,128]{2,1,0:T(8,128)S(1)} %bitcast.78), channel_id=1, source_target_pairs={{0,8},{8,0},{16,24},{24,16},{32,40},{40,32},{48,56},{56,48},{1,9},... | collective-permute-start | bytes 1572872 | tf_op jit(solution)/shard_map/ppermute | solution.py:300
  6.2 24.3 %collective-permute-start.3 = (f32[128,8,128]{2,1,0:T(8,128)S(1)}, f32[128,8,128]{2,1,0:T(8,128)S(1)}, u32[]{:S(2)}, u32[]{:S(2)}) collective-permute-start(f32[128,8,128]{2,1,0:T(8,128)S(1)} %bitcast.77), channel_id=1, source_target_pairs={{8,16},{16,8},{24,32},{32,24},{40,48},{48,40},{9,17},{17,9},{25,33... | collective-permute-start | bytes 1572872 | tf_op jit(solution)/shard_map/ppermute | solution.py:300
  6.9 25.2 %collective-permute-start.1 = (f32[128,8,128]{2,1,0:T(8,128)S(1)}, f32[128,8,128]{2,1,0:T(8,128)S(1)}, u32[]{:S(2)}, u32[]{:S(2)}) collective-permute-start(f32[128,8,128]{2,1,0:T(8,128)S(1)} %bitcast.76), channel_id=1, source_target_pairs={{1,2},{2,1},{3,4},{4,3},{5,6},{6,5},{9,10},{10,9},{11,12},{12,11},... | collective-permute-start | bytes 1572872 | tf_op jit(solution)/shard_map/ppermute | solution.py:300
  9.2 21.2 %collective-permute-start.4 = (f32[8,8,128]{2,1,0:T(8,128)S(1)}, f32[8,8,128]{2,1,0:T(8,128)S(1)}, u32[]{:S(2)}, u32[]{:S(2)}) collective-permute-start(f32[8,8,128]{2,1,0:T(8,128)S(1)} %bitcast.75), channel_id=1, source_target_pairs={{0,64},{64,0},{1,65},{65,1},{2,66},{66,2},{3,67},{67,3},{4,68},{68... | collective-permute-start | bytes 98312 | tf_op jit(solution)/shard_map/ppermute | solution.py:300
  32.0 23.8 %collective-permute-start.5 = (f32[128,8,128]{2,1,0:T(8,128)S(1)}, f32[128,8,128]{2,1,0:T(8,128)S(1)}, u32[]{:S(2)}, u32[]{:S(2)}) collective-permute-start(f32[128,8,128]{2,1,0:T(8,128)S(1)} %shard_map.65), channel_id=1, source_target_pairs={{0,1},{1,0},{2,3},{3,2},{4,5},{5,4},{6,7},{7,6},{8,9},{9,8},{10,11... | collective-permute-start | bytes 1572872 | tf_op jit(solution)/shard_map/ppermute | solution.py:300
  35.2 20.6 %collective-permute-start.7 = (f32[128,8,128]{2,1,0:T(8,128)S(1)}, f32[128,8,128]{2,1,0:T(8,128)S(1)}, u32[]{:S(2)}, u32[]{:S(2)}) collective-permute-start(f32[128,8,128]{2,1,0:T(8,128)S(1)} %get-tuple-element.36), channel_id=1, source_target_pairs={{0,8},{8,0},{16,24},{24,16},{32,40},{40,32},{48,56},{56,48},{1,9},... | collective-permute-start | bytes 1572872 | tf_op jit(solution)/shard_map/ppermute | solution.py:300
  35.3 20.5 %collective-permute-start.8 = (f32[128,8,128]{2,1,0:T(8,128)S(1)}, f32[128,8,128]{2,1,0:T(8,128)S(1)}, u32[]{:S(2)}, u32[]{:S(2)}) collective-permute-start(f32[128,8,128]{2,1,0:T(8,128)S(1)} %get-tuple-element.37), channel_id=1, source_target_pairs={{8,16},{16,8},{24,32},{32,24},{40,48},{48,40},{9,17},{17,9},{25,33... | collective-permute-start | bytes 1572872 | tf_op jit(solution)/shard_map/ppermute | solution.py:300
  36.0 21.3 %collective-permute-start.6 = (f32[128,8,128]{2,1,0:T(8,128)S(1)}, f32[128,8,128]{2,1,0:T(8,128)S(1)}, u32[]{:S(2)}, u32[]{:S(2)}) collective-permute-start(f32[128,8,128]{2,1,0:T(8,128)S(1)} %shard_map.62.order), channel_id=1, source_target_pairs={{1,2},{2,1},{3,4},{4,3},{5,6},{6,5},{9,10},{10,9},{11,12},{12,11},... | collective-permute-start | bytes 1572872 | tf_op jit(solution)/shard_map/ppermute | solution.py:300
  39.8 16.0 %collective-permute-start.9 = (f32[8,8,128]{2,1,0:T(8,128)S(1)}, f32[8,8,128]{2,1,0:T(8,128)S(1)}, u32[]{:S(2)}, u32[]{:S(2)}) collective-permute-start(f32[8,8,128]{2,1,0:T(8,128)S(1)} %get-tuple-element.35.order), channel_id=1, source_target_pairs={{0,64},{64,0},{1,65},{65,1},{2,66},{66,2},{3,67},{67,3},{4,68},{68... | collective-permute-start | bytes 98312 | tf_op jit(solution)/shard_map/ppermute | solution.py:300
  57.3 26.5 %collective-permute-start.10 = (f32[128,8,128]{2,1,0:T(8,128)S(1)}, f32[128,8,128]{2,1,0:T(8,128)S(1)}, u32[]{:S(2)}, u32[]{:S(2)}) collective-permute-start(f32[128,8,128]{2,1,0:T(8,128)S(1)} %shard_map.69), channel_id=1, source_target_pairs={{0,1},{1,0},{2,3},{3,2},{4,5},{5,4},{6,7},{7,6},{8,9},{9,8},{10,11... | collective-permute-start | bytes 1572872 | tf_op jit(solution)/shard_map/ppermute | solution.py:300
  60.5 23.2 %collective-permute-start.12 = (f32[128,8,128]{2,1,0:T(8,128)S(1)}, f32[128,8,128]{2,1,0:T(8,128)S(1)}, u32[]{:S(2)}, u32[]{:S(2)}) collective-permute-start(f32[128,8,128]{2,1,0:T(8,128)S(1)} %get-tuple-element.39), channel_id=1, source_target_pairs={{0,8},{8,0},{16,24},{24,16},{32,40},{40,32},{48,56},{56,48},{1,9},... | collective-permute-start | bytes 1572872 | tf_op jit(solution)/shard_map/ppermute | solution.py:300
  60.7 23.0 %collective-permute-start.13 = (f32[128,8,128]{2,1,0:T(8,128)S(1)}, f32[128,8,128]{2,1,0:T(8,128)S(1)}, u32[]{:S(2)}, u32[]{:S(2)}) collective-permute-start(f32[128,8,128]{2,1,0:T(8,128)S(1)} %get-tuple-element.40), channel_id=1, source_target_pairs={{8,16},{16,8},{24,32},{32,24},{40,48},{48,40},{9,17},{17,9},{25,33... | collective-permute-start | bytes 1572872 | tf_op jit(solution)/shard_map/ppermute | solution.py:300
  61.4 23.9 %collective-permute-start.11 = (f32[128,8,128]{2,1,0:T(8,128)S(1)}, f32[128,8,128]{2,1,0:T(8,128)S(1)}, u32[]{:S(2)}, u32[]{:S(2)}) collective-permute-start(f32[128,8,128]{2,1,0:T(8,128)S(1)} %shard_map.66.order), channel_id=1, source_target_pairs={{1,2},{2,1},{3,4},{4,3},{5,6},{6,5},{9,10},{10,9},{11,12},{12,11},... | collective-permute-start | bytes 1572872 | tf_op jit(solution)/shard_map/ppermute | solution.py:300
  65.9 17.8 %collective-permute-start.14 = (f32[8,8,128]{2,1,0:T(8,128)S(1)}, f32[8,8,128]{2,1,0:T(8,128)S(1)}, u32[]{:S(2)}, u32[]{:S(2)}) collective-permute-start(f32[8,8,128]{2,1,0:T(8,128)S(1)} %get-tuple-element.38.order), channel_id=1, source_target_pairs={{0,64},{64,0},{1,65},{65,1},{2,66},{66,2},{3,67},{67,3},{4,68},{68... | collective-permute-start | bytes 98312 | tf_op jit(solution)/shard_map/ppermute | solution.py:300
  85.2 25.3 %collective-permute-start.15 = (f32[128,8,128]{2,1,0:T(8,128)S(1)}, f32[128,8,128]{2,1,0:T(8,128)S(1)}, u32[]{:S(2)}, u32[]{:S(2)}) collective-permute-start(f32[128,8,128]{2,1,0:T(8,128)S(1)} %shard_map.73), channel_id=1, source_target_pairs={{0,1},{1,0},{2,3},{3,2},{4,5},{5,4},{6,7},{7,6},{8,9},{9,8},{10,11... | collective-permute-start | bytes 1572872 | tf_op jit(solution)/shard_map/ppermute | solution.py:300
  88.5 22.1 %collective-permute-start.17 = (f32[128,8,128]{2,1,0:T(8,128)S(1)}, f32[128,8,128]{2,1,0:T(8,128)S(1)}, u32[]{:S(2)}, u32[]{:S(2)}) collective-permute-start(f32[128,8,128]{2,1,0:T(8,128)S(1)} %get-tuple-element.42), channel_id=1, source_target_pairs={{0,8},{8,0},{16,24},{24,16},{32,40},{40,32},{48,56},{56,48},{1,9},... | collective-permute-start | bytes 1572872 | tf_op jit(solution)/shard_map/ppermute | solution.py:300
  88.5 22.0 %collective-permute-start.18 = (f32[128,8,128]{2,1,0:T(8,128)S(1)}, f32[128,8,128]{2,1,0:T(8,128)S(1)}, u32[]{:S(2)}, u32[]{:S(2)}) collective-permute-start(f32[128,8,128]{2,1,0:T(8,128)S(1)} %get-tuple-element.43), channel_id=1, source_target_pairs={{8,16},{16,8},{24,32},{32,24},{40,48},{48,40},{9,17},{17,9},{25,33... | collective-permute-start | bytes 1572872 | tf_op jit(solution)/shard_map/ppermute | solution.py:300
  89.2 22.8 %collective-permute-start.16 = (f32[128,8,128]{2,1,0:T(8,128)S(1)}, f32[128,8,128]{2,1,0:T(8,128)S(1)}, u32[]{:S(2)}, u32[]{:S(2)}) collective-permute-start(f32[128,8,128]{2,1,0:T(8,128)S(1)} %shard_map.70.order), channel_id=1, source_target_pairs={{1,2},{2,1},{3,4},{4,3},{5,6},{6,5},{9,10},{10,9},{11,12},{12,11},... | collective-permute-start | bytes 1572872 | tf_op jit(solution)/shard_map/ppermute | solution.py:300
  95.2 15.3 %collective-permute-start.19 = (f32[8,8,128]{2,1,0:T(8,128)S(1)}, f32[8,8,128]{2,1,0:T(8,128)S(1)}, u32[]{:S(2)}, u32[]{:S(2)}) collective-permute-start(f32[8,8,128]{2,1,0:T(8,128)S(1)} %get-tuple-element.41.order), channel_id=1, source_target_pairs={{0,64},{64,0},{1,65},{65,1},{2,66},{66,2},{3,67},{67,3},{4,68},{68... | collective-permute-start | bytes 98312 | tf_op jit(solution)/shard_map/ppermute | solution.py:300
  112.0 23.5 %collective-permute-start.20 = (f32[128,8,128]{2,1,0:T(8,128)S(1)}, f32[128,8,128]{2,1,0:T(8,128)S(1)}, u32[]{:S(2)}, u32[]{:S(2)}) collective-permute-start(f32[128,8,128]{2,1,0:T(8,128)S(1)} %shard_map.77), channel_id=1, source_target_pairs={{0,1},{1,0},{2,3},{3,2},{4,5},{5,4},{6,7},{7,6},{8,9},{9,8},{10,11... | collective-permute-start | bytes 1572872 | tf_op jit(solution)/shard_map/ppermute | solution.py:300
  115.2 20.3 %collective-permute-start.22 = (f32[128,8,128]{2,1,0:T(8,128)S(1)}, f32[128,8,128]{2,1,0:T(8,128)S(1)}, u32[]{:S(2)}, u32[]{:S(2)}) collective-permute-start(f32[128,8,128]{2,1,0:T(8,128)S(1)} %get-tuple-element.45), channel_id=1, source_target_pairs={{0,8},{8,0},{16,24},{24,16},{32,40},{40,32},{48,56},{56,48},{1,9},... | collective-permute-start | bytes 1572872 | tf_op jit(solution)/shard_map/ppermute | solution.py:300
  115.3 20.2 %collective-permute-start.23 = (f32[128,8,128]{2,1,0:T(8,128)S(1)}, f32[128,8,128]{2,1,0:T(8,128)S(1)}, u32[]{:S(2)}, u32[]{:S(2)}) collective-permute-start(f32[128,8,128]{2,1,0:T(8,128)S(1)} %get-tuple-element.46), channel_id=1, source_target_pairs={{8,16},{16,8},{24,32},{32,24},{40,48},{48,40},{9,17},{17,9},{25,33... | collective-permute-start | bytes 1572872 | tf_op jit(solution)/shard_map/ppermute | solution.py:300
  116.0 21.8 %collective-permute-start.21 = (f32[128,8,128]{2,1,0:T(8,128)S(1)}, f32[128,8,128]{2,1,0:T(8,128)S(1)}, u32[]{:S(2)}, u32[]{:S(2)}) collective-permute-start(f32[128,8,128]{2,1,0:T(8,128)S(1)} %shard_map.74.order), channel_id=1, source_target_pairs={{1,2},{2,1},{3,4},{4,3},{5,6},{6,5},{9,10},{10,9},{11,12},{12,11},... | collective-permute-start | bytes 1572872 | tf_op jit(solution)/shard_map/ppermute | solution.py:300
  120.2 15.3 %collective-permute-start.24 = (f32[8,8,128]{2,1,0:T(8,128)S(1)}, f32[8,8,128]{2,1,0:T(8,128)S(1)}, u32[]{:S(2)}, u32[]{:S(2)}) collective-permute-start(f32[8,8,128]{2,1,0:T(8,128)S(1)} %get-tuple-element.44.order), channel_id=1, source_target_pairs={{0,64},{64,0},{1,65},{65,1},{2,66},{66,2},{3,67},{67,3},{4,68},{68... | collective-permute-start | bytes 98312 | tf_op jit(solution)/shard_map/ppermute | solution.py:300
  136.9 28.0 %collective-permute-start.25 = (f32[128,8,128]{2,1,0:T(8,128)S(1)}, f32[128,8,128]{2,1,0:T(8,128)S(1)}, u32[]{:S(2)}, u32[]{:S(2)}) collective-permute-start(f32[128,8,128]{2,1,0:T(8,128)S(1)} %shard_map.81), channel_id=1, source_target_pairs={{0,1},{1,0},{2,3},{3,2},{4,5},{5,4},{6,7},{7,6},{8,9},{9,8},{10,11... | collective-permute-start | bytes 1572872 | tf_op jit(solution)/shard_map/ppermute | solution.py:300
  139.3 26.7 %collective-permute-start.26 = (f32[128,8,128]{2,1,0:T(8,128)S(1)}, f32[128,8,128]{2,1,0:T(8,128)S(1)}, u32[]{:S(2)}, u32[]{:S(2)}) collective-permute-start(f32[128,8,128]{2,1,0:T(8,128)S(1)} %shard_map.78.order), channel_id=1, source_target_pairs={{1,2},{2,1},{3,4},{4,3},{5,6},{6,5},{9,10},{10,9},{11,12},{12,11},... | collective-permute-start | bytes 1572872 | tf_op jit(solution)/shard_map/ppermute | solution.py:300
  148.8 17.2 %collective-permute-start.27 = (f32[128,8,128]{2,1,0:T(8,128)S(1)}, f32[128,8,128]{2,1,0:T(8,128)S(1)}, u32[]{:S(2)}, u32[]{:S(2)}) collective-permute-start(f32[128,8,128]{2,1,0:T(8,128)S(1)} %get-tuple-element.48), channel_id=1, source_target_pairs={{0,8},{8,0},{16,24},{24,16},{32,40},{40,32},{48,56},{56,48},{1,9},... | collective-permute-start | bytes 1572872 | tf_op jit(solution)/shard_map/ppermute | solution.py:300
  148.9 17.1 %collective-permute-start.28 = (f32[128,8,128]{2,1,0:T(8,128)S(1)}, f32[128,8,128]{2,1,0:T(8,128)S(1)}, u32[]{:S(2)}, u32[]{:S(2)}) collective-permute-start(f32[128,8,128]{2,1,0:T(8,128)S(1)} %get-tuple-element.49), channel_id=1, source_target_pairs={{8,16},{16,8},{24,32},{32,24},{40,48},{48,40},{9,17},{17,9},{25,33... | collective-permute-start | bytes 1572872 | tf_op jit(solution)/shard_map/ppermute | solution.py:300
  149.6 15.3 %collective-permute-start.29 = (f32[8,8,128]{2,1,0:T(8,128)S(1)}, f32[8,8,128]{2,1,0:T(8,128)S(1)}, u32[]{:S(2)}, u32[]{:S(2)}) collective-permute-start(f32[8,8,128]{2,1,0:T(8,128)S(1)} %get-tuple-element.47.order), channel_id=1, source_target_pairs={{0,64},{64,0},{1,65},{65,1},{2,66},{66,2},{3,67},{67,3},{4,68},{68... | collective-permute-start | bytes 98312 | tf_op jit(solution)/shard_map/ppermute | solution.py:300
  173.8 5.8 %collective-permute-start.30 = (f32[2,8,8,128]{3,2,1,0:T(8,128)S(1)}, f32[2,8,8,128]{3,2,1,0:T(8,128)S(1)}, u32[]{:S(2)}, u32[]{:S(2)}) collective-permute-start(f32[2,8,8,128]{3,2,1,0:T(8,128)S(1)} %get-tuple-element.51.mine), channel_id=1, source_target_pairs={{0,64},{64,0},{1,65},{65,1},{2,66},{66,2},{3,67},{67,3},{4,68},{68... | collective-permute-start | bytes 196616 | tf_op jit(solution)/shard_map/ppermute | solution.py:300
  179.6 2.2 %copy-start.1 = (f32[128,8,8,128]{3,2,1,0:T(8,128)S(1)}, f32[128,8,8,128]{3,2,1,0:T(8,128)}, u32[]{:S(2)}) copy-start(f32[128,8,8,128]{3,2,1,0:T(8,128)} %get-tuple-element.26.f) | copy-start | bytes 12582916

commit v3 on v2

--- a/solution.py
+++ b/solution.py
@@ -13,6 +13,8 @@
 SMEM = pltpu.SMEM
 HBM = pltpu.HBM
 ROWS = 8
+QUAD = 4
+PAIR = 2
 
 
 def swap_pairs(devices, first):
@@ -132,7 +134,7 @@
     lax.fori_loop(0, rows // n, body, before)
 
 
-def update_rows(flags, f, fj, fi, fk, ha, hb, e1, e2, s, emit):
+def sweep(flags, f, fj, fi, fk, ha, hb, e1, e2, s, start, visit, finish):
     rows, ni, nk, nl = f.shape
     i_even = flags[1] == 0
     low_south = flags[2] == 0
@@ -140,82 +142,98 @@
     a_edge = sub == jnp.where(flags[0] == 0, nk - 1, 0)
     first_k = sub == 0
     last_k = sub == nk - 1
-
-    def row(j, prev, cur, nxt):
-        x1 = e1[j]
-        x2 = e2[j]
-        below = jnp.where(i_even, x2, x1)
-        above = jnp.where(i_even, x1, x2)
-        new = []
-        for i in range(ni):
-            c = cur[i]
-            ra = jnp.broadcast_to(ha[j, pl.ds(i, 1), :], (nk, nl))
-            rb = jnp.broadcast_to(hb[j, pl.ds(i, 1), :], (nk, nl))
-            edge = jnp.where(a_edge, ra, rb)
-            kl = jnp.where(first_k, edge, pltpu.roll(c, 1, 0))
-            ku = jnp.where(last_k, edge, pltpu.roll(c, nk - 1, 0))
-            il = below if i == 0 else cur[i - 1]
-            iu = above if i == ni - 1 else cur[i + 1]
-            new.append(
-                combine(c, prev[i], nxt[i], il, iu, kl, ku, fj[j, i], fi[j, i], fk[j, i])
-            )
-        emit(j, new)
-
-    def body(j, carry):
-        prev, cur = carry
-        nxt = tuple(f[j + 1, i] for i in range(ni))
-        row(j, prev, cur, nxt)
-        return cur, nxt
-
     zero = jnp.zeros((nk, nl), F32)
-    start = (
-        tuple(jnp.where(low_south, zero, s[i]) for i in range(ni)),
-        tuple(f[0, i] for i in range(ni)),
-    )
-    prev, cur = lax.fori_loop(0, rows - 1, body, start, unroll=False)
-    row(rows - 1, prev, cur, tuple(jnp.where(low_south, s[i], zero) for i in range(ni)))
+
+    for i0 in range(0, ni, QUAD):
+        quad = range(i0, i0 + QUAD)
+        before = [jnp.where(low_south, zero, s[i]) for i in quad]
+        after = [jnp.where(low_south, s[i], zero) for i in quad]
+
+        def body(t, carry):
+            prev, state = carry
+            j0 = t * PAIR
+            end = j0 + PAIR == rows
+            jn = jnp.minimum(j0 + PAIR, rows - 1)
+            cur = [prev]
+            cur += [[f[j0 + r, i] for i in quad] for r in range(PAIR)]
+            cur.append([jnp.where(end, a, f[jn, i]) for a, i in zip(after, quad)])
+            for r in range(PAIR):
+                j = j0 + r
+                row = cur[r + 1]
+                if i0 == 0:
+                    below = jnp.where(i_even, e2[j], e1[j])
+                else:
+                    below = f[j, i0 - 1]
+                if i0 + QUAD == ni:
+                    above = jnp.where(i_even, e1[j], e2[j])
+                else:
+                    above = f[j, i0 + QUAD]
+                line = [below, *row, above]
+                new = []
+                for n, i in enumerate(quad):
+                    c = row[n]
+                    ra = jnp.broadcast_to(ha[j, pl.ds(i, 1), :], (nk, nl))
+                    rb = jnp.broadcast_to(hb[j, pl.ds(i, 1), :], (nk, nl))
+                    edge = jnp.where(a_edge, ra, rb)
+                    kl = jnp.where(first_k, edge, pltpu.roll(c, 1, 0))
+                    ku = jnp.where(last_k, edge, pltpu.roll(c, nk - 1, 0))
+                    new.append(
+                        combine(
+                            c, cur[r][n], cur[r + 2][n], line[n], line[n + 2], kl, ku,
+                            fj[j, i], fi[j, i], fk[j, i],
+                        )
+                    )
+                state = visit(j, r, quad, new, state)
+            return cur[PAIR], state
+
+        _, state = lax.fori_loop(0, rows // PAIR, body, (before, start(quad, zero)))
+        finish(quad, state)
 
 
 def full_body(flags, f, fj, fi, fk, ha, hb, e1, e2, s, order, out):
-    _, ni, _, _ = f.shape
-
-    def emit(j, new):
-        for i in range(ni):
-            out[j, i] = new[i]
-
-    update_rows(flags, f, fj, fi, fk, ha, hb, e1, e2, s, emit)
+    def visit(j, r, quad, new, state):
+        for i, x in zip(quad, new):
+            out[j, i] = x
+        return state
+
+    sweep(
+        flags, f, fj, fi, fk, ha, hb, e1, e2, s,
+        lambda quad, zero: 0, visit, lambda quad, state: None,
+    )
 
 
 def final_body(flags, f, fj, fi, fk, ha, hb, e1, e2, s, out, stats):
-    rows, ni, nk, nl = f.shape
-
-    def emit(j, new):
-        for i in range(ni):
-            out[j, i] = new[i]
-
-    update_rows(flags, f, fj, fi, fk, ha, hb, e1, e2, s, emit)
-    zero = tuple(jnp.zeros((nk, nl), F32) for _ in range(ni))
-
-    def add(j, sums):
-        return tuple(a + out[j, i] for i, a in enumerate(sums))
-
-    means = tuple(a * (1.0 / rows) for a in lax.fori_loop(0, rows, add, zero, unroll=2))
-
-    def add_square(j, sums):
-        new = []
-        for i, a in enumerate(sums):
-            d = out[j, i] - means[i]
-            new.append(a + d * d)
-        return tuple(new)
-
-    spread = lax.fori_loop(0, rows, add_square, zero, unroll=2)
-    for i in range(ni):
-        stats[0, i] = means[i]
-        stats[1, i] = spread[i]
-
-
-def scale_body(f, mine, other, out):
+    rows = f.shape[0]
+
+    def start(quad, zero):
+        return tuple([zero] * QUAD for _ in range(3))
+
+    def visit(j, r, quad, new, state):
+        shift, sums, squares = state
+        if r == 0:
+            shift = [jnp.where(j == 0, x, a) for x, a in zip(new, shift)]
+        moved = [x - a for x, a in zip(new, shift)]
+        for i, x in zip(quad, new):
+            out[j, i] = x
+        return (
+            shift,
+            [a + m for a, m in zip(sums, moved)],
+            [a + m * m for a, m in zip(squares, moved)],
+        )
+
+    def finish(quad, state):
+        for i, shift, total, square in zip(quad, *state):
+            mean = total * (1.0 / rows)
+            stats[0, i] = shift + mean
+            stats[1, i] = jnp.maximum(square - total * mean, 0.0)
+
+    sweep(flags, f, fj, fi, fk, ha, hb, e1, e2, s, start, visit, finish)
+
+
+def scale_body(f, mine, other, out, buf, sems):
     rows, ni, _, _ = f.shape
+    chunks = sems.shape[0]
+    size = rows // chunks
     mean = []
     scale = []
     for i in range(ni):
@@ -226,10 +244,23 @@
 
     def body(j, _):
         for i in range(ni):
-            out[j, i] = (f[j, i] - mean[i]) * scale[i]
+            buf[j, i] = (f[j, i] - mean[i]) * scale[i]
         return 0
 
-    lax.fori_loop(0, rows, body, 0, unroll=2)
+    copies = []
+    for n in range(chunks):
+        lax.fori_loop(n * size, (n + 1) * size, body, 0, unroll=2)
+        part = pl.ds(n * size, size)
+        copies.append(pltpu.make_async_copy(buf.at[part], out.at[part], sems.at[n]))
+        copies[-1].start()
+    for c in copies:
+        c.wait()
+
+
+def store_body(f, order, out, sem):
+    copy = pltpu.make_async_copy(f, out, sem)
+    copy.start()
+    copy.wait()
 
 
 def first_a_body(flags, f, ga, sem):
@@ -270,7 +301,7 @@
         c.wait()
 
 
-def call(body, args, outs, mib=2, spaces=None, scratch=()):
+def call(body, args, outs, mib=2, spaces=None, scratch=(), out_space=VMEM):
     spaces = spaces or [VMEM] * len(args)
     if args[0].dtype == jnp.int32:
         spaces = [SMEM, *spaces[1:]]
@@ -278,7 +309,7 @@
         body,
         out_shape=[jax.ShapeDtypeStruct(o, F32) for o in outs],
         in_specs=[pl.BlockSpec(memory_space=m) for m in spaces],
-        out_specs=[pl.BlockSpec(memory_space=VMEM) for _ in outs],
+        out_specs=[pl.BlockSpec(memory_space=out_space) for _ in outs],
         scratch_shapes=scratch,
         compiler_params=pltpu.CompilerParams(vmem_limit_bytes=mib << 20),
     )(*args)
@@ -336,11 +367,15 @@
         ha, hb = ha_next, hb_next
     field, stats = call(
         final_body, [flags, field, fj, fi, fk, ha, hb, e1, e2, s],
-        [field.shape, (2, ni, nk, nl)], 12,
+        [field.shape, (2, ni, nk, nl)],
     )
     other = swap(stats, "south", 0)
-    (standardized,) = call(scale_body, [field, stats, other], [field.shape], 12)
-    return (standardized, field)
+    (end,) = call(store_body, [field, stats], [field.shape], scratch=[sem], out_space=HBM)
+    (standardized,) = call(
+        scale_body, [field, stats, other], [field.shape], 8,
+        scratch=[pltpu.VMEM(field.shape, F32), sem((8,))], out_space=HBM,
+    )
+    return (standardized, end)
 
 
 def solution(mesh):

time: 187 us -> 182 us (0.973)
  local copies, waits for them, and re-layouts: 2.19 us -> 0.01 us
  waiting for transfers between devices: 69.5 us -> 67.5 us
    unnamed x4 -> x2, local copies, waits for them, and re-layouts: 2.19 us -> 0.01 us
    ppermute x31, waiting for transfers between devices: 69.5 us -> 67.5 us  [swap(): return lax.ppermute(x, axis, swap_pairs(lax.axis_size(axis), first))]
    pallas_call x25 -> x26, Pallas kernels: 65.4 us -> 64.6 us  [call(): pl.pallas_call(body, out_shape=[jax.ShapeDtypeStruct(o, F32) for o in out...]
  transfers between devices with their start and end apart: 31 -> 31, of which waited for: 9 -> 9; matrix products, arithmetic and copies ran while one was open for 0% -> 0% of each run, Pallas kernels for 29% -> 31%
where the time goes in v3:
time: 182 us; the launch traced here: 180 us
  waiting for transfers between devices  67.5 us (37%)
  Pallas kernels  64.6 us (35%)
  starting transfers between devices  46.4 us (25%)
    ppermute x31, waiting for transfers between devices, swap(): return lax.ppermute(x, axis, swap_pairs(lax.axis_size(axis), first))  67.5 us
    pallas_call x26, Pallas kernels, call(): pl.pallas_call(body, out_shape=[jax.ShapeDtypeStruct(o, F32) for o in out...  64.6 us
    ppermute x31, starting transfers between devices, swap(): return lax.ppermute(x, axis, swap_pairs(lax.axis_size(axis), first))  46.4 us
  transfers between devices with their start and end apart: 31, of which 9 were waited for; matrix products, arithmetic and copies ran while one was open for 0% of the time, Pallas kernels for 31%

profile of v3, /device:TPU:96, one launch (start us, length us, event | category | flops | bytes accessed | tf_op | source)
XLA Modules:
  0.0 179.6 jit_solution(2417119761290388820)
XLA Ops:
  0.7 1.9 %shard_map.59.order = f32[128,8,1,128]{3,2,1,0:T(1,128)S(1)} custom-call(s32[3]{0:T(128)S(1)} %pad_add_fusion.flags, f32[128,8,8,1,128]{4,3,2,1,0:T(1,128)} %bitcast.62), custom_call_target="tpu_custom_call" | custom-call | tf_op jit(solution)/shard_map/pallas_call | solution.py:308
  2.6 1.6 collective-permute-start
  4.2 1.9 %shard_map.60 = (f32[128,8,1,128]{3,2,1,0:T(1,128)S(1)}, f32[128,8,1,128]{3,2,1,0:T(1,128)S(1)}, f32[128,8,1,128]{3,2,1,0:T(1,128)S(1)}, f32[8,8,1,128]{3,2,1,0:T(1,128)S(1)}) custom-call(s32[3]{0:T(128)S(1)} %pad_add_fusion.flags, f32[128,8,8,1,128]{4,3,2,1,0:T(1,128)} %bitcast.63, f32[128,8,1,128]{3,2,1,0:T(1,128)S(1)} %shard_map.59.order), custom_call_target="tpu_custom_call" | custom-call | tf_op jit(solution)/shard_map/pallas_call | solution.py:308
  6.2 0.7 collective-permute-start.3
  6.9 2.3 %collective-permute-start.1 = (f32[128,8,128]{2,1,0:T(8,128)S(1)}, f32[128,8,128]{2,1,0:T(8,128)S(1)}, u32[]{:S(2)}, u32[]{:S(2)}) collective-permute-start(f32[128,8,128]{2,1,0:T(8,128)S(1)} %bitcast.76), channel_id=1, source_target_pairs={{1,2},{2,1},{3,4},{4,3},{5,6},{6,5},{9,10},{10,9},{11,12},{12,11},... | collective-permute-start | bytes 1572872 | tf_op jit(solution)/shard_map/ppermute | solution.py:331
  9.2 3.1 %collective-permute-start.4 = (f32[8,8,128]{2,1,0:T(8,128)S(1)}, f32[8,8,128]{2,1,0:T(8,128)S(1)}, u32[]{:S(2)}, u32[]{:S(2)}) collective-permute-start(f32[8,8,128]{2,1,0:T(8,128)S(1)} %bitcast.75), channel_id=1, source_target_pairs={{0,64},{64,0},{1,65},{65,1},{2,66},{66,2},{3,67},{67,3},{4,68},{68... | collective-permute-start | bytes 98312 | tf_op jit(solution)/shard_map/ppermute | solution.py:331
  12.4 5.0 %shard_map.61 = (f32[128,8,8,128]{3,2,1,0:T(8,128)S(1)}, f32[128,8,8,128]{3,2,1,0:T(8,128)S(1)}, f32[128,8,8,128]{3,2,1,0:T(8,128)S(1)}, f32[128,8,8,128]{3,2,1,0:T(8,128)S(1)}) custom-call(f32[128,8,8,128]{3,2,1,0:T(8,128)S(1)} %copy-done, f32[128,8,8,128]{3,2,1,0:T(8,128)} %refs_1_.1, f32[128,8,8,128]{3,2,1,0:T(8,128)} %refs_2_.1, ...), custom_call_target="tpu_custom_call" | custom-call | tf_op jit(solution)/shard_map/pallas_call | solution.py:308
  17.3 13.1 %collective-permute-done.4.s = f32[8,8,128]{2,1,0:T(8,128)S(1)} collective-permute-done((f32[8,8,128]{2,1,0:T(8,128)S(1)}, f32[8,8,128]{2,1,0:T(8,128)S(1)}, u32[]{:S(2)}, u32[]{:S(2)}) %collective-permute-start.4) | collective-permute-done | bytes 32800 | tf_op jit(solution)/shard_map/ppermute | solution.py:331
  30.5 1.5 shard_map.65
  32.1 1.5 shard_map.62.order
  33.6 1.7 shard_map.63
  36.0 3.8 %collective-permute-start.6 = (f32[128,8,128]{2,1,0:T(8,128)S(1)}, f32[128,8,128]{2,1,0:T(8,128)S(1)}, u32[]{:S(2)}, u32[]{:S(2)}) collective-permute-start(f32[128,8,128]{2,1,0:T(8,128)S(1)} %shard_map.62.order), channel_id=1, source_target_pairs={{1,2},{2,1},{3,4},{4,3},{5,6},{6,5},{9,10},{10,9},{11,12},{12,11},... | collective-permute-start | bytes 1572872 | tf_op jit(solution)/shard_map/ppermute | solution.py:331
  39.8 0.9 collective-permute-start.9
  40.7 4.6 %shard_map.64.f = f32[128,8,8,128]{3,2,1,0:T(8,128)S(1)} custom-call(s32[3]{0:T(128)S(1)} %pad_add_fusion.flags, f32[128,8,8,128]{3,2,1,0:T(8,128)S(1)} %get-tuple-element.28.f, f32[128,8,8,128]{3,2,1,0:T(8,128)S(1)} %get-tuple-element.29.fj, f32[128,8,8,128]{3,2,1,0:T(8,128)S(1)} %get-tuple-element.30.fi, f32[128,8,8,128]{3,2,1,0:T(8,128)S(1)} %get-tuple-element.31.fk, ...), custom_call_target="tpu_custom_call" | custom-call | tf_op jit(solution)/shard_map/pallas_call | solution.py:308
  45.3 10.5 %collective-permute-done.9.s = f32[8,8,128]{2,1,0:T(8,128)S(1)} collective-permute-done((f32[8,8,128]{2,1,0:T(8,128)S(1)}, f32[8,8,128]{2,1,0:T(8,128)S(1)}, u32[]{:S(2)}, u32[]{:S(2)}) %collective-permute-start.9) | collective-permute-done | bytes 32800 | tf_op jit(solution)/shard_map/ppermute | solution.py:331
  55.8 1.5 shard_map.69
  57.4 1.5 shard_map.66.order
  58.8 1.7 shard_map.67
  61.4 4.5 %collective-permute-start.11 = (f32[128,8,128]{2,1,0:T(8,128)S(1)}, f32[128,8,128]{2,1,0:T(8,128)S(1)}, u32[]{:S(2)}, u32[]{:S(2)}) collective-permute-start(f32[128,8,128]{2,1,0:T(8,128)S(1)} %shard_map.66.order), channel_id=1, source_target_pairs={{1,2},{2,1},{3,4},{4,3},{5,6},{6,5},{9,10},{10,9},{11,12},{12,11},... | collective-permute-start | bytes 1572872 | tf_op jit(solution)/shard_map/ppermute | solution.py:331
  65.9 2.1 %collective-permute-start.14 = (f32[8,8,128]{2,1,0:T(8,128)S(1)}, f32[8,8,128]{2,1,0:T(8,128)S(1)}, u32[]{:S(2)}, u32[]{:S(2)}) collective-permute-start(f32[8,8,128]{2,1,0:T(8,128)S(1)} %get-tuple-element.38.order), channel_id=1, source_target_pairs={{0,64},{64,0},{1,65},{65,1},{2,66},{66,2},{3,67},{67,3},{4,68},{68... | collective-permute-start | bytes 98312 | tf_op jit(solution)/shard_map/ppermute | solution.py:331
  68.0 4.6 %shard_map.68.f = f32[128,8,8,128]{3,2,1,0:T(8,128)S(1)} custom-call(s32[3]{0:T(128)S(1)} %pad_add_fusion.flags, f32[128,8,8,128]{3,2,1,0:T(8,128)S(1)} %shard_map.64.f, f32[128,8,8,128]{3,2,1,0:T(8,128)S(1)} %get-tuple-element.29.fj, f32[128,8,8,128]{3,2,1,0:T(8,128)S(1)} %get-tuple-element.30.fi, f32[128,8,8,128]{3,2,1,0:T(8,128)S(1)} %get-tuple-element.31.fk, ...), custom_call_target="tpu_custom_call" | custom-call | tf_op jit(solution)/shard_map/pallas_call | solution.py:308
  72.6 11.1 %collective-permute-done.14.s = f32[8,8,128]{2,1,0:T(8,128)S(1)} collective-permute-done((f32[8,8,128]{2,1,0:T(8,128)S(1)}, f32[8,8,128]{2,1,0:T(8,128)S(1)}, u32[]{:S(2)}, u32[]{:S(2)}) %collective-permute-start.14) | collective-permute-done | bytes 32800 | tf_op jit(solution)/shard_map/ppermute | solution.py:331
  83.7 1.5 shard_map.73
  85.3 1.5 shard_map.70.order
  86.8 1.7 shard_map.71
  89.2 6.0 %collective-permute-start.16 = (f32[128,8,128]{2,1,0:T(8,128)S(1)}, f32[128,8,128]{2,1,0:T(8,128)S(1)}, u32[]{:S(2)}, u32[]{:S(2)}) collective-permute-start(f32[128,8,128]{2,1,0:T(8,128)S(1)} %shard_map.70.order), channel_id=1, source_target_pairs={{1,2},{2,1},{3,4},{4,3},{5,6},{6,5},{9,10},{10,9},{11,12},{12,11},... | collective-permute-start | bytes 1572872 | tf_op jit(solution)/shard_map/ppermute | solution.py:331
  95.3 4.6 %shard_map.72.f = f32[128,8,8,128]{3,2,1,0:T(8,128)S(1)} custom-call(s32[3]{0:T(128)S(1)} %pad_add_fusion.flags, f32[128,8,8,128]{3,2,1,0:T(8,128)S(1)} %shard_map.68.f, f32[128,8,8,128]{3,2,1,0:T(8,128)S(1)} %get-tuple-element.29.fj, f32[128,8,8,128]{3,2,1,0:T(8,128)S(1)} %get-tuple-element.30.fi, f32[128,8,8,128]{3,2,1,0:T(8,128)S(1)} %get-tuple-element.31.fk, ...), custom_call_target="tpu_custom_call" | custom-call | tf_op jit(solution)/shard_map/pallas_call | solution.py:308
  100.0 10.6 %collective-permute-done.19.s = f32[8,8,128]{2,1,0:T(8,128)S(1)} collective-permute-done((f32[8,8,128]{2,1,0:T(8,128)S(1)}, f32[8,8,128]{2,1,0:T(8,128)S(1)}, u32[]{:S(2)}, u32[]{:S(2)}) %collective-permute-start.19) | collective-permute-done | bytes 32800 | tf_op jit(solution)/shard_map/ppermute | solution.py:331
  110.5 1.5 shard_map.77
  112.1 1.5 shard_map.74.order
  113.5 1.7 shard_map.75
  116.0 4.2 %collective-permute-start.21 = (f32[128,8,128]{2,1,0:T(8,128)S(1)}, f32[128,8,128]{2,1,0:T(8,128)S(1)}, u32[]{:S(2)}, u32[]{:S(2)}) collective-permute-start(f32[128,8,128]{2,1,0:T(8,128)S(1)} %shard_map.74.order), channel_id=1, source_target_pairs={{1,2},{2,1},{3,4},{4,3},{5,6},{6,5},{9,10},{10,9},{11,12},{12,11},... | collective-permute-start | bytes 1572872 | tf_op jit(solution)/shard_map/ppermute | solution.py:331
  120.2 3.4 %collective-permute-start.24 = (f32[8,8,128]{2,1,0:T(8,128)S(1)}, f32[8,8,128]{2,1,0:T(8,128)S(1)}, u32[]{:S(2)}, u32[]{:S(2)}) collective-permute-start(f32[8,8,128]{2,1,0:T(8,128)S(1)} %get-tuple-element.44.order), channel_id=1, source_target_pairs={{0,64},{64,0},{1,65},{65,1},{2,66},{66,2},{3,67},{67,3},{4,68},{68... | collective-permute-start | bytes 98312 | tf_op jit(solution)/shard_map/ppermute | solution.py:331
  123.6 4.6 %shard_map.76.f = f32[128,8,8,128]{3,2,1,0:T(8,128)S(1)} custom-call(s32[3]{0:T(128)S(1)} %pad_add_fusion.flags, f32[128,8,8,128]{3,2,1,0:T(8,128)S(1)} %shard_map.72.f, f32[128,8,8,128]{3,2,1,0:T(8,128)S(1)} %get-tuple-element.29.fj, f32[128,8,8,128]{3,2,1,0:T(8,128)S(1)} %get-tuple-element.30.fi, f32[128,8,8,128]{3,2,1,0:T(8,128)S(1)} %get-tuple-element.31.fk, ...), custom_call_target="tpu_custom_call" | custom-call | tf_op jit(solution)/shard_map/pallas_call | solution.py:308
  128.2 7.2 %collective-permute-done.24.s = f32[8,8,128]{2,1,0:T(8,128)S(1)} collective-permute-done((f32[8,8,128]{2,1,0:T(8,128)S(1)}, f32[8,8,128]{2,1,0:T(8,128)S(1)}, u32[]{:S(2)}, u32[]{:S(2)}) %collective-permute-start.24) | collective-permute-done | bytes 32800 | tf_op jit(solution)/shard_map/ppermute | solution.py:331
  135.5 1.5 shard_map.81
  137.0 0.8 collective-permute-done.21.halo.hb
  137.9 1.5 shard_map.78.order
  139.3 7.8 %collective-permute-start.26 = (f32[128,8,128]{2,1,0:T(8,128)S(1)}, f32[128,8,128]{2,1,0:T(8,128)S(1)}, u32[]{:S(2)}, u32[]{:S(2)}) collective-permute-start(f32[128,8,128]{2,1,0:T(8,128)S(1)} %shard_map.78.order), channel_id=1, source_target_pairs={{1,2},{2,1},{3,4},{4,3},{5,6},{6,5},{9,10},{10,9},{11,12},{12,11},... | collective-permute-start | bytes 1572872 | tf_op jit(solution)/shard_map/ppermute | solution.py:331
  147.1 1.7 shard_map.79
  149.8 4.6 %shard_map.80.f = f32[128,8,8,128]{3,2,1,0:T(8,128)S(1)} custom-call(s32[3]{0:T(128)S(1)} %pad_add_fusion.flags, f32[128,8,8,128]{3,2,1,0:T(8,128)S(1)} %shard_map.76.f, f32[128,8,8,128]{3,2,1,0:T(8,128)S(1)} %get-tuple-element.29.fj, f32[128,8,8,128]{3,2,1,0:T(8,128)S(1)} %get-tuple-element.30.fi, f32[128,8,8,128]{3,2,1,0:T(8,128)S(1)} %get-tuple-element.31.fk, ...), custom_call_target="tpu_custom_call" | custom-call | tf_op jit(solution)/shard_map/pallas_call | solution.py:308
  154.5 10.4 %collective-permute-done.29.s = f32[8,8,128]{2,1,0:T(8,128)S(1)} collective-permute-done((f32[8,8,128]{2,1,0:T(8,128)S(1)}, f32[8,8,128]{2,1,0:T(8,128)S(1)}, u32[]{:S(2)}, u32[]{:S(2)}) %collective-permute-start.29) | collective-permute-done | bytes 32800 | tf_op jit(solution)/shard_map/ppermute | solution.py:331
  164.9 1.1 collective-permute-done.26.hb
  166.0 5.6 %shard_map.82 = (f32[128,8,8,128]{3,2,1,0:T(8,128)S(1)}, f32[2,8,8,128]{3,2,1,0:T(8,128)S(1)}) custom-call(s32[3]{0:T(128)S(1)} %pad_add_fusion.flags, f32[128,8,8,128]{3,2,1,0:T(8,128)S(1)} %shard_map.80.f, f32[128,8,8,128]{3,2,1,0:T(8,128)S(1)} %get-tuple-element.29.fj, f32[128,8,8,128]{3,2,1,0:T(8,128)S(1)} %get-tuple-element.30.fi, ...), custom_call_target="tpu_custom_call" | custom-call | tf_op jit(solution)/shard_map/pallas_call | solution.py:308
  171.6 1.2 collective-permute-start.30
  172.7 2.0 %shard_map.84 = f32[128,8,8,128]{3,2,1,0:T(8,128)} custom-call(f32[128,8,8,128]{3,2,1,0:T(8,128)S(1)} %get-tuple-element.50.f, f32[2,8,8,128]{3,2,1,0:T(8,128)S(1)} %get-tuple-element.51.mine.order), custom_call_target="tpu_custom_call" | custom-call | tf_op jit(solution)/shard_map/pallas_call | solution.py:308
  174.8 2.6 %collective-permute-done.30.other = f32[2,8,8,128]{3,2,1,0:T(8,128)S(1)} collective-permute-done((f32[2,8,8,128]{3,2,1,0:T(8,128)S(1)}, f32[2,8,8,128]{3,2,1,0:T(8,128)S(1)}, u32[]{:S(2)}, u32[]{:S(2)}) %collective-permute-start.30) | collective-permute-done | bytes 65568 | tf_op jit(solution)/shard_map/ppermute | solution.py:331
  177.4 2.2 %shard_map.83 = f32[128,8,8,128]{3,2,1,0:T(8,128)} custom-call(f32[128,8,8,128]{3,2,1,0:T(8,128)S(1)} %get-tuple-element.50.f, f32[2,8,8,128]{3,2,1,0:T(8,128)S(1)} %get-tuple-element.51.mine.order, f32[2,8,8,128]{3,2,1,0:T(8,128)S(1)} %collective-permute-done.30.other), custom_call_target="tpu_custom_call" | custom-call | tf_op jit(solution)/shard_map/pallas_call | solution.py:308
  (43 shorter events, 5.0 us)
Async XLA Ops:
  0.7 11.6 %copy-start = (f32[128,8,8,128]{3,2,1,0:T(8,128)S(1)}, f32[128,8,8,128]{3,2,1,0:T(8,128)}, u32[]{:S(2)}) copy-start(f32[128,8,8,128]{3,2,1,0:T(8,128)} %refs_0_.1) | copy-start | bytes 12582916
  2.6 27.9 %collective-permute-start = (f32[128,8,128]{2,1,0:T(8,128)S(1)}, f32[128,8,128]{2,1,0:T(8,128)S(1)}, u32[]{:S(2)}, u32[]{:S(2)}) collective-permute-start(f32[128,8,128]{2,1,0:T(8,128)S(1)} %bitcast.64), channel_id=1, source_target_pairs={{0,1},{1,0},{2,3},{3,2},{4,5},{5,4},{6,7},{7,6},{8,9},{9,8},{10,11... | collective-permute-start | bytes 1572872 | tf_op jit(solution)/shard_map/ppermute | solution.py:331
  6.1 24.4 %collective-permute-start.2 = (f32[128,8,128]{2,1,0:T(8,128)S(1)}, f32[128,8,128]{2,1,0:T(8,128)S(1)}, u32[]{:S(2)}, u32[]{:S(2)}) collective-permute-start(f32[128,8,128]{2,1,0:T(8,128)S(1)} %bitcast.78), channel_id=1, source_target_pairs={{0,8},{8,0},{16,24},{24,16},{32,40},{40,32},{48,56},{56,48},{1,9},... | collective-permute-start | bytes 1572872 | tf_op jit(solution)/shard_map/ppermute | solution.py:331
  6.2 24.3 %collective-permute-start.3 = (f32[128,8,128]{2,1,0:T(8,128)S(1)}, f32[128,8,128]{2,1,0:T(8,128)S(1)}, u32[]{:S(2)}, u32[]{:S(2)}) collective-permute-start(f32[128,8,128]{2,1,0:T(8,128)S(1)} %bitcast.77), channel_id=1, source_target_pairs={{8,16},{16,8},{24,32},{32,24},{40,48},{48,40},{9,17},{17,9},{25,33... | collective-permute-start | bytes 1572872 | tf_op jit(solution)/shard_map/ppermute | solution.py:331
  6.9 25.2 %collective-permute-start.1 = (f32[128,8,128]{2,1,0:T(8,128)S(1)}, f32[128,8,128]{2,1,0:T(8,128)S(1)}, u32[]{:S(2)}, u32[]{:S(2)}) collective-permute-start(f32[128,8,128]{2,1,0:T(8,128)S(1)} %bitcast.76), channel_id=1, source_target_pairs={{1,2},{2,1},{3,4},{4,3},{5,6},{6,5},{9,10},{10,9},{11,12},{12,11},... | collective-permute-start | bytes 1572872 | tf_op jit(solution)/shard_map/ppermute | solution.py:331
  9.2 21.2 %collective-permute-start.4 = (f32[8,8,128]{2,1,0:T(8,128)S(1)}, f32[8,8,128]{2,1,0:T(8,128)S(1)}, u32[]{:S(2)}, u32[]{:S(2)}) collective-permute-start(f32[8,8,128]{2,1,0:T(8,128)S(1)} %bitcast.75), channel_id=1, source_target_pairs={{0,64},{64,0},{1,65},{65,1},{2,66},{66,2},{3,67},{67,3},{4,68},{68... | collective-permute-start | bytes 98312 | tf_op jit(solution)/shard_map/ppermute | solution.py:331
  32.0 23.8 %collective-permute-start.5 = (f32[128,8,128]{2,1,0:T(8,128)S(1)}, f32[128,8,128]{2,1,0:T(8,128)S(1)}, u32[]{:S(2)}, u32[]{:S(2)}) collective-permute-start(f32[128,8,128]{2,1,0:T(8,128)S(1)} %shard_map.65), channel_id=1, source_target_pairs={{0,1},{1,0},{2,3},{3,2},{4,5},{5,4},{6,7},{7,6},{8,9},{9,8},{10,11... | collective-permute-start | bytes 1572872 | tf_op jit(solution)/shard_map/ppermute | solution.py:331
  35.2 20.6 %collective-permute-start.7 = (f32[128,8,128]{2,1,0:T(8,128)S(1)}, f32[128,8,128]{2,1,0:T(8,128)S(1)}, u32[]{:S(2)}, u32[]{:S(2)}) collective-permute-start(f32[128,8,128]{2,1,0:T(8,128)S(1)} %get-tuple-element.36), channel_id=1, source_target_pairs={{0,8},{8,0},{16,24},{24,16},{32,40},{40,32},{48,56},{56,48},{1,9},... | collective-permute-start | bytes 1572872 | tf_op jit(solution)/shard_map/ppermute | solution.py:331
  35.3 20.5 %collective-permute-start.8 = (f32[128,8,128]{2,1,0:T(8,128)S(1)}, f32[128,8,128]{2,1,0:T(8,128)S(1)}, u32[]{:S(2)}, u32[]{:S(2)}) collective-permute-start(f32[128,8,128]{2,1,0:T(8,128)S(1)} %get-tuple-element.37), channel_id=1, source_target_pairs={{8,16},{16,8},{24,32},{32,24},{40,48},{48,40},{9,17},{17,9},{25,33... | collective-permute-start | bytes 1572872 | tf_op jit(solution)/shard_map/ppermute | solution.py:331
  36.0 21.3 %collective-permute-start.6 = (f32[128,8,128]{2,1,0:T(8,128)S(1)}, f32[128,8,128]{2,1,0:T(8,128)S(1)}, u32[]{:S(2)}, u32[]{:S(2)}) collective-permute-start(f32[128,8,128]{2,1,0:T(8,128)S(1)} %shard_map.62.order), channel_id=1, source_target_pairs={{1,2},{2,1},{3,4},{4,3},{5,6},{6,5},{9,10},{10,9},{11,12},{12,11},... | collective-permute-start | bytes 1572872 | tf_op jit(solution)/shard_map/ppermute | solution.py:331
  39.8 16.0 %collective-permute-start.9 = (f32[8,8,128]{2,1,0:T(8,128)S(1)}, f32[8,8,128]{2,1,0:T(8,128)S(1)}, u32[]{:S(2)}, u32[]{:S(2)}) collective-permute-start(f32[8,8,128]{2,1,0:T(8,128)S(1)} %get-tuple-element.35.order), channel_id=1, source_target_pairs={{0,64},{64,0},{1,65},{65,1},{2,66},{66,2},{3,67},{67,3},{4,68},{68... | collective-permute-start | bytes 98312 | tf_op jit(solution)/shard_map/ppermute | solution.py:331
  57.3 26.5 %collective-permute-start.10 = (f32[128,8,128]{2,1,0:T(8,128)S(1)}, f32[128,8,128]{2,1,0:T(8,128)S(1)}, u32[]{:S(2)}, u32[]{:S(2)}) collective-permute-start(f32[128,8,128]{2,1,0:T(8,128)S(1)} %shard_map.69), channel_id=1, source_target_pairs={{0,1},{1,0},{2,3},{3,2},{4,5},{5,4},{6,7},{7,6},{8,9},{9,8},{10,11... | collective-permute-start | bytes 1572872 | tf_op jit(solution)/shard_map/ppermute | solution.py:331
  60.5 23.2 %collective-permute-start.12 = (f32[128,8,128]{2,1,0:T(8,128)S(1)}, f32[128,8,128]{2,1,0:T(8,128)S(1)}, u32[]{:S(2)}, u32[]{:S(2)}) collective-permute-start(f32[128,8,128]{2,1,0:T(8,128)S(1)} %get-tuple-element.39), channel_id=1, source_target_pairs={{0,8},{8,0},{16,24},{24,16},{32,40},{40,32},{48,56},{56,48},{1,9},... | collective-permute-start | bytes 1572872 | tf_op jit(solution)/shard_map/ppermute | solution.py:331
  60.7 23.0 %collective-permute-start.13 = (f32[128,8,128]{2,1,0:T(8,128)S(1)}, f32[128,8,128]{2,1,0:T(8,128)S(1)}, u32[]{:S(2)}, u32[]{:S(2)}) collective-permute-start(f32[128,8,128]{2,1,0:T(8,128)S(1)} %get-tuple-element.40), channel_id=1, source_target_pairs={{8,16},{16,8},{24,32},{32,24},{40,48},{48,40},{9,17},{17,9},{25,33... | collective-permute-start | bytes 1572872 | tf_op jit(solution)/shard_map/ppermute | solution.py:331
  61.4 23.9 %collective-permute-start.11 = (f32[128,8,128]{2,1,0:T(8,128)S(1)}, f32[128,8,128]{2,1,0:T(8,128)S(1)}, u32[]{:S(2)}, u32[]{:S(2)}) collective-permute-start(f32[128,8,128]{2,1,0:T(8,128)S(1)} %shard_map.66.order), channel_id=1, source_target_pairs={{1,2},{2,1},{3,4},{4,3},{5,6},{6,5},{9,10},{10,9},{11,12},{12,11},... | collective-permute-start | bytes 1572872 | tf_op jit(solution)/shard_map/ppermute | solution.py:331
  65.9 17.8 %collective-permute-start.14 = (f32[8,8,128]{2,1,0:T(8,128)S(1)}, f32[8,8,128]{2,1,0:T(8,128)S(1)}, u32[]{:S(2)}, u32[]{:S(2)}) collective-permute-start(f32[8,8,128]{2,1,0:T(8,128)S(1)} %get-tuple-element.38.order), channel_id=1, source_target_pairs={{0,64},{64,0},{1,65},{65,1},{2,66},{66,2},{3,67},{67,3},{4,68},{68... | collective-permute-start | bytes 98312 | tf_op jit(solution)/shard_map/ppermute | solution.py:331
  85.2 25.3 %collective-permute-start.15 = (f32[128,8,128]{2,1,0:T(8,128)S(1)}, f32[128,8,128]{2,1,0:T(8,128)S(1)}, u32[]{:S(2)}, u32[]{:S(2)}) collective-permute-start(f32[128,8,128]{2,1,0:T(8,128)S(1)} %shard_map.73), channel_id=1, source_target_pairs={{0,1},{1,0},{2,3},{3,2},{4,5},{5,4},{6,7},{7,6},{8,9},{9,8},{10,11... | collective-permute-start | bytes 1572872 | tf_op jit(solution)/shard_map/ppermute | solution.py:331
  88.5 22.1 %collective-permute-start.17 = (f32[128,8,128]{2,1,0:T(8,128)S(1)}, f32[128,8,128]{2,1,0:T(8,128)S(1)}, u32[]{:S(2)}, u32[]{:S(2)}) collective-permute-start(f32[128,8,128]{2,1,0:T(8,128)S(1)} %get-tuple-element.42), channel_id=1, source_target_pairs={{0,8},{8,0},{16,24},{24,16},{32,40},{40,32},{48,56},{56,48},{1,9},... | collective-permute-start | bytes 1572872 | tf_op jit(solution)/shard_map/ppermute | solution.py:331
  88.5 22.0 %collective-permute-start.18 = (f32[128,8,128]{2,1,0:T(8,128)S(1)}, f32[128,8,128]{2,1,0:T(8,128)S(1)}, u32[]{:S(2)}, u32[]{:S(2)}) collective-permute-start(f32[128,8,128]{2,1,0:T(8,128)S(1)} %get-tuple-element.43), channel_id=1, source_target_pairs={{8,16},{16,8},{24,32},{32,24},{40,48},{48,40},{9,17},{17,9},{25,33... | collective-permute-start | bytes 1572872 | tf_op jit(solution)/shard_map/ppermute | solution.py:331
  89.2 22.8 %collective-permute-start.16 = (f32[128,8,128]{2,1,0:T(8,128)S(1)}, f32[128,8,128]{2,1,0:T(8,128)S(1)}, u32[]{:S(2)}, u32[]{:S(2)}) collective-permute-start(f32[128,8,128]{2,1,0:T(8,128)S(1)} %shard_map.70.order), channel_id=1, source_target_pairs={{1,2},{2,1},{3,4},{4,3},{5,6},{6,5},{9,10},{10,9},{11,12},{12,11},... | collective-permute-start | bytes 1572872 | tf_op jit(solution)/shard_map/ppermute | solution.py:331
  95.2 15.3 %collective-permute-start.19 = (f32[8,8,128]{2,1,0:T(8,128)S(1)}, f32[8,8,128]{2,1,0:T(8,128)S(1)}, u32[]{:S(2)}, u32[]{:S(2)}) collective-permute-start(f32[8,8,128]{2,1,0:T(8,128)S(1)} %get-tuple-element.41.order), channel_id=1, source_target_pairs={{0,64},{64,0},{1,65},{65,1},{2,66},{66,2},{3,67},{67,3},{4,68},{68... | collective-permute-start | bytes 98312 | tf_op jit(solution)/shard_map/ppermute | solution.py:331
  112.0 23.5 %collective-permute-start.20 = (f32[128,8,128]{2,1,0:T(8,128)S(1)}, f32[128,8,128]{2,1,0:T(8,128)S(1)}, u32[]{:S(2)}, u32[]{:S(2)}) collective-permute-start(f32[128,8,128]{2,1,0:T(8,128)S(1)} %shard_map.77), channel_id=1, source_target_pairs={{0,1},{1,0},{2,3},{3,2},{4,5},{5,4},{6,7},{7,6},{8,9},{9,8},{10,11... | collective-permute-start | bytes 1572872 | tf_op jit(solution)/shard_map/ppermute | solution.py:331
  115.2 20.3 %collective-permute-start.22 = (f32[128,8,128]{2,1,0:T(8,128)S(1)}, f32[128,8,128]{2,1,0:T(8,128)S(1)}, u32[]{:S(2)}, u32[]{:S(2)}) collective-permute-start(f32[128,8,128]{2,1,0:T(8,128)S(1)} %get-tuple-element.45), channel_id=1, source_target_pairs={{0,8},{8,0},{16,24},{24,16},{32,40},{40,32},{48,56},{56,48},{1,9},... | collective-permute-start | bytes 1572872 | tf_op jit(solution)/shard_map/ppermute | solution.py:331
  115.3 20.2 %collective-permute-start.23 = (f32[128,8,128]{2,1,0:T(8,128)S(1)}, f32[128,8,128]{2,1,0:T(8,128)S(1)}, u32[]{:S(2)}, u32[]{:S(2)}) collective-permute-start(f32[128,8,128]{2,1,0:T(8,128)S(1)} %get-tuple-element.46), channel_id=1, source_target_pairs={{8,16},{16,8},{24,32},{32,24},{40,48},{48,40},{9,17},{17,9},{25,33... | collective-permute-start | bytes 1572872 | tf_op jit(solution)/shard_map/ppermute | solution.py:331
  116.0 21.8 %collective-permute-start.21 = (f32[128,8,128]{2,1,0:T(8,128)S(1)}, f32[128,8,128]{2,1,0:T(8,128)S(1)}, u32[]{:S(2)}, u32[]{:S(2)}) collective-permute-start(f32[128,8,128]{2,1,0:T(8,128)S(1)} %shard_map.74.order), channel_id=1, source_target_pairs={{1,2},{2,1},{3,4},{4,3},{5,6},{6,5},{9,10},{10,9},{11,12},{12,11},... | collective-permute-start | bytes 1572872 | tf_op jit(solution)/shard_map/ppermute | solution.py:331
  120.2 15.3 %collective-permute-start.24 = (f32[8,8,128]{2,1,0:T(8,128)S(1)}, f32[8,8,128]{2,1,0:T(8,128)S(1)}, u32[]{:S(2)}, u32[]{:S(2)}) collective-permute-start(f32[8,8,128]{2,1,0:T(8,128)S(1)} %get-tuple-element.44.order), channel_id=1, source_target_pairs={{0,64},{64,0},{1,65},{65,1},{2,66},{66,2},{3,67},{67,3},{4,68},{68... | collective-permute-start | bytes 98312 | tf_op jit(solution)/shard_map/ppermute | solution.py:331
  136.9 28.0 %collective-permute-start.25 = (f32[128,8,128]{2,1,0:T(8,128)S(1)}, f32[128,8,128]{2,1,0:T(8,128)S(1)}, u32[]{:S(2)}, u32[]{:S(2)}) collective-permute-start(f32[128,8,128]{2,1,0:T(8,128)S(1)} %shard_map.81), channel_id=1, source_target_pairs={{0,1},{1,0},{2,3},{3,2},{4,5},{5,4},{6,7},{7,6},{8,9},{9,8},{10,11... | collective-permute-start | bytes 1572872 | tf_op jit(solution)/shard_map/ppermute | solution.py:331
  139.3 26.7 %collective-permute-start.26 = (f32[128,8,128]{2,1,0:T(8,128)S(1)}, f32[128,8,128]{2,1,0:T(8,128)S(1)}, u32[]{:S(2)}, u32[]{:S(2)}) collective-permute-start(f32[128,8,128]{2,1,0:T(8,128)S(1)} %shard_map.78.order), channel_id=1, source_target_pairs={{1,2},{2,1},{3,4},{4,3},{5,6},{6,5},{9,10},{10,9},{11,12},{12,11},... | collective-permute-start | bytes 1572872 | tf_op jit(solution)/shard_map/ppermute | solution.py:331
  148.8 17.2 %collective-permute-start.27 = (f32[128,8,128]{2,1,0:T(8,128)S(1)}, f32[128,8,128]{2,1,0:T(8,128)S(1)}, u32[]{:S(2)}, u32[]{:S(2)}) collective-permute-start(f32[128,8,128]{2,1,0:T(8,128)S(1)} %get-tuple-element.48), channel_id=1, source_target_pairs={{0,8},{8,0},{16,24},{24,16},{32,40},{40,32},{48,56},{56,48},{1,9},... | collective-permute-start | bytes 1572872 | tf_op jit(solution)/shard_map/ppermute | solution.py:331
  148.9 17.1 %collective-permute-start.28 = (f32[128,8,128]{2,1,0:T(8,128)S(1)}, f32[128,8,128]{2,1,0:T(8,128)S(1)}, u32[]{:S(2)}, u32[]{:S(2)}) collective-permute-start(f32[128,8,128]{2,1,0:T(8,128)S(1)} %get-tuple-element.49), channel_id=1, source_target_pairs={{8,16},{16,8},{24,32},{32,24},{40,48},{48,40},{9,17},{17,9},{25,33... | collective-permute-start | bytes 1572872 | tf_op jit(solution)/shard_map/ppermute | solution.py:331
  149.6 15.3 %collective-permute-start.29 = (f32[8,8,128]{2,1,0:T(8,128)S(1)}, f32[8,8,128]{2,1,0:T(8,128)S(1)}, u32[]{:S(2)}, u32[]{:S(2)}) collective-permute-start(f32[8,8,128]{2,1,0:T(8,128)S(1)} %get-tuple-element.47.order), channel_id=1, source_target_pairs={{0,64},{64,0},{1,65},{65,1},{2,66},{66,2},{3,67},{67,3},{4,68},{68... | collective-permute-start | bytes 98312 | tf_op jit(solution)/shard_map/ppermute | solution.py:331
  171.6 5.8 %collective-permute-start.30 = (f32[2,8,8,128]{3,2,1,0:T(8,128)S(1)}, f32[2,8,8,128]{3,2,1,0:T(8,128)S(1)}, u32[]{:S(2)}, u32[]{:S(2)}) collective-permute-start(f32[2,8,8,128]{3,2,1,0:T(8,128)S(1)} %get-tuple-element.51.mine.order), channel_id=1, source_target_pairs={{0,64},{64,0},{1,65},{65,1},{2,66},{66,2},{3,67},{67,3},{4,68},{68... | collective-permute-start | bytes 196616 | tf_op jit(solution)/shard_map/ppermute | solution.py:331

commit v4 on v3

--- a/solution.py
+++ b/solution.py
@@ -78,15 +78,13 @@
     lax.fori_loop(0, rows // ROWS, body, before)
 
 
-def edge_body(flags, f, fj, fi, fk, ha, hb, e1, e2, s, order, g1, g2, gs):
-    rows, ni, nk, nl = f.shape
+def cells(flags, f, fj, fi, fk, ha, hb, e1, e2):
+    _, _, nk, nl = f.shape
     i_even = flags[1] == 0
-    low_south = flags[2] == 0
     sub = lax.broadcasted_iota(jnp.int32, (nk, nl), 0)
     a_edge = sub == jnp.where(flags[0] == 0, nk - 1, 0)
     first_k = sub == 0
     last_k = sub == nk - 1
-    zero = jnp.zeros((nk, nl), F32)
 
     def cell(j, i, c, prev, nxt, il, iu):
         ra = jnp.broadcast_to(ha[j, pl.ds(i, 1), :], (nk, nl))
@@ -100,6 +98,13 @@
         x1, x2 = e1[j], e2[j]
         return jnp.where(i_even, x2, x1), jnp.where(i_even, x1, x2)
 
+    return cell, sides
+
+
+def south_body(flags, f, fj, fi, fk, ha, hb, e1, e2, s, gs):
+    rows, ni, _, _ = f.shape
+    low_south = flags[2] == 0
+    cell, sides = cells(flags, f, fj, fi, fk, ha, hb, e1, e2)
     js = jnp.where(low_south, rows - 1, 0)
     jin = jnp.where(low_south, rows - 2, 1)
     below, above = sides(js)
@@ -110,6 +115,19 @@
             js, i, row[i], jnp.where(low_south, inner, s[i]), jnp.where(low_south, s[i], inner),
             row[i - 1] if i else below, row[i + 1] if i + 1 < ni else above,
         )
+
+
+def face_b_body(flags, fr, fjr, fir, fkr, hb, e1, e2, sr, f, fj, fi, fk, ha, s, gb, gs):
+    south_body(flags, f, fj, fi, fk, ha, hb, e1, e2, s, gs)
+    face_body(1, flags, fr, fjr, fir, fkr, hb, e1, e2, sr, gb)
+
+
+def edge_body(flags, f, fj, fi, fk, ha, hb, e1, e2, s, order, g1, g2):
+    rows, ni, nk, nl = f.shape
+    i_even = flags[1] == 0
+    low_south = flags[2] == 0
+    zero = jnp.zeros((nk, nl), F32)
+    cell, sides = cells(flags, f, fj, fi, fk, ha, hb, e1, e2)
 
     before = tuple(jnp.where(low_south, zero, s[i]) for i in (0, ni - 1))
     after = tuple(jnp.where(low_south, s[i], zero) for i in (0, ni - 1))
@@ -341,9 +359,9 @@
         [(rows, ni, 1, nl), (rows, nk, 1, nl), (rows, nk, 1, nl), (ni, nk, 1, nl)],
         51, [SMEM, HBM, VMEM], [sem((4,))],
     )
+    s = swap(gs.reshape(jface), "south", 0)
     hb = swap(gb.reshape(kface), "down", 1)
     e2 = swap(g2.reshape(iface), "east", 1)
-    s = swap(gs.reshape(jface), "south", 0)
     e1 = swap(g1.reshape(iface), "east", 0)
     field, fj, fi, fk = call(
         load_body, [field, fj, fi, fk, gs], [field.shape] * 4,
@@ -356,14 +374,18 @@
         sr = s.reshape(ni * nk, nl)
         (ga,) = call(functools.partial(face_body, 0), [flags, fr, fjr, fir, fkr, ha, e1, e2, sr], [kface])
         ha_next = swap(ga, "down", 0)
-        (gb,) = call(functools.partial(face_body, 1), [flags, fr, fjr, fir, fkr, hb, e1, e2, sr], [kface])
+        halos = [flags, field, fj, fi, fk, ha, hb, e1, e2, s]
+        gb, gs = call(
+            face_b_body,
+            [flags, fr, fjr, fir, fkr, hb, e1, e2, sr, field, fj, fi, fk, ha, s],
+            [kface, jface],
+        )
+        s = swap(gs, "south", 0)
         hb_next = swap(gb, "down", 1)
-        halos = [flags, field, fj, fi, fk, ha, hb, e1, e2, s]
-        g1, g2, gs = call(edge_body, [*halos, gb], [iface, iface, jface])
+        g1, g2 = call(edge_body, [*halos, gb], [iface, iface])
         e2 = swap(g2, "east", 1)
-        s = swap(gs, "south", 0)
         e1 = swap(g1, "east", 0)
-        (field,) = call(full_body, [*halos, gs], [field.shape])
+        (field,) = call(full_body, [*halos, g1], [field.shape])
         ha, hb = ha_next, hb_next
     field, stats = call(
         final_body, [flags, field, fj, fi, fk, ha, hb, e1, e2, s],

time: 182 us -> 182 us (level)
  no operation moved by 1% of the time
where the time goes in v4:
time: 182 us; the launch traced here: 180 us
  waiting for transfers between devices  67.4 us (37%)
  Pallas kernels  64.8 us (36%)
  starting transfers between devices  46.4 us (25%)
    ppermute x31, waiting for transfers between devices, swap(): return lax.ppermute(x, axis, swap_pairs(lax.axis_size(axis), first))  67.4 us
    pallas_call x26, Pallas kernels, call(): pl.pallas_call(body, out_shape=[jax.ShapeDtypeStruct(o, F32) for o in out...  64.8 us
    ppermute x31, starting transfers between devices, swap(): return lax.ppermute(x, axis, swap_pairs(lax.axis_size(axis), first))  46.4 us
  transfers between devices with their start and end apart: 31, of which 9 were waited for; matrix products, arithmetic and copies ran while one was open for 0% of the time, Pallas kernels for 31%

profile of v4, /device:TPU:96, one launch (start us, length us, event | category | flops | bytes accessed | tf_op | source)
XLA Modules:
  0.0 179.7 jit_solution(2193902805323960464)
XLA Ops:
  0.7 1.9 %shard_map.59.order = f32[128,8,1,128]{3,2,1,0:T(1,128)S(1)} custom-call(s32[3]{0:T(128)S(1)} %pad_add_fusion.flags, f32[128,8,8,1,128]{4,3,2,1,0:T(1,128)} %bitcast.62), custom_call_target="tpu_custom_call" | custom-call | tf_op jit(solution)/shard_map/pallas_call | solution.py:326
  2.6 1.6 collective-permute-start
  4.2 1.9 %shard_map.60 = (f32[128,8,1,128]{3,2,1,0:T(1,128)S(1)}, f32[128,8,1,128]{3,2,1,0:T(1,128)S(1)}, f32[128,8,1,128]{3,2,1,0:T(1,128)S(1)}, f32[8,8,1,128]{3,2,1,0:T(1,128)S(1)}) custom-call(s32[3]{0:T(128)S(1)} %pad_add_fusion.flags, f32[128,8,8,1,128]{4,3,2,1,0:T(1,128)} %bitcast.63, f32[128,8,1,128]{3,2,1,0:T(1,128)S(1)} %shard_map.59.order), custom_call_target="tpu_custom_call" | custom-call | tf_op jit(solution)/shard_map/pallas_call | solution.py:326
  6.9 2.3 %collective-permute-start.1 = (f32[128,8,128]{2,1,0:T(8,128)S(1)}, f32[128,8,128]{2,1,0:T(8,128)S(1)}, u32[]{:S(2)}, u32[]{:S(2)}) collective-permute-start(f32[128,8,128]{2,1,0:T(8,128)S(1)} %bitcast.76), channel_id=1, source_target_pairs={{1,2},{2,1},{3,4},{4,3},{5,6},{6,5},{9,10},{10,9},{11,12},{12,11},... | collective-permute-start | bytes 1572872 | tf_op jit(solution)/shard_map/ppermute | solution.py:349
  9.2 3.1 %collective-permute-start.4 = (f32[8,8,128]{2,1,0:T(8,128)S(1)}, f32[8,8,128]{2,1,0:T(8,128)S(1)}, u32[]{:S(2)}, u32[]{:S(2)}) collective-permute-start(f32[8,8,128]{2,1,0:T(8,128)S(1)} %bitcast.75), channel_id=1, source_target_pairs={{0,64},{64,0},{1,65},{65,1},{2,66},{66,2},{3,67},{67,3},{4,68},{68... | collective-permute-start | bytes 98312 | tf_op jit(solution)/shard_map/ppermute | solution.py:349
  12.4 5.0 %shard_map.61 = (f32[128,8,8,128]{3,2,1,0:T(8,128)S(1)}, f32[128,8,8,128]{3,2,1,0:T(8,128)S(1)}, f32[128,8,8,128]{3,2,1,0:T(8,128)S(1)}, f32[128,8,8,128]{3,2,1,0:T(8,128)S(1)}) custom-call(f32[128,8,8,128]{3,2,1,0:T(8,128)S(1)} %copy-done, f32[128,8,8,128]{3,2,1,0:T(8,128)} %refs_1_.1, f32[128,8,8,128]{3,2,1,0:T(8,128)} %refs_2_.1, ...), custom_call_target="tpu_custom_call" | custom-call | tf_op jit(solution)/shard_map/pallas_call | solution.py:326
  17.3 13.1 %collective-permute-done.4.s = f32[8,8,128]{2,1,0:T(8,128)S(1)} collective-permute-done((f32[8,8,128]{2,1,0:T(8,128)S(1)}, f32[8,8,128]{2,1,0:T(8,128)S(1)}, u32[]{:S(2)}, u32[]{:S(2)}) %collective-permute-start.4) | collective-permute-done | bytes 32800 | tf_op jit(solution)/shard_map/ppermute | solution.py:349
  30.5 1.5 shard_map.65
  32.1 1.5 shard_map.62
  33.6 1.6 shard_map.63
  35.3 0.7 collective-permute-start.8
  36.0 3.7 %collective-permute-start.6 = (f32[128,8,128]{2,1,0:T(8,128)S(1)}, f32[128,8,128]{2,1,0:T(8,128)S(1)}, u32[]{:S(2)}, u32[]{:S(2)}) collective-permute-start(f32[128,8,128]{2,1,0:T(8,128)S(1)} %get-tuple-element.40.order), channel_id=1, source_target_pairs={{1,2},{2,1},{3,4},{4,3},{5,6},{6,5},{9,10},{10,9},{11,12},{12,11},... | collective-permute-start | bytes 1572872 | tf_op jit(solution)/shard_map/ppermute | solution.py:349
  39.8 0.9 collective-permute-start.9
  40.7 4.6 %shard_map.64.f = f32[128,8,8,128]{3,2,1,0:T(8,128)S(1)} custom-call(s32[3]{0:T(128)S(1)} %pad_add_fusion.flags, f32[128,8,8,128]{3,2,1,0:T(8,128)S(1)} %get-tuple-element.33.f, f32[128,8,8,128]{3,2,1,0:T(8,128)S(1)} %get-tuple-element.34.fj, f32[128,8,8,128]{3,2,1,0:T(8,128)S(1)} %get-tuple-element.35.fi, f32[128,8,8,128]{3,2,1,0:T(8,128)S(1)} %get-tuple-element.36.fk, ...), custom_call_target="tpu_custom_call" | custom-call | tf_op jit(solution)/shard_map/pallas_call | solution.py:326
  45.3 10.6 %collective-permute-done.9.s = f32[8,8,128]{2,1,0:T(8,128)S(1)} collective-permute-done((f32[8,8,128]{2,1,0:T(8,128)S(1)}, f32[8,8,128]{2,1,0:T(8,128)S(1)}, u32[]{:S(2)}, u32[]{:S(2)}) %collective-permute-start.9) | collective-permute-done | bytes 32800 | tf_op jit(solution)/shard_map/ppermute | solution.py:349
  55.8 1.5 shard_map.69
  57.5 1.6 shard_map.66
  59.0 1.6 shard_map.67
  61.5 4.4 %collective-permute-start.11 = (f32[128,8,128]{2,1,0:T(8,128)S(1)}, f32[128,8,128]{2,1,0:T(8,128)S(1)}, u32[]{:S(2)}, u32[]{:S(2)}) collective-permute-start(f32[128,8,128]{2,1,0:T(8,128)S(1)} %get-tuple-element.44.order), channel_id=1, source_target_pairs={{1,2},{2,1},{3,4},{4,3},{5,6},{6,5},{9,10},{10,9},{11,12},{12,11},... | collective-permute-start | bytes 1572872 | tf_op jit(solution)/shard_map/ppermute | solution.py:349
  66.0 2.1 %collective-permute-start.14 = (f32[8,8,128]{2,1,0:T(8,128)S(1)}, f32[8,8,128]{2,1,0:T(8,128)S(1)}, u32[]{:S(2)}, u32[]{:S(2)}) collective-permute-start(f32[8,8,128]{2,1,0:T(8,128)S(1)} %get-tuple-element.47), channel_id=1, source_target_pairs={{0,64},{64,0},{1,65},{65,1},{2,66},{66,2},{3,67},{67,3},{4,68},{68... | collective-permute-start | bytes 98312 | tf_op jit(solution)/shard_map/ppermute | solution.py:349
  68.1 4.6 %shard_map.68.f = f32[128,8,8,128]{3,2,1,0:T(8,128)S(1)} custom-call(s32[3]{0:T(128)S(1)} %pad_add_fusion.flags, f32[128,8,8,128]{3,2,1,0:T(8,128)S(1)} %shard_map.64.f, f32[128,8,8,128]{3,2,1,0:T(8,128)S(1)} %get-tuple-element.34.fj, f32[128,8,8,128]{3,2,1,0:T(8,128)S(1)} %get-tuple-element.35.fi, f32[128,8,8,128]{3,2,1,0:T(8,128)S(1)} %get-tuple-element.36.fk, ...), custom_call_target="tpu_custom_call" | custom-call | tf_op jit(solution)/shard_map/pallas_call | solution.py:326
  72.8 11.0 %collective-permute-done.14.s = f32[8,8,128]{2,1,0:T(8,128)S(1)} collective-permute-done((f32[8,8,128]{2,1,0:T(8,128)S(1)}, f32[8,8,128]{2,1,0:T(8,128)S(1)}, u32[]{:S(2)}, u32[]{:S(2)}) %collective-permute-start.14) | collective-permute-done | bytes 32800 | tf_op jit(solution)/shard_map/ppermute | solution.py:349
  83.8 1.5 shard_map.73
  85.4 1.5 shard_map.70
  86.9 1.6 shard_map.71
  89.3 6.0 %collective-permute-start.16 = (f32[128,8,128]{2,1,0:T(8,128)S(1)}, f32[128,8,128]{2,1,0:T(8,128)S(1)}, u32[]{:S(2)}, u32[]{:S(2)}) collective-permute-start(f32[128,8,128]{2,1,0:T(8,128)S(1)} %get-tuple-element.48.order), channel_id=1, source_target_pairs={{1,2},{2,1},{3,4},{4,3},{5,6},{6,5},{9,10},{10,9},{11,12},{12,11},... | collective-permute-start | bytes 1572872 | tf_op jit(solution)/shard_map/ppermute | solution.py:349
  95.4 4.6 %shard_map.72.f = f32[128,8,8,128]{3,2,1,0:T(8,128)S(1)} custom-call(s32[3]{0:T(128)S(1)} %pad_add_fusion.flags, f32[128,8,8,128]{3,2,1,0:T(8,128)S(1)} %shard_map.68.f, f32[128,8,8,128]{3,2,1,0:T(8,128)S(1)} %get-tuple-element.34.fj, f32[128,8,8,128]{3,2,1,0:T(8,128)S(1)} %get-tuple-element.35.fi, f32[128,8,8,128]{3,2,1,0:T(8,128)S(1)} %get-tuple-element.36.fk, ...), custom_call_target="tpu_custom_call" | custom-call | tf_op jit(solution)/shard_map/pallas_call | solution.py:326
  100.0 10.6 %collective-permute-done.19.s = f32[8,8,128]{2,1,0:T(8,128)S(1)} collective-permute-done((f32[8,8,128]{2,1,0:T(8,128)S(1)}, f32[8,8,128]{2,1,0:T(8,128)S(1)}, u32[]{:S(2)}, u32[]{:S(2)}) %collective-permute-start.19) | collective-permute-done | bytes 32800 | tf_op jit(solution)/shard_map/ppermute | solution.py:349
  110.6 1.5 shard_map.77
  112.2 1.5 shard_map.74
  113.7 1.6 shard_map.75
  116.2 4.3 %collective-permute-start.21 = (f32[128,8,128]{2,1,0:T(8,128)S(1)}, f32[128,8,128]{2,1,0:T(8,128)S(1)}, u32[]{:S(2)}, u32[]{:S(2)}) collective-permute-start(f32[128,8,128]{2,1,0:T(8,128)S(1)} %get-tuple-element.52.order), channel_id=1, source_target_pairs={{1,2},{2,1},{3,4},{4,3},{5,6},{6,5},{9,10},{10,9},{11,12},{12,11},... | collective-permute-start | bytes 1572872 | tf_op jit(solution)/shard_map/ppermute | solution.py:349
  120.4 3.3 %collective-permute-start.24 = (f32[8,8,128]{2,1,0:T(8,128)S(1)}, f32[8,8,128]{2,1,0:T(8,128)S(1)}, u32[]{:S(2)}, u32[]{:S(2)}) collective-permute-start(f32[8,8,128]{2,1,0:T(8,128)S(1)} %get-tuple-element.55), channel_id=1, source_target_pairs={{0,64},{64,0},{1,65},{65,1},{2,66},{66,2},{3,67},{67,3},{4,68},{68... | collective-permute-start | bytes 98312 | tf_op jit(solution)/shard_map/ppermute | solution.py:349
  123.7 4.6 %shard_map.76.f = f32[128,8,8,128]{3,2,1,0:T(8,128)S(1)} custom-call(s32[3]{0:T(128)S(1)} %pad_add_fusion.flags, f32[128,8,8,128]{3,2,1,0:T(8,128)S(1)} %shard_map.72.f, f32[128,8,8,128]{3,2,1,0:T(8,128)S(1)} %get-tuple-element.34.fj, f32[128,8,8,128]{3,2,1,0:T(8,128)S(1)} %get-tuple-element.35.fi, f32[128,8,8,128]{3,2,1,0:T(8,128)S(1)} %get-tuple-element.36.fk, ...), custom_call_target="tpu_custom_call" | custom-call | tf_op jit(solution)/shard_map/pallas_call | solution.py:326
  128.3 7.2 %collective-permute-done.24.s = f32[8,8,128]{2,1,0:T(8,128)S(1)} collective-permute-done((f32[8,8,128]{2,1,0:T(8,128)S(1)}, f32[8,8,128]{2,1,0:T(8,128)S(1)}, u32[]{:S(2)}, u32[]{:S(2)}) %collective-permute-start.24) | collective-permute-done | bytes 32800 | tf_op jit(solution)/shard_map/ppermute | solution.py:349
  135.6 1.5 shard_map.81
  137.1 1.0 collective-permute-done.21.hb
  138.1 1.5 shard_map.78
  139.6 7.7 %collective-permute-start.26 = (f32[128,8,128]{2,1,0:T(8,128)S(1)}, f32[128,8,128]{2,1,0:T(8,128)S(1)}, u32[]{:S(2)}, u32[]{:S(2)}) collective-permute-start(f32[128,8,128]{2,1,0:T(8,128)S(1)} %get-tuple-element.56.order), channel_id=1, source_target_pairs={{1,2},{2,1},{3,4},{4,3},{5,6},{6,5},{9,10},{10,9},{11,12},{12,11},... | collective-permute-start | bytes 1572872 | tf_op jit(solution)/shard_map/ppermute | solution.py:349
  147.3 1.6 shard_map.79
  150.1 4.6 %shard_map.80.f = f32[128,8,8,128]{3,2,1,0:T(8,128)S(1)} custom-call(s32[3]{0:T(128)S(1)} %pad_add_fusion.flags, f32[128,8,8,128]{3,2,1,0:T(8,128)S(1)} %shard_map.76.f, f32[128,8,8,128]{3,2,1,0:T(8,128)S(1)} %get-tuple-element.34.fj, f32[128,8,8,128]{3,2,1,0:T(8,128)S(1)} %get-tuple-element.35.fi, f32[128,8,8,128]{3,2,1,0:T(8,128)S(1)} %get-tuple-element.36.fk, ...), custom_call_target="tpu_custom_call" | custom-call | tf_op jit(solution)/shard_map/pallas_call | solution.py:326
  154.7 10.4 %collective-permute-done.29.s = f32[8,8,128]{2,1,0:T(8,128)S(1)} collective-permute-done((f32[8,8,128]{2,1,0:T(8,128)S(1)}, f32[8,8,128]{2,1,0:T(8,128)S(1)}, u32[]{:S(2)}, u32[]{:S(2)}) %collective-permute-start.29) | collective-permute-done | bytes 32800 | tf_op jit(solution)/shard_map/ppermute | solution.py:349
  165.1 1.0 collective-permute-done.26.hb
  166.1 5.6 %shard_map.82 = (f32[128,8,8,128]{3,2,1,0:T(8,128)S(1)}, f32[2,8,8,128]{3,2,1,0:T(8,128)S(1)}) custom-call(s32[3]{0:T(128)S(1)} %pad_add_fusion.flags, f32[128,8,8,128]{3,2,1,0:T(8,128)S(1)} %shard_map.80.f, f32[128,8,8,128]{3,2,1,0:T(8,128)S(1)} %get-tuple-element.34.fj, f32[128,8,8,128]{3,2,1,0:T(8,128)S(1)} %get-tuple-element.35.fi, ...), custom_call_target="tpu_custom_call" | custom-call | tf_op jit(solution)/shard_map/pallas_call | solution.py:326
  171.7 1.3 collective-permute-start.30
  173.0 2.0 %shard_map.84 = f32[128,8,8,128]{3,2,1,0:T(8,128)} custom-call(f32[128,8,8,128]{3,2,1,0:T(8,128)S(1)} %get-tuple-element.60.f, f32[2,8,8,128]{3,2,1,0:T(8,128)S(1)} %get-tuple-element.61.mine.order), custom_call_target="tpu_custom_call" | custom-call | tf_op jit(solution)/shard_map/pallas_call | solution.py:326
  175.0 2.5 %collective-permute-done.30.other = f32[2,8,8,128]{3,2,1,0:T(8,128)S(1)} collective-permute-done((f32[2,8,8,128]{3,2,1,0:T(8,128)S(1)}, f32[2,8,8,128]{3,2,1,0:T(8,128)S(1)}, u32[]{:S(2)}, u32[]{:S(2)}) %collective-permute-start.30) | collective-permute-done | bytes 65568 | tf_op jit(solution)/shard_map/ppermute | solution.py:349
  177.5 2.2 %shard_map.83 = f32[128,8,8,128]{3,2,1,0:T(8,128)} custom-call(f32[128,8,8,128]{3,2,1,0:T(8,128)S(1)} %get-tuple-element.60.f, f32[2,8,8,128]{3,2,1,0:T(8,128)S(1)} %get-tuple-element.61.mine.order, f32[2,8,8,128]{3,2,1,0:T(8,128)S(1)} %collective-permute-done.30.other), custom_call_target="tpu_custom_call" | custom-call | tf_op jit(solution)/shard_map/pallas_call | solution.py:326
  (43 shorter events, 5.1 us)
Async XLA Ops:
  0.7 11.6 %copy-start = (f32[128,8,8,128]{3,2,1,0:T(8,128)S(1)}, f32[128,8,8,128]{3,2,1,0:T(8,128)}, u32[]{:S(2)}) copy-start(f32[128,8,8,128]{3,2,1,0:T(8,128)} %refs_0_.1) | copy-start | bytes 12582916
  2.6 27.9 %collective-permute-start = (f32[128,8,128]{2,1,0:T(8,128)S(1)}, f32[128,8,128]{2,1,0:T(8,128)S(1)}, u32[]{:S(2)}, u32[]{:S(2)}) collective-permute-start(f32[128,8,128]{2,1,0:T(8,128)S(1)} %bitcast.64), channel_id=1, source_target_pairs={{0,1},{1,0},{2,3},{3,2},{4,5},{5,4},{6,7},{7,6},{8,9},{9,8},{10,11... | collective-permute-start | bytes 1572872 | tf_op jit(solution)/shard_map/ppermute | solution.py:349
  6.1 24.4 %collective-permute-start.2 = (f32[128,8,128]{2,1,0:T(8,128)S(1)}, f32[128,8,128]{2,1,0:T(8,128)S(1)}, u32[]{:S(2)}, u32[]{:S(2)}) collective-permute-start(f32[128,8,128]{2,1,0:T(8,128)S(1)} %bitcast.78), channel_id=1, source_target_pairs={{0,8},{8,0},{16,24},{24,16},{32,40},{40,32},{48,56},{56,48},{1,9},... | collective-permute-start | bytes 1572872 | tf_op jit(solution)/shard_map/ppermute | solution.py:349
  6.2 24.3 %collective-permute-start.3 = (f32[128,8,128]{2,1,0:T(8,128)S(1)}, f32[128,8,128]{2,1,0:T(8,128)S(1)}, u32[]{:S(2)}, u32[]{:S(2)}) collective-permute-start(f32[128,8,128]{2,1,0:T(8,128)S(1)} %bitcast.77), channel_id=1, source_target_pairs={{8,16},{16,8},{24,32},{32,24},{40,48},{48,40},{9,17},{17,9},{25,33... | collective-permute-start | bytes 1572872 | tf_op jit(solution)/shard_map/ppermute | solution.py:349
  6.9 25.2 %collective-permute-start.1 = (f32[128,8,128]{2,1,0:T(8,128)S(1)}, f32[128,8,128]{2,1,0:T(8,128)S(1)}, u32[]{:S(2)}, u32[]{:S(2)}) collective-permute-start(f32[128,8,128]{2,1,0:T(8,128)S(1)} %bitcast.76), channel_id=1, source_target_pairs={{1,2},{2,1},{3,4},{4,3},{5,6},{6,5},{9,10},{10,9},{11,12},{12,11},... | collective-permute-start | bytes 1572872 | tf_op jit(solution)/shard_map/ppermute | solution.py:349
  9.2 21.2 %collective-permute-start.4 = (f32[8,8,128]{2,1,0:T(8,128)S(1)}, f32[8,8,128]{2,1,0:T(8,128)S(1)}, u32[]{:S(2)}, u32[]{:S(2)}) collective-permute-start(f32[8,8,128]{2,1,0:T(8,128)S(1)} %bitcast.75), channel_id=1, source_target_pairs={{0,64},{64,0},{1,65},{65,1},{2,66},{66,2},{3,67},{67,3},{4,68},{68... | collective-permute-start | bytes 98312 | tf_op jit(solution)/shard_map/ppermute | solution.py:349
  32.0 23.8 %collective-permute-start.5 = (f32[128,8,128]{2,1,0:T(8,128)S(1)}, f32[128,8,128]{2,1,0:T(8,128)S(1)}, u32[]{:S(2)}, u32[]{:S(2)}) collective-permute-start(f32[128,8,128]{2,1,0:T(8,128)S(1)} %shard_map.65), channel_id=1, source_target_pairs={{0,1},{1,0},{2,3},{3,2},{4,5},{5,4},{6,7},{7,6},{8,9},{9,8},{10,11... | collective-permute-start | bytes 1572872 | tf_op jit(solution)/shard_map/ppermute | solution.py:349
  35.2 20.6 %collective-permute-start.7 = (f32[128,8,128]{2,1,0:T(8,128)S(1)}, f32[128,8,128]{2,1,0:T(8,128)S(1)}, u32[]{:S(2)}, u32[]{:S(2)}) collective-permute-start(f32[128,8,128]{2,1,0:T(8,128)S(1)} %get-tuple-element.41.order), channel_id=1, source_target_pairs={{0,8},{8,0},{16,24},{24,16},{32,40},{40,32},{48,56},{56,48},{1,9},... | collective-permute-start | bytes 1572872 | tf_op jit(solution)/shard_map/ppermute | solution.py:349
  35.3 20.5 %collective-permute-start.8 = (f32[128,8,128]{2,1,0:T(8,128)S(1)}, f32[128,8,128]{2,1,0:T(8,128)S(1)}, u32[]{:S(2)}, u32[]{:S(2)}) collective-permute-start(f32[128,8,128]{2,1,0:T(8,128)S(1)} %get-tuple-element.42), channel_id=1, source_target_pairs={{8,16},{16,8},{24,32},{32,24},{40,48},{48,40},{9,17},{17,9},{25,33... | collective-permute-start | bytes 1572872 | tf_op jit(solution)/shard_map/ppermute | solution.py:349
  36.0 21.4 %collective-permute-start.6 = (f32[128,8,128]{2,1,0:T(8,128)S(1)}, f32[128,8,128]{2,1,0:T(8,128)S(1)}, u32[]{:S(2)}, u32[]{:S(2)}) collective-permute-start(f32[128,8,128]{2,1,0:T(8,128)S(1)} %get-tuple-element.40.order), channel_id=1, source_target_pairs={{1,2},{2,1},{3,4},{4,3},{5,6},{6,5},{9,10},{10,9},{11,12},{12,11},... | collective-permute-start | bytes 1572872 | tf_op jit(solution)/shard_map/ppermute | solution.py:349
  39.8 16.0 %collective-permute-start.9 = (f32[8,8,128]{2,1,0:T(8,128)S(1)}, f32[8,8,128]{2,1,0:T(8,128)S(1)}, u32[]{:S(2)}, u32[]{:S(2)}) collective-permute-start(f32[8,8,128]{2,1,0:T(8,128)S(1)} %get-tuple-element.43), channel_id=1, source_target_pairs={{0,64},{64,0},{1,65},{65,1},{2,66},{66,2},{3,67},{67,3},{4,68},{68... | collective-permute-start | bytes 98312 | tf_op jit(solution)/shard_map/ppermute | solution.py:349
  57.3 26.4 %collective-permute-start.10 = (f32[128,8,128]{2,1,0:T(8,128)S(1)}, f32[128,8,128]{2,1,0:T(8,128)S(1)}, u32[]{:S(2)}, u32[]{:S(2)}) collective-permute-start(f32[128,8,128]{2,1,0:T(8,128)S(1)} %shard_map.69), channel_id=1, source_target_pairs={{0,1},{1,0},{2,3},{3,2},{4,5},{5,4},{6,7},{7,6},{8,9},{9,8},{10,11... | collective-permute-start | bytes 1572872 | tf_op jit(solution)/shard_map/ppermute | solution.py:349
  60.6 23.2 %collective-permute-start.12 = (f32[128,8,128]{2,1,0:T(8,128)S(1)}, f32[128,8,128]{2,1,0:T(8,128)S(1)}, u32[]{:S(2)}, u32[]{:S(2)}) collective-permute-start(f32[128,8,128]{2,1,0:T(8,128)S(1)} %get-tuple-element.45.order), channel_id=1, source_target_pairs={{0,8},{8,0},{16,24},{24,16},{32,40},{40,32},{48,56},{56,48},{1,9},... | collective-permute-start | bytes 1572872 | tf_op jit(solution)/shard_map/ppermute | solution.py:349
  60.8 23.0 %collective-permute-start.13 = (f32[128,8,128]{2,1,0:T(8,128)S(1)}, f32[128,8,128]{2,1,0:T(8,128)S(1)}, u32[]{:S(2)}, u32[]{:S(2)}) collective-permute-start(f32[128,8,128]{2,1,0:T(8,128)S(1)} %get-tuple-element.46), channel_id=1, source_target_pairs={{8,16},{16,8},{24,32},{32,24},{40,48},{48,40},{9,17},{17,9},{25,33... | collective-permute-start | bytes 1572872 | tf_op jit(solution)/shard_map/ppermute | solution.py:349
  61.5 23.9 %collective-permute-start.11 = (f32[128,8,128]{2,1,0:T(8,128)S(1)}, f32[128,8,128]{2,1,0:T(8,128)S(1)}, u32[]{:S(2)}, u32[]{:S(2)}) collective-permute-start(f32[128,8,128]{2,1,0:T(8,128)S(1)} %get-tuple-element.44.order), channel_id=1, source_target_pairs={{1,2},{2,1},{3,4},{4,3},{5,6},{6,5},{9,10},{10,9},{11,12},{12,11},... | collective-permute-start | bytes 1572872 | tf_op jit(solution)/shard_map/ppermute | solution.py:349
  66.0 17.8 %collective-permute-start.14 = (f32[8,8,128]{2,1,0:T(8,128)S(1)}, f32[8,8,128]{2,1,0:T(8,128)S(1)}, u32[]{:S(2)}, u32[]{:S(2)}) collective-permute-start(f32[8,8,128]{2,1,0:T(8,128)S(1)} %get-tuple-element.47), channel_id=1, source_target_pairs={{0,64},{64,0},{1,65},{65,1},{2,66},{66,2},{3,67},{67,3},{4,68},{68... | collective-permute-start | bytes 98312 | tf_op jit(solution)/shard_map/ppermute | solution.py:349
  85.3 25.3 %collective-permute-start.15 = (f32[128,8,128]{2,1,0:T(8,128)S(1)}, f32[128,8,128]{2,1,0:T(8,128)S(1)}, u32[]{:S(2)}, u32[]{:S(2)}) collective-permute-start(f32[128,8,128]{2,1,0:T(8,128)S(1)} %shard_map.73), channel_id=1, source_target_pairs={{0,1},{1,0},{2,3},{3,2},{4,5},{5,4},{6,7},{7,6},{8,9},{9,8},{10,11... | collective-permute-start | bytes 1572872 | tf_op jit(solution)/shard_map/ppermute | solution.py:349
  88.5 22.1 %collective-permute-start.17 = (f32[128,8,128]{2,1,0:T(8,128)S(1)}, f32[128,8,128]{2,1,0:T(8,128)S(1)}, u32[]{:S(2)}, u32[]{:S(2)}) collective-permute-start(f32[128,8,128]{2,1,0:T(8,128)S(1)} %get-tuple-element.49.order), channel_id=1, source_target_pairs={{0,8},{8,0},{16,24},{24,16},{32,40},{40,32},{48,56},{56,48},{1,9},... | collective-permute-start | bytes 1572872 | tf_op jit(solution)/shard_map/ppermute | solution.py:349
  88.6 22.0 %collective-permute-start.18 = (f32[128,8,128]{2,1,0:T(8,128)S(1)}, f32[128,8,128]{2,1,0:T(8,128)S(1)}, u32[]{:S(2)}, u32[]{:S(2)}) collective-permute-start(f32[128,8,128]{2,1,0:T(8,128)S(1)} %get-tuple-element.50), channel_id=1, source_target_pairs={{8,16},{16,8},{24,32},{32,24},{40,48},{48,40},{9,17},{17,9},{25,33... | collective-permute-start | bytes 1572872 | tf_op jit(solution)/shard_map/ppermute | solution.py:349
  89.3 22.9 %collective-permute-start.16 = (f32[128,8,128]{2,1,0:T(8,128)S(1)}, f32[128,8,128]{2,1,0:T(8,128)S(1)}, u32[]{:S(2)}, u32[]{:S(2)}) collective-permute-start(f32[128,8,128]{2,1,0:T(8,128)S(1)} %get-tuple-element.48.order), channel_id=1, source_target_pairs={{1,2},{2,1},{3,4},{4,3},{5,6},{6,5},{9,10},{10,9},{11,12},{12,11},... | collective-permute-start | bytes 1572872 | tf_op jit(solution)/shard_map/ppermute | solution.py:349
  95.3 15.3 %collective-permute-start.19 = (f32[8,8,128]{2,1,0:T(8,128)S(1)}, f32[8,8,128]{2,1,0:T(8,128)S(1)}, u32[]{:S(2)}, u32[]{:S(2)}) collective-permute-start(f32[8,8,128]{2,1,0:T(8,128)S(1)} %get-tuple-element.51), channel_id=1, source_target_pairs={{0,64},{64,0},{1,65},{65,1},{2,66},{66,2},{3,67},{67,3},{4,68},{68... | collective-permute-start | bytes 98312 | tf_op jit(solution)/shard_map/ppermute | solution.py:349
  112.1 23.4 %collective-permute-start.20 = (f32[128,8,128]{2,1,0:T(8,128)S(1)}, f32[128,8,128]{2,1,0:T(8,128)S(1)}, u32[]{:S(2)}, u32[]{:S(2)}) collective-permute-start(f32[128,8,128]{2,1,0:T(8,128)S(1)} %shard_map.77), channel_id=1, source_target_pairs={{0,1},{1,0},{2,3},{3,2},{4,5},{5,4},{6,7},{7,6},{8,9},{9,8},{10,11... | collective-permute-start | bytes 1572872 | tf_op jit(solution)/shard_map/ppermute | solution.py:349
  115.4 20.2 %collective-permute-start.22 = (f32[128,8,128]{2,1,0:T(8,128)S(1)}, f32[128,8,128]{2,1,0:T(8,128)S(1)}, u32[]{:S(2)}, u32[]{:S(2)}) collective-permute-start(f32[128,8,128]{2,1,0:T(8,128)S(1)} %get-tuple-element.53.order), channel_id=1, source_target_pairs={{0,8},{8,0},{16,24},{24,16},{32,40},{40,32},{48,56},{56,48},{1,9},... | collective-permute-start | bytes 1572872 | tf_op jit(solution)/shard_map/ppermute | solution.py:349
  115.5 20.1 %collective-permute-start.23 = (f32[128,8,128]{2,1,0:T(8,128)S(1)}, f32[128,8,128]{2,1,0:T(8,128)S(1)}, u32[]{:S(2)}, u32[]{:S(2)}) collective-permute-start(f32[128,8,128]{2,1,0:T(8,128)S(1)} %get-tuple-element.54), channel_id=1, source_target_pairs={{8,16},{16,8},{24,32},{32,24},{40,48},{48,40},{9,17},{17,9},{25,33... | collective-permute-start | bytes 1572872 | tf_op jit(solution)/shard_map/ppermute | solution.py:349
  116.2 21.9 %collective-permute-start.21 = (f32[128,8,128]{2,1,0:T(8,128)S(1)}, f32[128,8,128]{2,1,0:T(8,128)S(1)}, u32[]{:S(2)}, u32[]{:S(2)}) collective-permute-start(f32[128,8,128]{2,1,0:T(8,128)S(1)} %get-tuple-element.52.order), channel_id=1, source_target_pairs={{1,2},{2,1},{3,4},{4,3},{5,6},{6,5},{9,10},{10,9},{11,12},{12,11},... | collective-permute-start | bytes 1572872 | tf_op jit(solution)/shard_map/ppermute | solution.py:349
  120.4 15.1 %collective-permute-start.24 = (f32[8,8,128]{2,1,0:T(8,128)S(1)}, f32[8,8,128]{2,1,0:T(8,128)S(1)}, u32[]{:S(2)}, u32[]{:S(2)}) collective-permute-start(f32[8,8,128]{2,1,0:T(8,128)S(1)} %get-tuple-element.55), channel_id=1, source_target_pairs={{0,64},{64,0},{1,65},{65,1},{2,66},{66,2},{3,67},{67,3},{4,68},{68... | collective-permute-start | bytes 98312 | tf_op jit(solution)/shard_map/ppermute | solution.py:349
  137.0 28.1 %collective-permute-start.25 = (f32[128,8,128]{2,1,0:T(8,128)S(1)}, f32[128,8,128]{2,1,0:T(8,128)S(1)}, u32[]{:S(2)}, u32[]{:S(2)}) collective-permute-start(f32[128,8,128]{2,1,0:T(8,128)S(1)} %shard_map.81), channel_id=1, source_target_pairs={{0,1},{1,0},{2,3},{3,2},{4,5},{5,4},{6,7},{7,6},{8,9},{9,8},{10,11... | collective-permute-start | bytes 1572872 | tf_op jit(solution)/shard_map/ppermute | solution.py:349
  139.6 26.5 %collective-permute-start.26 = (f32[128,8,128]{2,1,0:T(8,128)S(1)}, f32[128,8,128]{2,1,0:T(8,128)S(1)}, u32[]{:S(2)}, u32[]{:S(2)}) collective-permute-start(f32[128,8,128]{2,1,0:T(8,128)S(1)} %get-tuple-element.56.order), channel_id=1, source_target_pairs={{1,2},{2,1},{3,4},{4,3},{5,6},{6,5},{9,10},{10,9},{11,12},{12,11},... | collective-permute-start | bytes 1572872 | tf_op jit(solution)/shard_map/ppermute | solution.py:349
  148.9 17.2 %collective-permute-start.27 = (f32[128,8,128]{2,1,0:T(8,128)S(1)}, f32[128,8,128]{2,1,0:T(8,128)S(1)}, u32[]{:S(2)}, u32[]{:S(2)}) collective-permute-start(f32[128,8,128]{2,1,0:T(8,128)S(1)} %get-tuple-element.57.order), channel_id=1, source_target_pairs={{0,8},{8,0},{16,24},{24,16},{32,40},{40,32},{48,56},{56,48},{1,9},... | collective-permute-start | bytes 1572872 | tf_op jit(solution)/shard_map/ppermute | solution.py:349
  149.0 17.1 %collective-permute-start.28 = (f32[128,8,128]{2,1,0:T(8,128)S(1)}, f32[128,8,128]{2,1,0:T(8,128)S(1)}, u32[]{:S(2)}, u32[]{:S(2)}) collective-permute-start(f32[128,8,128]{2,1,0:T(8,128)S(1)} %get-tuple-element.58), channel_id=1, source_target_pairs={{8,16},{16,8},{24,32},{32,24},{40,48},{48,40},{9,17},{17,9},{25,33... | collective-permute-start | bytes 1572872 | tf_op jit(solution)/shard_map/ppermute | solution.py:349
  149.7 15.4 %collective-permute-start.29 = (f32[8,8,128]{2,1,0:T(8,128)S(1)}, f32[8,8,128]{2,1,0:T(8,128)S(1)}, u32[]{:S(2)}, u32[]{:S(2)}) collective-permute-start(f32[8,8,128]{2,1,0:T(8,128)S(1)} %get-tuple-element.59), channel_id=1, source_target_pairs={{0,64},{64,0},{1,65},{65,1},{2,66},{66,2},{3,67},{67,3},{4,68},{68... | collective-permute-start | bytes 98312 | tf_op jit(solution)/shard_map/ppermute | solution.py:349
  171.7 5.8 %collective-permute-start.30 = (f32[2,8,8,128]{3,2,1,0:T(8,128)S(1)}, f32[2,8,8,128]{3,2,1,0:T(8,128)S(1)}, u32[]{:S(2)}, u32[]{:S(2)}) collective-permute-start(f32[2,8,8,128]{3,2,1,0:T(8,128)S(1)} %get-tuple-element.61.mine.order), channel_id=1, source_target_pairs={{0,64},{64,0},{1,65},{65,1},{2,66},{66,2},{3,67},{67,3},{4,68},{68... | collective-permute-start | bytes 196616 | tf_op jit(solution)/shard_map/ppermute | solution.py:349
